TPU v7x, 32 devices: a whole 2x2x4 slice. The times are simulated.
32 devices in a mesh: grp: 4 (over y, x), gx: 2 (over core), gy: 4 (over z).
Axes of the slice: x: 2, y: 2, z: 4, core: 2. Of those that a mesh axis runs over, the one named last changes fastest.
Arguments:
- velocity: float32 [3, 32, 32, 128], P(None, ('grp', 'gx'), 'gy'), may hold values from -12 to 12
- first_weight: bfloat16 [3, 3, 3, 64, 9], replicated, may hold values from -0.375 to 0.375
- first_bias: float32 [64], replicated, may hold values from -3 to 3
- second_weight: bfloat16 [3, 3, 3, 64, 64], replicated, may hold values from -0.15625 to 0.15625
- second_bias: float32 [64], replicated, may hold values from -3 to 3
- third_weight: bfloat16 [3, 3, 3, 64, 64], replicated, may hold values from -0.15625 to 0.15625
- third_bias: float32 [64], replicated, may hold values from -3 to 3
- last_weight: bfloat16 [3, 3, 3, 6, 64], replicated, may hold values from -0.15625 to 0.15625
Outputs:
- updated: float32 [3, 32, 32, 128], P(None, ('grp', 'gx'), 'gy')
- stress: float32 [6, 32, 32, 128], P(None, ('grp', 'gx'), 'gy')
All inputs are finite; a program needn't handle non-finite values.
Results may differ from a plain program's by a relative error of at most 0.002.
The roundings to bfloat16 on the way count: a program that leaves them out, or rounds other values in their place, can miss the bound.
Values may be sent and summed in bfloat16 or wider, within the bound.
No kernel may reach another device: no remote copies, remote signals or barrier semaphores. Data moves between devices by JAX's collectives and lax.ppermute only.
A program may use at most 192 MiB of HBM per device.

v0:
```python
import functools

import jax
import jax.numpy as jnp
from jax import lax
from jax.experimental import pallas as pl
from jax.experimental.pallas import tpu as pltpu
from jax.sharding import PartitionSpec as P

time_step = 0.1
viscosity = 0.05
power_input = 5.0
pairing = ((0, 3, 4), (3, 1, 5), (4, 5, 2))
halo = 6
axis_x = ("grp", "gx")
axis_y = "gy"
slot = 32
f32 = jnp.float32
bf16 = jnp.bfloat16


def shifted(cells, axis, step):
    count = lax.axis_size(axis)
    return lax.ppermute(cells, axis, [(i, (i + step) % count) for i in range(count)])


def neighbours(cells, axis, dim):
    extent = cells.shape[dim]
    before, after = [], []
    hop, need = 1, halo
    while need > 0:
        width = min(extent, need)
        tail = lax.slice_in_dim(cells, extent - width, extent, axis=dim)
        head = lax.slice_in_dim(cells, 0, width, axis=dim)
        before.insert(0, shifted(tail, axis, hop))
        after.append(shifted(head, axis, -hop))
        hop += 1
        need -= width
    return before, after


def blocks_in(extent, count):
    size = 1
    while count % (2 * size) == 0 and 2 * size * extent <= extent + 2 * halo:
        size *= 2
    return size


def pair_rows(get, xin, xout):
    parts = []
    for xo in range(xout):
        parts.append(get(xin - xo) if 0 <= xin - xo <= 2 else None)
    return parts


def expand_hidden(w_ref, out_ref):
    channels = w_ref.shape[3]
    outs = w_ref.shape[4 - 1]
    zero = jnp.zeros((outs, channels), f32)
    blank = jnp.zeros((channels, 2 * outs), bf16)
    for dz in range(3):
        for xin in range(4):
            tall = []
            for dy in range(3):
                rows = [
                    w_ref[xin - xo, dy, dz].astype(f32) if 0 <= xin - xo <= 2 else zero
                    for xo in range(2)
                ]
                tall.append(jnp.concatenate(rows, axis=0).T.astype(bf16))
            for yin in range(4):
                base = ((dz * 4 + yin) * 4 + xin) * channels
                for yo in range(2):
                    piece = tall[yin - yo] if 0 <= yin - yo <= 2 else blank
                    out_ref[base : base + channels, yo * 2 * outs : (yo + 1) * 2 * outs] = piece


def expand_first(w_ref, out_ref):
    outs, inner = w_ref.shape[3], w_ref.shape[4]
    fill = slot - 3 * inner
    zero = jnp.zeros((outs, slot), f32)
    blank = jnp.zeros((slot, 2 * outs), bf16)
    flat = {}
    for dx in range(3):
        for dy in range(3):
            parts = [w_ref[dx, dy, dz].astype(f32) for dz in range(3)]
            parts.append(jnp.zeros((outs, fill), f32))
            flat[dx, dy] = jnp.concatenate(parts, axis=1)
    for xin in range(4):
        tall = []
        for dy in range(3):
            rows = [flat[xin - xo, dy] if 0 <= xin - xo <= 2 else zero for xo in range(2)]
            tall.append(jnp.concatenate(rows, axis=0).T.astype(bf16))
        for yin in range(4):
            base = (xin * 4 + yin) * slot
            for yo in range(2):
                piece = tall[yin - yo] if 0 <= yin - yo <= 2 else blank
                out_ref[base : base + slot, yo * 2 * outs : (yo + 1) * 2 * outs] = piece


def expand_last(w_ref, out_ref):
    outs, channels = w_ref.shape[3], w_ref.shape[4]
    zero = jnp.zeros((8, channels), f32)
    pad = jnp.zeros((8 - outs, channels), f32)
    taps = {}
    for dx in range(3):
        for dy in range(3):
            for dz in range(3):
                taps[dx, dy, dz] = jnp.concatenate([w_ref[dx, dy, dz].astype(f32), pad], axis=0)
    for yin in range(4):
        for pair in range(2):
            column = []
            for dz in range(3):
                for yo in range(2):
                    for xo in range(2):
                        halves = []
                        for xin in (2 * pair, 2 * pair + 1):
                            dx, dy = xin - xo, yin - yo
                            inside = 0 <= dx <= 2 and 0 <= dy <= 2
                            halves.append(taps[dx, dy, dz] if inside else zero)
                        column.append(jnp.concatenate(halves, axis=1))
            base = (yin * 2 + pair) * 2 * channels
            out_ref[:, base : base + 2 * channels] = jnp.concatenate(column, axis=0).astype(bf16)


def prepare_kernel(w1, w2, w3, w4, o1, o2, o3, o4):
    expand_first(w1, o1)
    expand_hidden(w2, o2)
    expand_hidden(w3, o3)
    expand_last(w4, o4)


def prepare(w1, w2, w3, w4):
    outs, channels = w2.shape[3], w2.shape[4]
    vmem = pl.BlockSpec(memory_space=pltpu.VMEM)
    return pl.pallas_call(
        prepare_kernel,
        out_shape=(
            jax.ShapeDtypeStruct((16 * slot, 4 * outs), bf16),
            jax.ShapeDtypeStruct((48 * channels, 4 * outs), bf16),
            jax.ShapeDtypeStruct((48 * channels, 4 * outs), bf16),
            jax.ShapeDtypeStruct((96, 16 * channels), bf16),
        ),
        in_specs=[vmem] * 4,
        out_specs=(vmem,) * 4,
        cost_estimate=pl.CostEstimate(flops=10**9, bytes_accessed=8 * 10**6, transcendentals=0),
        compiler_params=pltpu.CompilerParams(vmem_limit_bytes=24 * 2**20),
        name="prepare",
    )(w1, w2, w3, w4)


def main_kernel(count, *refs):
    pieces = refs[:count]
    (w1, b1, w2, b2, w3, b3, w4) = refs[count : count + 7]
    base_ref, stress_ref = refs[count + 7 : count + 9]
    vel, feat, turned, h1, h2, h3, tau = refs[count + 9 :]
    depth = vel.shape[3]
    wide_x, wide_y = vel.shape[1], vel.shape[2]
    fx, fy = wide_x - 2, wide_y - 2

    at = 0
    for piece in pieces:
        vel[:, at : at + piece.shape[1]] = piece[...]
        at += piece.shape[1]

    feat[...] = jnp.zeros_like(feat)

    def features(x, carry):
        for i in range(3):
            row = vel[i, x + 1]
            center = row[1:-1]
            diffs = (
                (vel[i, x + 2][1:-1] - vel[i, x][1:-1]) * 0.5,
                (row[2:] - row[:-2]) * 0.5,
                (pltpu.roll(center, depth - 1, 1) - pltpu.roll(center, 1, 1)) * 0.5,
            )
            for j in range(3):
                value = diffs[j].astype(bf16).astype(f32)
                for dz, amount in enumerate((1, 0, depth - 1)):
                    moved = pltpu.roll(value, amount, 1) if amount else value
                    feat[pl.ds(dz * 9 + 3 * i + j, fy, stride=slot), :] = moved
        for half in range(fy // 2 - 1):
            block = feat[half * 2 * slot : half * 2 * slot + 4 * slot, :]
            turned[x, half] = block.astype(bf16).T
        return carry

    lax.fori_loop(0, fx, features, 0)

    def layer(gather, weight, bias_ref, target, steps, variants):
        bias = jnp.concatenate([bias_ref[...]] * 4, axis=1)

        def step(xp, carry):
            left = gather(xp)
            total = jnp.dot(left, weight[...], preferred_element_type=f32)
            value = jnp.tanh(total + bias)
            rows = value.shape[0] // depth
            value = value.reshape(rows, depth, value.shape[1])
            width = value.shape[2] // 2
            for dz, amount in enumerate((1, 0, depth - 1)):
                if dz not in variants:
                    continue
                moved = pltpu.roll(value, amount, 1) if amount else value
                moved = moved.astype(bf16)
                for yo in range(2):
                    where = (xp, yo) if len(variants) == 1 else (dz, xp, yo)
                    target[where] = moved[:, :, yo * width : (yo + 1) * width]
            return carry

        lax.fori_loop(0, steps, step, 0)

    def gather_first(xp):
        parts = []
        for a in range(4):
            block = turned[2 * xp + a]
            parts.append(block.reshape(block.shape[0] * block.shape[1], block.shape[2]))
        return jnp.concatenate(parts, axis=1)

    def gather_hidden(source, variants):
        rows = source.shape[-3] - 1

        def gather(xp):
            parts = []
            for dz in variants:
                for yin in range(4):
                    for pair in range(2):
                        where = (xp + pair, yin % 2, slice(yin // 2, yin // 2 + rows))
                        block = source[where if len(source.shape) == 5 else (dz, *where)]
                        parts.append(block.reshape(rows * block.shape[1], block.shape[2]))
            return jnp.concatenate(parts, axis=1)

        return gather

    every = (0, 1, 2)
    layer(gather_first, w1, b1, h1, h1.shape[1], every)
    layer(gather_hidden(h1, every), w2, b2, h2, h2.shape[1], every)
    layer(gather_hidden(h2, every), w3, b3, h3, h3.shape[0], (1,))

    last = gather_hidden(h3, (1,))

    def final(xp, carry):
        sides = lax.dot_general(
            w4[...], last(xp), (((1,), (1,)), ((), ())), preferred_element_type=f32
        )
        for yp in range(sides.shape[1] // depth):
            part = sides[:, yp * depth : (yp + 1) * depth]
            total = pltpu.roll(part[0:32], 1, 1) + part[32:64] + pltpu.roll(part[64:96], depth - 1, 1)
            for yo in range(2):
                for xo in range(2):
                    cell = (2 * yo + xo) * 8
                    row = (2 * yp + yo) * 8
                    tau[2 * xp + xo, row : row + 8, :] = total[cell : cell + 8]
        return carry

    lax.fori_loop(0, h3.shape[0] - 1, final, 0)

    own_x, own_y = base_ref.shape[1], base_ref.shape[2]

    def stress_at(c, x, y):
        return tau[x, pl.ds(y * 8 + c, own_y, stride=8), :]

    def turn(a, amount):
        return pltpu.roll(a, amount % depth, 1)

    for x in range(own_x):
        for c in range(6):
            stress_ref[c, x] = stress_at(c, x + 1, 1)
        center = [vel[i, x + halo, halo : halo + own_y, :] for i in range(3)]
        for i in range(3):
            xm = vel[i, x + halo - 1, halo : halo + own_y, :]
            xp = vel[i, x + halo + 1, halo : halo + own_y, :]
            ym = vel[i, x + halo, halo - 1 : halo - 1 + own_y, :]
            yp = vel[i, x + halo, halo + 1 : halo + 1 + own_y, :]
            zm, zp = turn(center[i], 1), turn(center[i], -1)
            advect = (
                center[0] * ((xp - xm) * 0.5)
                + center[1] * ((yp - ym) * 0.5)
                + center[2] * ((zp - zm) * 0.5)
            )
            laplacian = xp + xm + yp + ym + zm + zp - 6.0 * center[i]
            px, py, pz = pairing[i]
            along_z = stress_at(pz, x + 1, 1)
            divergence = (
                (stress_at(px, x + 2, 1) - stress_at(px, x, 1)) * 0.5
                + (stress_at(py, x + 1, 2) - stress_at(py, x + 1, 0)) * 0.5
                + (turn(along_z, -1) - turn(along_z, 1)) * 0.5
            )
            tendency = viscosity * laplacian - advect - divergence
            base_ref[i, x] = center[i] + time_step * tendency


def evolve(velocity, pieces, weights):
    parts, own_x, own_y, depth = velocity.shape
    w1, b1, w2, b2, w3, b3, w4 = weights
    width = 2 * b1.shape[1]
    wide_x, wide_y = own_x + 2 * halo, own_y + 2 * halo
    qx, qy = (wide_x - 4) // 2, (wide_y - 4) // 2
    vmem = pl.BlockSpec(memory_space=pltpu.VMEM)
    stress_count = 6
    cells1 = 4 * qx * qy * depth
    flops = 2 * depth * 256 * (qx * qy * 512 + (qx - 1) * (qy - 1) * 3072 + (qx - 2) * (qy - 2) * 3072)
    return pl.pallas_call(
        functools.partial(main_kernel, len(pieces)),
        out_shape=(
            jax.ShapeDtypeStruct(velocity.shape, f32),
            jax.ShapeDtypeStruct((stress_count,) + velocity.shape[1:], f32),
        ),
        in_specs=[vmem] * (len(pieces) + 7),
        out_specs=(vmem, vmem),
        scratch_shapes=[
            pltpu.VMEM((parts, wide_x, wide_y, depth), f32),
            pltpu.VMEM(((wide_y - 2) * slot, depth), f32),
            pltpu.VMEM((wide_x - 2, qy, depth, 4 * slot), bf16),
            pltpu.VMEM((3, qx, 2, qy, depth, width), bf16),
            pltpu.VMEM((3, qx - 1, 2, qy - 1, depth, width), bf16),
            pltpu.VMEM((qx - 2, 2, qy - 2, depth, width), bf16),
            pltpu.VMEM((wide_x - 10, (wide_y - 10) * 8, depth), f32),
        ],
        cost_estimate=pl.CostEstimate(
            flops=flops, bytes_accessed=8 * 10**6, transcendentals=cells1 * 64
        ),
        compiler_params=pltpu.CompilerParams(vmem_limit_bytes=44 * 2**20),
        name="evolve",
    )(*pieces, *weights)


def box_energy(pieces, own_x, own_y, count_x, count_y):
    wide_y = pieces[0].shape[2]
    span_x, span_y = count_x * own_x, count_y * own_y
    low_x = (own_x + 2 * halo - span_x) // 2
    low_y = (wide_y - span_y) // 2
    total, at = None, 0
    for piece in pieces:
        low, high = max(low_x - at, 0), min(low_x + span_x - at, piece.shape[1])
        if low < high:
            part = piece[:, low:high, low_y : low_y + span_y]
            part = jnp.sum(0.5 * part * part, axis=(0, 1, 2))
            total = part if total is None else total + part
        at += piece.shape[1]
    return jnp.sum(total, keepdims=True).reshape(1, 1) * jnp.ones((1, 128), f32)


def total_energy(box, size_x, size_y):
    count_x, count_y = lax.axis_size(axis_x), lax.axis_size(axis_y)
    left_x, left_y = count_x // size_x, count_y // size_y
    if (left_x & (left_x - 1)) or (left_y & (left_y - 1)):
        return lax.psum(box, axis_x + (axis_y,)) / (size_x * size_y)
    step = size_x
    while left_x > 2:
        box = box + shifted(box, axis_x, step)
        step, left_x = 2 * step, left_x // 2
    hop = size_y
    while left_y > 2:
        box = box + shifted(box, axis_y, hop)
        hop, left_y = 2 * hop, left_y // 2
    total = box
    if left_x == 2:
        total = total + shifted(box, axis_x, step)
    if left_y == 2:
        total = total + shifted(box, axis_y, hop)
    if left_x == 2 and left_y == 2:
        order = [
            (
                x * count_y + y,
                ((x + step) % count_x) * count_y + (y + hop) % count_y,
            )
            for x in range(count_x)
            for y in range(count_y)
        ]
        total = total + lax.ppermute(box, axis_x + (axis_y,), order)
    return total


def local(v, w1, b1, w2, b2, w3, b3, w4):
    own_x, own_y, depth = v.shape[1:]
    count_x, count_y = lax.axis_size(axis_x), lax.axis_size(axis_y)
    e1, e2, e3, e4 = prepare(w1, w2, w3, w4)
    before, after = neighbours(v, axis_y, 2)
    strip = jnp.concatenate(before + [v] + after, axis=2)
    before, after = neighbours(strip, axis_x, 1)
    pieces = before + [strip] + after
    size_x, size_y = blocks_in(own_x, count_x), blocks_in(own_y, count_y)
    box = box_energy(pieces, own_x, own_y, size_x, size_y)
    energy = total_energy(box, size_x, size_y)[0, 0]
    energy = energy / (own_x * own_y * depth * count_x * count_y)
    forcing = power_input / (2.0 * energy + 1e-06)
    weights = (e1, b1.reshape(1, -1), e2, b2.reshape(1, -1), e3, b3.reshape(1, -1), e4)
    base, stress = evolve(v, pieces, weights)
    return base + (time_step * forcing) * v, stress


def solution(mesh):
    block = P(None, axis_x, axis_y, None)
    return jax.shard_map(
        local,
        mesh=mesh,
        in_specs=(block,) + (P(),) * 7,
        out_specs=(block, block),
        check_vma=False,
    )
```

profile of v0, /device:TPU:0, one launch (start us, length us, event | category | flops | bytes accessed | tf_op | source)
XLA Modules:
  0.0 54.3 jit_solution(18237179082370060682)
XLA Ops:
  0.6 0.9 %fusion.6 = (f32[3,4,6,128]{3,2,1,0:T(8,128)S(1)}, f32[3,4,6,128]{3,2,1,0:T(8,128)S(1)}) fusion(f32[3,4,8,128]{3,2,1,0:T(8,128)} %param.8), kind=kLoop, calls=%fused_computation.15 | loop fusion | bytes 147456 | tf_op jit(solution)/shard_map/slice | solution.py:33
  1.5 5.1 %collective-permute-start.1 = (f32[3,4,6,128]{3,2,1,0:T(8,128)S(1)}, f32[3,4,6,128]{3,2,1,0:T(8,128)S(1)}, u32[]{:S(2)}, u32[]{:S(2)}) collective-permute-start(f32[3,4,6,128]{3,2,1,0:T(8,128)S(1)} %get-tuple-element.17), channel_id=1, source_target_pairs={{0,3},{1,0},{2,1},{3,2},{4,7},{5,4},{6,5},{7,6},{8,11},{9,8},{10,9... | collective-permute-start | bytes 110600 | tf_op jit(solution)/shard_map/ppermute | solution.py:24
  6.6 0.0 collective-permute-start
  6.7 1.2 %copy.10.w1 = bf16[3,3,3,64,9]{4,3,2,1,0:T(8,128)(2,1)S(1)} copy(bf16[3,3,3,64,9]{3,2,4,1,0:T(4,128)(2,1)} %param.9) | data formatting | bytes 62208 | tf_op args[1]
  7.8 0.0 copy-start
  7.8 1.0 %copy-done = bf16[3,3,3,64,64]{4,3,2,1,0:T(8,128)(2,1)S(1)} copy-done((bf16[3,3,3,64,64]{4,3,2,1,0:T(8,128)(2,1)S(1)}, bf16[3,3,3,64,64]{4,3,2,1,0:T(8,128)(2,1)}, u32[]{:S(2)}) %copy-start) | copy-done | bytes 221208
  8.8 0.0 copy-start.1
  8.8 1.0 %copy-done.1 = bf16[3,3,3,64,64]{4,3,2,1,0:T(8,128)(2,1)S(1)} copy-done((bf16[3,3,3,64,64]{4,3,2,1,0:T(8,128)(2,1)S(1)}, bf16[3,3,3,64,64]{4,3,2,1,0:T(8,128)(2,1)}, u32[]{:S(2)}) %copy-start.1) | copy-done | bytes 221208
  9.9 0.0 copy-start.2
  9.9 0.8 %copy-done.2 = bf16[3,3,3,6,64]{4,3,2,1,0:T(8,128)(2,1)S(1)} copy-done((bf16[3,3,3,6,64]{4,3,2,1,0:T(8,128)(2,1)S(1)}, bf16[3,3,3,6,64]{4,3,2,1,0:T(8,128)(2,1)}, u32[]{:S(2)}) %copy-start.2) | copy-done | bytes 20760
  10.7 0.0 copy-start.6
  10.7 0.0 copy-start.3
  10.7 0.0 copy-start.4
  10.7 0.0 copy-start.5
  10.7 0.9 %prepare.1 = (bf16[512,256]{1,0:T(8,128)(2,1)S(1)}, bf16[3072,256]{1,0:T(8,128)(2,1)S(1)}, bf16[3072,256]{1,0:T(8,128)(2,1)S(1)}, bf16[96,1024]{1,0:T(8,128)(2,1)S(1)}) custom-call(bf16[3,3,3,64,9]{4,3,2,1,0:T(8,128)(2,1)S(1)} %copy.10.w1, bf16[3,3,3,64,64]{4,3,2,1,0:T(8,128)(2,1)S(1)} %copy-done, bf16[3,3,3,64,64]{4,3,2,1,0:T(8,128)(2,1)S(1)} %copy-done.1, ...), custom_call_target="tpu_custom_call" | custom-call | flops 1000000000 | bytes 8000000 | tf_op jit(solution)/shard_map/prepare/pallas_call | solution.py:135
  11.6 0.0 collective-permute-done.1
  11.6 0.9 %collective-permute-done = f32[3,4,6,128]{3,2,1,0:T(8,128)S(1)} collective-permute-done((f32[3,4,6,128]{3,2,1,0:T(8,128)S(1)}, f32[3,4,6,128]{3,2,1,0:T(8,128)S(1)}, u32[]{:S(2)}, u32[]{:S(2)}) %collective-permute-start) | collective-permute-done | bytes 36896 | tf_op jit(solution)/shard_map/ppermute | solution.py:24
  12.5 0.0 copy-done.6
  12.6 0.1 collective-permute-start.3
  12.7 2.6 %collective-permute-start.4 = (f32[3,4,20,128]{3,2,1,0:T(8,128)S(1)}, f32[3,4,20,128]{3,2,1,0:T(8,128)S(1)}, u32[]{:S(2)}, u32[]{:S(2)}) collective-permute-start(f32[3,4,20,128]{3,2,1,0:T(8,128)S(1)} %pad_maximum_fusion.refs_2_), channel_id=1, source_target_pairs={{0,28},{4,0},{8,4},{12,8},{16,12},{20,16},{24,20},{28,24},{1,29},{... | collective-permute-start | bytes 368648 | tf_op jit(solution)/shard_map/ppermute | solution.py:24
  15.3 0.6 %collective-permute-start.2 = (f32[3,2,20,128]{3,2,1,0:T(8,128)S(1)}, f32[3,2,20,128]{3,2,1,0:T(8,128)S(1)}, u32[]{:S(2)}, u32[]{:S(2)}) collective-permute-start(f32[3,2,20,128]{3,2,1,0:T(8,128)S(1)} %get-tuple-element.15), channel_id=1, source_target_pairs={{0,8},{4,12},{8,16},{12,20},{16,24},{20,28},{24,0},{28,4},{1,9},{5... | collective-permute-start | bytes 184328 | tf_op jit(solution)/shard_map/ppermute | solution.py:24
  15.9 2.3 %collective-permute-start.5 = (f32[3,2,20,128]{3,2,1,0:T(8,128)S(1)}, f32[3,2,20,128]{3,2,1,0:T(8,128)S(1)}, u32[]{:S(2)}, u32[]{:S(2)}) collective-permute-start(f32[3,2,20,128]{3,2,1,0:T(8,128)S(1)} %get-tuple-element.14), channel_id=1, source_target_pairs={{0,24},{4,28},{8,0},{12,4},{16,8},{20,12},{24,16},{28,20},{1,25},{... | collective-permute-start | bytes 184328 | tf_op jit(solution)/shard_map/ppermute | solution.py:24
  18.3 4.6 %collective-permute-done.5.refs_4_ = f32[3,2,20,128]{3,2,1,0:T(8,128)S(1)} collective-permute-done((f32[3,2,20,128]{3,2,1,0:T(8,128)S(1)}, f32[3,2,20,128]{3,2,1,0:T(8,128)S(1)}, u32[]{:S(2)}, u32[]{:S(2)}) %collective-permute-start.5) | collective-permute-done | bytes 61472 | tf_op jit(solution)/shard_map/ppermute | solution.py:24
  22.9 0.0 collective-permute-done.2.refs_0_
  23.0 0.0 collective-permute-done.4.refs_3_
  23.0 0.0 collective-permute-done.3.refs_1_
  23.1 0.6 %add_reduce_fusion = f32[]{:T(128)} fusion(f32[128]{0:T(128)S(1)} %fusion.4, f32[128]{0:T(128)S(1)} %fusion.2, f32[128]{0:T(128)S(1)} %fusion.1, f32[128]{0:T(128)S(1)} %fusion.3, f32[128]{0:T(128)S(1)} %fusion), kind=kLoop, calls=%fused_computation.13 | loop fusion | flops 639 | bytes 2564 | tf_op jit(solution)/shard_map/reduce_sum | solution.py:338
  23.7 0.6 %mul.51 = f32[1,128]{1,0:T(1,128)S(1)} broadcast(f32[]{:T(128)} %add_reduce_fusion), dimensions={} | broadcast | bytes 516 | tf_op jit(solution)/shard_map/mul | solution.py:338
  24.3 0.2 collective-permute-start.8
  24.6 2.8 %collective-permute-start.7 = (f32[1,128]{1,0:T(1,128)S(1)}, f32[1,128]{1,0:T(1,128)S(1)}, u32[]{:S(2)}, u32[]{:S(2)}) collective-permute-start(f32[1,128]{1,0:T(1,128)S(1)} %mul.51), channel_id=1, source_target_pairs={{0,2},{1,3},{2,0},{3,1},{4,6},{5,7},{6,4},{7,5},{8,10},{9,11},{10,... | collective-permute-start | bytes 1544 | tf_op jit(solution)/shard_map/ppermute | solution.py:24
  27.4 1.4 %collective-permute-start.6 = (f32[1,128]{1,0:T(1,128)S(1)}, f32[1,128]{1,0:T(1,128)S(1)}, u32[]{:S(2)}, u32[]{:S(2)}) collective-permute-start(f32[1,128]{1,0:T(1,128)S(1)} %mul.51), channel_id=1, source_target_pairs={{0,16},{4,20},{8,24},{12,28},{16,0},{20,4},{24,8},{28,12},{1,17},{... | collective-permute-start | bytes 1544 | tf_op jit(solution)/shard_map/ppermute | solution.py:24
  28.8 0.0 copy-done.3
  28.8 0.0 copy-done.4
  28.8 0.0 copy-done.5
  28.8 24.1 %evolve.1 = (f32[3,4,8,128]{3,2,1,0:T(8,128)S(1)}, f32[6,4,8,128]{3,2,1,0:T(8,128)}) custom-call(f32[3,2,20,128]{3,2,1,0:T(8,128)S(1)} %collective-permute-done.2.refs_0_, f32[3,4,20,128]{3,2,1,0:T(8,128)S(1)} %collective-permute-done.3.refs_1_, f32[3,4,20,128]{3,2,1,0:T(8,128)S(1)} %pad_maximum_fusion.refs_2_, ...), custom_call_target="tpu_custom_call" | custom-call | flops 13488881664 | bytes 8000000 | tf_op jit(solution)/shard_map/evolve/pallas_call | solution.py:300
  52.9 0.0 collective-permute-done.8
  52.9 0.0 collective-permute-done.7
  52.9 0.0 collective-permute-done.6
  52.9 0.7 %add_add_fusion = f32[1,128]{1,0:T(1,128)S(1)} fusion(f32[1,128]{1,0:T(1,128)S(1)} %collective-permute-done.8, f32[1,128]{1,0:T(1,128)S(1)} %collective-permute-done.7, f32[1,128]{1,0:T(1,128)S(1)} %collective-permute-done.6, f32[]{:T(128)} %add_reduce_fusion), kind=kLoop, calls=%fused_computation.12 | loop fusion | flops 384 | bytes 2052 | tf_op jit(solution)/shard_map/add | solution.py:368
  53.7 0.6 %multiply_add_fusion = f32[3,4,8,128]{3,2,1,0:T(8,128)} fusion(f32[3,4,8,128]{3,2,1,0:T(8,128)S(1)} %get-tuple-element.12, f32[3,4,8,128]{3,2,1,0:T(8,128)S(1)} %copy-done.6, f32[]{:T(128)} %bitcast.3), kind=kLoop, calls=%fused_computation.11 | loop fusion | flops 24576 | bytes 147460 | tf_op jit(solution)/shard_map/add | solution.py:387
  (7 shorter events, 0.2 us)
Async XLA Ops:
  1.5 10.1 %collective-permute-start.1 = (f32[3,4,6,128]{3,2,1,0:T(8,128)S(1)}, f32[3,4,6,128]{3,2,1,0:T(8,128)S(1)}, u32[]{:S(2)}, u32[]{:S(2)}) collective-permute-start(f32[3,4,6,128]{3,2,1,0:T(8,128)S(1)} %get-tuple-element.17), channel_id=1, source_target_pairs={{0,3},{1,0},{2,1},{3,2},{4,7},{5,4},{6,5},{7,6},{8,11},{9,8},{10,9... | collective-permute-start | bytes 110600 | tf_op jit(solution)/shard_map/ppermute | solution.py:24
  6.6 5.9 %collective-permute-start = (f32[3,4,6,128]{3,2,1,0:T(8,128)S(1)}, f32[3,4,6,128]{3,2,1,0:T(8,128)S(1)}, u32[]{:S(2)}, u32[]{:S(2)}) collective-permute-start(f32[3,4,6,128]{3,2,1,0:T(8,128)S(1)} %get-tuple-element.16), channel_id=1, source_target_pairs={{0,1},{1,2},{2,3},{3,0},{4,5},{5,6},{6,7},{7,4},{8,9},{9,10},{10,1... | collective-permute-start | bytes 110600 | tf_op jit(solution)/shard_map/ppermute | solution.py:24
  7.8 1.0 %copy-start = (bf16[3,3,3,64,64]{4,3,2,1,0:T(8,128)(2,1)S(1)}, bf16[3,3,3,64,64]{4,3,2,1,0:T(8,128)(2,1)}, u32[]{:S(2)}) copy-start(bf16[3,3,3,64,64]{4,3,2,1,0:T(8,128)(2,1)} %w2.1) | copy-start | bytes 663556
  8.8 1.0 %copy-start.1 = (bf16[3,3,3,64,64]{4,3,2,1,0:T(8,128)(2,1)S(1)}, bf16[3,3,3,64,64]{4,3,2,1,0:T(8,128)(2,1)}, u32[]{:S(2)}) copy-start(bf16[3,3,3,64,64]{4,3,2,1,0:T(8,128)(2,1)} %w3.1) | copy-start | bytes 663556
  9.9 0.8 %copy-start.2 = (bf16[3,3,3,6,64]{4,3,2,1,0:T(8,128)(2,1)S(1)}, bf16[3,3,3,6,64]{4,3,2,1,0:T(8,128)(2,1)}, u32[]{:S(2)}) copy-start(bf16[3,3,3,6,64]{4,3,2,1,0:T(8,128)(2,1)} %w4.1) | copy-start | bytes 62212
  10.7 1.9 %copy-start.6 = (f32[3,4,8,128]{3,2,1,0:T(8,128)S(1)}, f32[3,4,8,128]{3,2,1,0:T(8,128)}, u32[]{:S(2)}) copy-start(f32[3,4,8,128]{3,2,1,0:T(8,128)} %param.8) | copy-start | bytes 147460
  10.7 18.1 %copy-start.3 = (f32[64]{0:T(128)S(1)}, f32[64]{0:T(128)}, u32[]{:S(2)}) copy-start(f32[64]{0:T(128)} %param.10) | copy-start | bytes 772
  10.7 18.1 %copy-start.4 = (f32[64]{0:T(128)S(1)}, f32[64]{0:T(128)}, u32[]{:S(2)}) copy-start(f32[64]{0:T(128)} %param.12) | copy-start | bytes 772
  10.7 18.1 %copy-start.5 = (f32[64]{0:T(128)S(1)}, f32[64]{0:T(128)}, u32[]{:S(2)}) copy-start(f32[64]{0:T(128)} %param.14) | copy-start | bytes 772
  12.6 10.4 %collective-permute-start.3 = (f32[3,4,20,128]{3,2,1,0:T(8,128)S(1)}, f32[3,4,20,128]{3,2,1,0:T(8,128)S(1)}, u32[]{:S(2)}, u32[]{:S(2)}) collective-permute-start(f32[3,4,20,128]{3,2,1,0:T(8,128)S(1)} %pad_maximum_fusion.refs_2_), channel_id=1, source_target_pairs={{0,4},{4,8},{8,12},{12,16},{16,20},{20,24},{24,28},{28,0},{1,5},{5... | collective-permute-start | bytes 368648 | tf_op jit(solution)/shard_map/ppermute | solution.py:24
  12.7 10.3 %collective-permute-start.4 = (f32[3,4,20,128]{3,2,1,0:T(8,128)S(1)}, f32[3,4,20,128]{3,2,1,0:T(8,128)S(1)}, u32[]{:S(2)}, u32[]{:S(2)}) collective-permute-start(f32[3,4,20,128]{3,2,1,0:T(8,128)S(1)} %pad_maximum_fusion.refs_2_), channel_id=1, source_target_pairs={{0,28},{4,0},{8,4},{12,8},{16,12},{20,16},{24,20},{28,24},{1,29},{... | collective-permute-start | bytes 368648 | tf_op jit(solution)/shard_map/ppermute | solution.py:24
  15.3 7.7 %collective-permute-start.2 = (f32[3,2,20,128]{3,2,1,0:T(8,128)S(1)}, f32[3,2,20,128]{3,2,1,0:T(8,128)S(1)}, u32[]{:S(2)}, u32[]{:S(2)}) collective-permute-start(f32[3,2,20,128]{3,2,1,0:T(8,128)S(1)} %get-tuple-element.15), channel_id=1, source_target_pairs={{0,8},{4,12},{8,16},{12,20},{16,24},{20,28},{24,0},{28,4},{1,9},{5... | collective-permute-start | bytes 184328 | tf_op jit(solution)/shard_map/ppermute | solution.py:24
  15.9 7.0 %collective-permute-start.5 = (f32[3,2,20,128]{3,2,1,0:T(8,128)S(1)}, f32[3,2,20,128]{3,2,1,0:T(8,128)S(1)}, u32[]{:S(2)}, u32[]{:S(2)}) collective-permute-start(f32[3,2,20,128]{3,2,1,0:T(8,128)S(1)} %get-tuple-element.14), channel_id=1, source_target_pairs={{0,24},{4,28},{8,0},{12,4},{16,8},{20,12},{24,16},{28,20},{1,25},{... | collective-permute-start | bytes 184328 | tf_op jit(solution)/shard_map/ppermute | solution.py:24
  24.3 28.6 %collective-permute-start.8 = (f32[1,128]{1,0:T(1,128)S(1)}, f32[1,128]{1,0:T(1,128)S(1)}, u32[]{:S(2)}, u32[]{:S(2)}) collective-permute-start(f32[1,128]{1,0:T(1,128)S(1)} %mul.51), channel_id=1, source_target_pairs={{0,18},{1,19},{2,16},{3,17},{4,22},{5,23},{6,20},{7,21},{8,26},{9,... | collective-permute-start | bytes 1544 | tf_op jit(solution)/shard_map/ppermute | solution.py:368
  24.6 28.3 %collective-permute-start.7 = (f32[1,128]{1,0:T(1,128)S(1)}, f32[1,128]{1,0:T(1,128)S(1)}, u32[]{:S(2)}, u32[]{:S(2)}) collective-permute-start(f32[1,128]{1,0:T(1,128)S(1)} %mul.51), channel_id=1, source_target_pairs={{0,2},{1,3},{2,0},{3,1},{4,6},{5,7},{6,4},{7,5},{8,10},{9,11},{10,... | collective-permute-start | bytes 1544 | tf_op jit(solution)/shard_map/ppermute | solution.py:24
  27.4 25.5 %collective-permute-start.6 = (f32[1,128]{1,0:T(1,128)S(1)}, f32[1,128]{1,0:T(1,128)S(1)}, u32[]{:S(2)}, u32[]{:S(2)}) collective-permute-start(f32[1,128]{1,0:T(1,128)S(1)} %mul.51), channel_id=1, source_target_pairs={{0,16},{4,20},{8,24},{12,28},{16,0},{20,4},{24,8},{28,12},{1,17},{... | collective-permute-start | bytes 1544 | tf_op jit(solution)/shard_map/ppermute | solution.py:24
where the time goes:
time: 54.7 us; the launch traced here: 54.3 us
  Pallas kernels  25 us (46%)
  starting transfers between devices  15.2 us (28%)
  waiting for transfers between devices  5.6 us (10%)
  local copies, waits for them, and re-layouts  5.57 us (10%)
  other arithmetic  2.11 us (4%)
  between operations  0.8 us (1%)
    pallas_call x1, Pallas kernels, evolve(): pl.pallas_call(functools.partial(main_kernel, len(pieces)), out_shape=(ja...  24.1 us
    ppermute x8, starting transfers between devices, shifted(): lax.ppermute(cells, axis, [(i, (i + step) % count) for i in range(count)])  15 us
    ppermute x8, waiting for transfers between devices, shifted(): lax.ppermute(cells, axis, [(i, (i + step) % count) for i in range(count)])  5.6 us
    unnamed x15, local copies, waits for them, and re-layouts  4.03 us
  transfers between devices with their start and end apart: 9, of which 2 were waited for; matrix products, arithmetic and copies ran while one was open for 2% of the time, Pallas kernels for 46%

commit v1 on v0

v1 whole, which is shorter than its diff:
```python
import functools

import jax
import jax.numpy as jnp
from jax import lax
from jax.experimental import pallas as pl
from jax.experimental.pallas import tpu as pltpu
from jax.sharding import PartitionSpec as P

time_step = 0.1
viscosity = 0.05
power_input = 5.0
pairing = ((0, 3, 4), (3, 1, 5), (4, 5, 2))
halo = 6
axis_x = ("grp", "gx")
axis_y = "gy"
groups = 8
f32 = jnp.float32
bf16 = jnp.bfloat16


def shifted(cells, axis, step):
    count = lax.axis_size(axis)
    return lax.ppermute(cells, axis, [(i, (i + step) % count) for i in range(count)])


def neighbours(cells, axis, dim):
    extent = cells.shape[dim]
    before, after = [], []
    hop, need = 1, halo
    while need > 0:
        width = min(extent, need)
        tail = lax.slice_in_dim(cells, extent - width, extent, axis=dim)
        head = lax.slice_in_dim(cells, 0, width, axis=dim)
        before.insert(0, shifted(tail, axis, hop))
        after.append(shifted(head, axis, -hop))
        hop += 1
        need -= width
    return before, after


def blocks_in(extent, count):
    size = 1
    while count % (2 * size) == 0 and 2 * size * extent <= extent + 2 * halo:
        size *= 2
    return size


def expand_hidden(w_ref, out_ref):
    outs, channels = w_ref.shape[3], w_ref.shape[4]
    zero = jnp.zeros((outs, channels), f32)
    blank = jnp.zeros((channels, 2 * outs), bf16)
    for dz in range(3):
        for xin in range(4):
            tall = []
            for dy in range(3):
                rows = [
                    w_ref[xin - xo, dy, dz].astype(f32) if 0 <= xin - xo <= 2 else zero
                    for xo in range(2)
                ]
                tall.append(jnp.concatenate(rows, axis=0).T.astype(bf16))
            for yin in range(4):
                base = ((dz * 4 + yin) * 4 + xin) * channels
                for yo in range(2):
                    piece = tall[yin - yo] if 0 <= yin - yo <= 2 else blank
                    out_ref[base : base + channels, yo * 2 * outs : (yo + 1) * 2 * outs] = piece


def selector(yo):
    row = lax.broadcasted_iota(jnp.int32, (128, 128), 0)
    column = lax.broadcasted_iota(jnp.int32, (128, 128), 1)
    group, yin, part = row >> 4, (row >> 2) & 3, row & 3
    one, two = jnp.where(group >= 3, 1, 0), jnp.where(group >= 6, 1, 0)
    along = one + two
    dz = group - 3 * along
    spare = part == 3
    along = jnp.where(spare, 2, along)
    dz = jnp.where(spare, 2, dz)
    part = jnp.where(spare, group, part)
    wanted = (yin - yo) * 32 + (3 * part + along) * 3 + dz
    fits = (yin >= yo) & (yin - yo <= 2) & (part <= 2) & (column == wanted)
    return jnp.where(fits, 1.0, 0.0).astype(bf16)


def expand_first(w_ref, out_ref, flat):
    features, outs = w_ref.shape[2], w_ref.shape[4]
    flat[...] = jnp.zeros_like(flat)
    for dx in range(3):
        for dy in range(3):
            for channel in range(features):
                row = dy * 32 + channel * 3
                flat[dx, row : row + 3, :] = w_ref[dx, dy, channel].astype(f32)
    zero = jnp.zeros(flat.shape[1:], f32)
    for yo in range(2):
        pick = selector(yo)
        for xin in range(4):
            sides = [flat[xin - xo] if 0 <= xin - xo <= 2 else zero for xo in range(2)]
            both = jnp.concatenate(sides, axis=1).astype(bf16)
            block = jnp.dot(pick, both, preferred_element_type=f32)
            out_ref[xin * 128 : (xin + 1) * 128, yo * 2 * outs : (yo + 1) * 2 * outs] = (
                block.astype(bf16)
            )


def expand_last(w_ref, out_ref):
    outs, channels = w_ref.shape[3], w_ref.shape[4]
    zero = jnp.zeros((8, channels), f32)
    pad = jnp.zeros((8 - outs, channels), f32)
    taps = {}
    for dx in range(3):
        for dy in range(3):
            for dz in range(3):
                taps[dx, dy, dz] = jnp.concatenate([w_ref[dx, dy, dz].astype(f32), pad], axis=0)
    for yin in range(4):
        for pair in range(2):
            column = []
            for dz in range(3):
                for yo in range(2):
                    for xo in range(2):
                        halves = []
                        for xin in (2 * pair, 2 * pair + 1):
                            dx, dy = xin - xo, yin - yo
                            inside = 0 <= dx <= 2 and 0 <= dy <= 2
                            halves.append(taps[dx, dy, dz] if inside else zero)
                        column.append(jnp.concatenate(halves, axis=1))
            base = (yin * 2 + pair) * 2 * channels
            out_ref[:, base : base + 2 * channels] = jnp.concatenate(column, axis=0).astype(bf16)


def first_kernel(w1, b1, out_ref, bias, flat):
    bias[...] = jnp.concatenate([b1[...]] * 4, axis=1)
    expand_first(w1, out_ref, flat)


def later_kernel(w2, w3, w4, o2, o3, o4):
    expand_hidden(w2, o2)
    expand_hidden(w3, o3)
    expand_last(w4, o4)


def ends_kernel(width, v, head, tail):
    extent = v.shape[2]
    head[...] = v[:, :, 0:width, :]
    tail[...] = v[:, :, extent - width : extent, :]


def whole():
    return pl.BlockSpec(memory_space=pltpu.VMEM)


def granted(mib):
    return pltpu.CompilerParams(vmem_limit_bytes=mib * 2**20)


def priced(flops):
    return pl.CostEstimate(flops=int(flops), bytes_accessed=10**6, transcendentals=0)


def ends(v, width):
    shape = jax.ShapeDtypeStruct(v.shape[:2] + (width,) + v.shape[3:], f32)
    return pl.pallas_call(
        functools.partial(ends_kernel, width),
        out_shape=(shape, shape),
        in_specs=[whole()],
        out_specs=(whole(), whole()),
        compiler_params=granted(4),
        name="ends",
    )(v)


def prepare_first(w1, b1):
    outs = w1.shape[3]
    w1 = jnp.transpose(w1, (0, 1, 4, 2, 3))
    return pl.pallas_call(
        first_kernel,
        out_shape=(
            jax.ShapeDtypeStruct((512, 4 * outs), bf16),
            jax.ShapeDtypeStruct((1, 4 * outs), f32),
        ),
        in_specs=[whole()] * 2,
        out_specs=(whole(),) * 2,
        scratch_shapes=[pltpu.VMEM((3, 128, outs), f32)],
        cost_estimate=pl.CostEstimate(flops=4 * 10**9, bytes_accessed=10**7, transcendentals=0),
        compiler_params=granted(10),
        name="prepare_first",
    )(w1, b1.reshape(1, -1))


def prepare_later(w2, w3, w4):
    outs, channels = w2.shape[3], w2.shape[4]
    return pl.pallas_call(
        later_kernel,
        out_shape=(
            jax.ShapeDtypeStruct((48 * channels, 4 * outs), bf16),
            jax.ShapeDtypeStruct((48 * channels, 4 * outs), bf16),
            jax.ShapeDtypeStruct((96, 16 * channels), bf16),
        ),
        in_specs=[whole()] * 3,
        out_specs=(whole(),) * 3,
        cost_estimate=priced(10**9),
        compiler_params=granted(10),
        name="prepare_later",
    )(w2, w3, w4)


def lay_rows(target, at, piece, x):
    count = piece.shape[2]
    for c in range(3):
        target[at, pl.ds(c, count, stride=4), :] = piece[c, x]
    target[at, pl.ds(3, count, stride=4), :] = jnp.zeros((count, piece.shape[3]), f32)


def features(rows, at, depth):
    total = rows.shape[1]
    center = rows[at + 1, 4 : total - 4, :]
    diffs = (
        (rows[at + 2, 4 : total - 4, :] - rows[at, 4 : total - 4, :]) * 0.5,
        (rows[at + 1, 8:total, :] - rows[at + 1, 0 : total - 8, :]) * 0.5,
        (pltpu.roll(center, depth - 1, 1) - pltpu.roll(center, 1, 1)) * 0.5,
    )
    parts = []
    for j in range(3):
        for amount in (1, 0, depth - 1):
            parts.append(pltpu.roll(diffs[j], amount, 1) if amount else diffs[j])
    spare = parts.pop()
    lane = lax.broadcasted_iota(jnp.int32, spare.shape, 0) & 3
    for c in range(3):
        parts[c] = jnp.where(lane == 3, pltpu.roll(spare, 3 - c, 0), parts[c])
    turned = []
    for half in range((total // 4 - 2) // 2 - 1):
        block = jnp.concatenate([part[8 * half : 8 * half + 16] for part in parts], axis=0)
        turned.append(block.astype(bf16).T)
    return turned


def merge(block):
    return block.reshape(block.shape[0] * block.shape[1], block.shape[2])


def layer(left, weight, bias, store, depth, variants):
    total = jnp.dot(left, weight[...], preferred_element_type=f32)
    value = jnp.tanh(total + bias)
    value = value.reshape(value.shape[0] // depth, depth, value.shape[1])
    width = value.shape[2] // 2
    for dz, amount in enumerate((1, 0, depth - 1)):
        if dz not in variants:
            continue
        moved = pltpu.roll(value, amount, 1) if amount else value
        moved = moved.astype(bf16)
        for yo in range(2):
            store(dz, yo, moved[:, :, yo * width : (yo + 1) * width])


every = (0, 1, 2)


def gather_hidden(source, xp, variants):
    rows = source.shape[-3] - 1
    parts = []
    for dz in variants:
        for yin in range(4):
            for pair in range(2):
                where = (xp + pair, yin % 2, slice(yin // 2, yin // 2 + rows))
                parts.append(merge(source[where if len(source.shape) == 5 else (dz, *where)]))
    return jnp.concatenate(parts, axis=1)


def store_hidden(target, xp):
    def store(dz, yo, block):
        target[(xp, yo) if len(target.shape) == 5 else (dz, xp, yo)] = block

    return store


def inner_kernel(low, near, own, far, w1, bias, h1, turned, rows):
    depth = own.shape[3]
    at = 0
    for piece in (near, own, far):
        for x in range(piece.shape[1]):
            lay_rows(rows, at, piece, x)
            at += 1

    def one(x, carry):
        for half, block in enumerate(features(rows, x, depth)):
            turned[x, half] = block
        return carry

    lax.fori_loop(0, turned.shape[0], one, 0, unroll=2)

    def step(q, carry):
        left = jnp.concatenate([merge(turned[2 * q + a]) for a in range(4)], axis=1)
        layer(left, w1, bias[...], store_hidden(h1, q + low), depth, every)
        return carry

    lax.fori_loop(0, turned.shape[0] // 2 - 1, step, 0)


def outer_kernel(count, box, *refs):
    pieces = refs[:count]
    turned, w1, bias, _, h1, energy, rows, edges = refs[count:]
    depth = pieces[0].shape[3]
    columns = [(piece, x) for piece in pieces for x in range(piece.shape[1])]
    need = rows.shape[1]
    edge = need - 2
    for side, part in enumerate((columns[:need], columns[-need:])):
        for at, (piece, x) in enumerate(part):
            lay_rows(rows.at[side], at, piece, x)
        for at in range(edge):
            for half, block in enumerate(features(rows.at[side], at, depth)):
                edges[side, at, half] = block
    inside = turned.shape[0]
    held = [edges.at[0, k] for k in range(edge)] + [turned.at[k] for k in range(inside)]
    held += [edges.at[1, k] for k in range(edge)]
    pairs = h1.shape[1]
    for k in range(edge // 2):
        for xp in (k, pairs - 1 - k):
            left = jnp.concatenate([merge(held[2 * xp + a][...]) for a in range(4)], axis=1)
            layer(left, w1, bias[...], store_hidden(h1, xp), depth, every)
    low_x, span_x, low_y, span_y = box
    total = None
    for piece, x in columns[low_x : low_x + span_x]:
        for c in range(3):
            part = piece[c, x, low_y : low_y + span_y, :]
            total = part * part if total is None else total + part * part
    energy[...] = jnp.broadcast_to(0.5 * jnp.sum(total, keepdims=True), energy.shape)


def second_kernel(h1, w2, bias, h2):
    depth = h1.shape[4]

    def step(xp, carry):
        layer(gather_hidden(h1, xp, every), w2, jnp.concatenate([bias[...]] * 4, axis=1), store_hidden(h2, xp), depth, every)
        return carry

    lax.fori_loop(0, h2.shape[1], step, 0)


def third_kernel(h2, w3, bias, h3):
    depth = h2.shape[4]

    def step(xp, carry):
        layer(gather_hidden(h2, xp, every), w3, jnp.concatenate([bias[...]] * 4, axis=1), store_hidden(h3, xp), depth, (1,))
        return carry

    lax.fori_loop(0, h3.shape[0], step, 0)


def final_kernel(cells, h3, w4, near, own, far, energy, updated_ref, stress_ref, tau):
    depth = own.shape[3]
    forcing = power_input / (2.0 * (energy[0, 0] / cells) + 1e-06)

    def final(xp, carry):
        sides = lax.dot_general(
            w4[...],
            gather_hidden(h3, xp, (1,)),
            (((1,), (1,)), ((), ())),
            preferred_element_type=f32,
        )
        for yp in range(sides.shape[1] // depth):
            part = sides[:, yp * depth : (yp + 1) * depth]
            total = pltpu.roll(part[0:32], 1, 1) + part[32:64] + pltpu.roll(part[64:96], depth - 1, 1)
            for yo in range(2):
                for xo in range(2):
                    cell = (2 * yo + xo) * 8
                    row = (2 * yp + yo) * 8
                    tau[2 * xp + xo, row : row + 8, :] = total[cell : cell + 8]
        return carry

    lax.fori_loop(0, h3.shape[0] - 1, final, 0)

    own_x, own_y = updated_ref.shape[1], updated_ref.shape[2]

    def stress_at(c, x, y):
        return tau[x, pl.ds(y * 8 + c, own_y, stride=8), :]

    def turn(a, amount):
        return pltpu.roll(a, amount % depth, 1)

    def vel(i, x, y):
        piece, at = own, x
        if x < 0:
            piece, at = near, x + near.shape[1]
        elif x >= own_x:
            piece, at = far, x - own_x
        return piece[i, at, halo + y : halo + y + own_y, :]

    for x in range(own_x):
        for c in range(6):
            stress_ref[c, x] = stress_at(c, x + 1, 1)
        center = [vel(i, x, 0) for i in range(3)]
        for i in range(3):
            xm, xp, ym, yp = vel(i, x - 1, 0), vel(i, x + 1, 0), vel(i, x, -1), vel(i, x, 1)
            zm, zp = turn(center[i], 1), turn(center[i], -1)
            advect = (
                center[0] * ((xp - xm) * 0.5)
                + center[1] * ((yp - ym) * 0.5)
                + center[2] * ((zp - zm) * 0.5)
            )
            laplacian = xp + xm + yp + ym + zm + zp - 6.0 * center[i]
            px, py, pz = pairing[i]
            along_z = stress_at(pz, x + 1, 1)
            divergence = (
                (stress_at(px, x + 2, 1) - stress_at(px, x, 1)) * 0.5
                + (stress_at(py, x + 1, 2) - stress_at(py, x + 1, 0)) * 0.5
                + (turn(along_z, -1) - turn(along_z, 1)) * 0.5
            )
            tendency = viscosity * laplacian - advect - divergence + forcing * center[i]
            updated_ref[i, x] = center[i] + time_step * tendency


def box_total(box, size_x, size_y):
    count_x, count_y = lax.axis_size(axis_x), lax.axis_size(axis_y)
    left_x, left_y = count_x // size_x, count_y // size_y
    if (left_x & (left_x - 1)) or (left_y & (left_y - 1)):
        return lax.psum(box, axis_x + (axis_y,)) / (size_x * size_y)
    while size_x < count_x:
        box = box + shifted(box, axis_x, size_x)
        size_x *= 2
    while size_y < count_y:
        box = box + shifted(box, axis_y, size_y)
        size_y *= 2
    return box


def local(v, w1, b1, w2, b2, w3, b3, w4):
    parts, own_x, own_y, depth = v.shape
    count_x, count_y = lax.axis_size(axis_x), lax.axis_size(axis_y)
    width = 2 * w2.shape[3]
    bias2, bias3 = b2.reshape(1, -1), b3.reshape(1, -1)
    if own_y >= halo:
        head, tail = ends(v, halo)
        before, after = [shifted(tail, axis_y, 1)], [shifted(head, axis_y, -1)]
    else:
        before, after = neighbours(v, axis_y, 2)
    e1, bias1 = prepare_first(w1, b1)
    strip = jnp.concatenate(before + [v] + after, axis=2)
    w2, w3, w4, strip = lax.optimization_barrier((w2, w3, w4, strip))
    e2, e3, e4 = prepare_later(w2, w3, w4)
    before, after = neighbours(strip, axis_x, 1)
    near, far = before[-1], after[0]
    pieces = before + [strip] + after

    wide_x, wide_y = own_x + 2 * halo, own_y + 2 * halo
    qx, qy = (wide_x - 4) // 2, (wide_y - 4) // 2
    edge = halo - near.shape[1]
    inside = wide_x - 2 - 2 * edge
    h1_shape = jax.ShapeDtypeStruct((3, qx, 2, qy, depth, width), bf16)
    h2_shape = jax.ShapeDtypeStruct((3, qx - 1, 2, qy - 1, depth, width), bf16)

    tile = 2 * depth * 256 * 256
    h1, turned = pl.pallas_call(
        functools.partial(inner_kernel, edge // 2),
        out_shape=(h1_shape, jax.ShapeDtypeStruct((inside, qy, depth, 128), bf16)),
        in_specs=[whole()] * 5,
        out_specs=(whole(), whole()),
        scratch_shapes=[pltpu.VMEM((inside + 2, 4 * wide_y, depth), f32)],
        cost_estimate=priced(4 * tile * qx * qy),
        compiler_params=granted(12),
        name="inner",
    )(near, strip, far, e1, bias1)

    size_x, size_y = blocks_in(own_x, count_x), blocks_in(own_y, count_y)
    box = (
        (wide_x - size_x * own_x) // 2,
        size_x * own_x,
        (wide_y - size_y * own_y) // 2,
        size_y * own_y,
    )
    count = len(pieces)
    h1, energy = pl.pallas_call(
        functools.partial(outer_kernel, count, box),
        out_shape=(h1_shape, jax.ShapeDtypeStruct((1, 1, 1, depth), f32)),
        in_specs=[whole()] * (count + 4),
        out_specs=(whole(), whole()),
        scratch_shapes=[
            pltpu.VMEM((2, edge + 2, 4 * wide_y, depth), f32),
            pltpu.VMEM((2, edge, qy, depth, 128), bf16),
        ],
        input_output_aliases={count + 3: 0},
        cost_estimate=priced(2 * tile * qx * qy),
        compiler_params=granted(12),
        name="outer",
    )(*pieces, turned, e1, bias1, h1)

    h2 = pl.pallas_call(
        second_kernel,
        out_shape=h2_shape,
        in_specs=[whole()] * 3,
        out_specs=whole(),
        cost_estimate=priced(12 * tile * (qx - 1) * (qy - 1)),
        compiler_params=granted(20),
        name="second",
    )(h1, e2, bias2)

    energy = box_total(energy, size_x, size_y)
    cells = own_x * own_y * depth * count_x * count_y

    h3 = pl.pallas_call(
        third_kernel,
        out_shape=jax.ShapeDtypeStruct((qx - 2, 2, qy - 2, depth, width), bf16),
        in_specs=[whole()] * 3,
        out_specs=whole(),
        cost_estimate=priced(12 * tile * (qx - 2) * (qy - 2)),
        compiler_params=granted(20),
        name="third",
    )(h2, e3, bias3)

    return pl.pallas_call(
        functools.partial(final_kernel, cells),
        out_shape=(
            jax.ShapeDtypeStruct(v.shape, f32),
            jax.ShapeDtypeStruct((6,) + v.shape[1:], f32),
        ),
        in_specs=[whole()] * 6,
        out_specs=(whole(), whole()),
        scratch_shapes=[pltpu.VMEM((2 * (qx - 3), 8 * 2 * (qy - 3), depth), f32)],
        cost_estimate=priced(8 * tile * (qx - 3) * (qy - 3)),
        compiler_params=granted(20),
        name="final",
    )(h3, e4, near, strip, far, energy)


def solution(mesh):
    block = P(None, axis_x, axis_y, None)
    return jax.shard_map(
        local,
        mesh=mesh,
        in_specs=(block,) + (P(),) * 7,
        out_specs=(block, block),
        check_vma=False,
    )
```

time: 54.7 us -> 42.2 us (0.77)
  waiting for transfers between devices: 5.6 us -> 1.04 us
  local copies, waits for them, and re-layouts: 5.57 us -> 2.37 us
  other arithmetic: 2.11 us -> 0.03 us
  Pallas kernels: 25 us -> 23.2 us
  starting transfers between devices: 15.2 us -> 14.6 us
    ppermute x8, waiting for transfers between devices: 5.6 us -> 1.04 us  [shifted(): lax.ppermute(cells, axis, [(i, (i + step) % count) for i in range(count)])]
    pallas_call x2 -> x8, Pallas kernels: 25 us -> 23.2 us  [the longest x1 8.14 us: local(): pl.pallas_call(second_kernel, out_shape=h2_shape, in_specs=[whole()] * 3,...]
    unnamed x15 -> x18, local copies, waits for them, and re-layouts: 4.03 us -> 2.36 us
    add x2, other arithmetic: 1.28 us -> 0.01 us  [the longest x1 0.01 us: box_total(): box = box + shifted(box, axis_x, size_x)]
    slice x1 -> x0, local copies, waits for them, and re-layouts: 0.88 us -> none  [neighbours(): tail = lax.slice_in_dim(cells, extent - width, extent, axis=dim)]
    reduce_sum x6 -> x0, other arithmetic: 0.8 us -> none  [the longest x1 0.61 us: box_energy(): return jnp.sum(total, keepdims=True).reshape(1, 1) * jnp.ones((1, 128), f32)]
    mul x1 -> x0, local copies, waits for them, and re-layouts: 0.65 us -> none  [box_energy(): return jnp.sum(total, keepdims=True).reshape(1, 1) * jnp.ones((1, 128), f32)]
  transfers between devices with their start and end apart: 9 -> 8, of which waited for: 2 -> 3; matrix products, arithmetic and copies ran while one was open for 2% -> 0% of each run, Pallas kernels for 46% -> 45%
where the time goes in v1:
time: 42.2 us; the launch traced here: 42 us
  Pallas kernels  23.2 us (55%)
  starting transfers between devices  14.6 us (35%)
  local copies, waits for them, and re-layouts  2.37 us (6%)
  waiting for transfers between devices  1.04 us (2%)
  between operations  0.77 us (2%)
    ppermute x8, starting transfers between devices, shifted(): lax.ppermute(cells, axis, [(i, (i + step) % count) for i in range(count)])  14.6 us
    pallas_call x1, Pallas kernels, local(): pl.pallas_call(second_kernel, out_shape=h2_shape, in_specs=[whole()] * 3,...  8.14 us
    pallas_call x1, Pallas kernels, local(): pl.pallas_call(third_kernel, out_shape=jax.ShapeDtypeStruct((qx - 2, 2, q...  5.55 us
    pallas_call x1, Pallas kernels, local(): pl.pallas_call(functools.partial(inner_kernel, edge // 2), out_shape=(h1_...  4.15 us
    pallas_call x1, Pallas kernels, local(): pl.pallas_call(functools.partial(final_kernel, cells), out_shape=(jax.Sha...  2.57 us
    unnamed x18, local copies, waits for them, and re-layouts  2.36 us
    pallas_call x1, Pallas kernels, local(): pl.pallas_call(functools.partial(outer_kernel, count, box), out_shape=(h1...  1.75 us
    ppermute x8, waiting for transfers between devices, shifted(): lax.ppermute(cells, axis, [(i, (i + step) % count) for i in range(count)])  1.04 us
  transfers between devices with their start and end apart: 8, of which 3 were waited for; matrix products, arithmetic and copies ran while one was open for 0% of the time, Pallas kernels for 45%

profile of v1, /device:TPU:0, one launch (start us, length us, event | category | flops | bytes accessed | tf_op | source)
XLA Modules:
  0.0 42.0 jit_solution(9682244358665618074)
XLA Ops:
  0.6 0.0 copy-start
  0.6 0.8 %copy-done = f32[3,4,8,128]{3,2,1,0:T(8,128)S(1)} copy-done((f32[3,4,8,128]{3,2,1,0:T(8,128)S(1)}, f32[3,4,8,128]{3,2,1,0:T(8,128)}, u32[]{:S(2)}) %copy-start) | copy-done | bytes 49176
  1.4 3.1 %collective-permute-start = (f32[3,4,6,128]{3,2,1,0:T(8,128)S(1)}, f32[3,4,6,128]{3,2,1,0:T(8,128)S(1)}, u32[]{:S(2)}, u32[]{:S(2)}) collective-permute-start(f32[3,4,6,128]{3,2,1,0:T(8,128)S(1)} %get-tuple-element.17), channel_id=1, source_target_pairs={{0,1},{1,2},{2,3},{3,0},{4,5},{5,6},{6,7},{7,4},{8,9},{9,10},{10,1... | collective-permute-start | bytes 110600 | tf_op jit(solution)/shard_map/ppermute | solution.py:24
  4.5 2.1 %collective-permute-start.1 = (f32[3,4,6,128]{3,2,1,0:T(8,128)S(1)}, f32[3,4,6,128]{3,2,1,0:T(8,128)S(1)}, u32[]{:S(2)}, u32[]{:S(2)}) collective-permute-start(f32[3,4,6,128]{3,2,1,0:T(8,128)S(1)} %get-tuple-element.18), channel_id=1, source_target_pairs={{0,3},{1,0},{2,1},{3,2},{4,7},{5,4},{6,5},{7,6},{8,11},{9,8},{10,9... | collective-permute-start | bytes 110600 | tf_op jit(solution)/shard_map/ppermute | solution.py:24
  6.6 0.0 copy-start.4
  6.6 0.9 %copy-done.4 = bf16[3,3,3,64,9]{3,2,4,1,0:T(4,128)(2,1)S(1)} copy-done((bf16[3,3,3,64,9]{3,2,4,1,0:T(4,128)(2,1)S(1)}, bf16[3,3,3,64,9]{3,2,4,1,0:T(4,128)(2,1)}, u32[]{:S(2)}) %copy-start.4) | copy-done | bytes 31128
  7.5 0.0 copy-start.6
  7.5 0.7 %copy-done.6 = f32[64]{0:T(128)S(1)} copy-done((f32[64]{0:T(128)S(1)}, f32[64]{0:T(128)}, u32[]{:S(2)}) %copy-start.6) | copy-done | bytes 280
  8.2 0.0 copy-start.1
  8.2 0.0 copy-start.2
  8.2 0.0 copy-start.3
  8.2 0.0 copy-start.5
  8.2 0.3 prepare_first.1
  8.5 0.2 collective-permute-done
  8.7 0.4 %collective-permute-done.1 = f32[3,4,6,128]{3,2,1,0:T(8,128)S(1)} collective-permute-done((f32[3,4,6,128]{3,2,1,0:T(8,128)S(1)}, f32[3,4,6,128]{3,2,1,0:T(8,128)S(1)}, u32[]{:S(2)}, u32[]{:S(2)}) %collective-permute-start.1) | collective-permute-done | bytes 36896 | tf_op jit(solution)/shard_map/ppermute | solution.py:24
  9.2 0.0 copy-done.1
  9.2 0.1 collective-permute-start.3
  9.3 2.6 %collective-permute-start.4 = (f32[3,4,20,128]{3,2,1,0:T(8,128)S(1)}, f32[3,4,20,128]{3,2,1,0:T(8,128)S(1)}, u32[]{:S(2)}, u32[]{:S(2)}) collective-permute-start(f32[3,4,20,128]{3,2,1,0:T(8,128)S(1)} %pad_maximum_fusion.own.refs_2_), channel_id=1, source_target_pairs={{0,28},{4,0},{8,4},{12,8},{16,12},{20,16},{24,20},{28,24},{1,29},{... | collective-permute-start | bytes 368648 | tf_op jit(solution)/shard_map/ppermute | solution.py:24
  11.9 0.6 %collective-permute-start.2 = (f32[3,2,20,128]{3,2,1,0:T(8,128)S(1)}, f32[3,2,20,128]{3,2,1,0:T(8,128)S(1)}, u32[]{:S(2)}, u32[]{:S(2)}) collective-permute-start(f32[3,2,20,128]{3,2,1,0:T(8,128)S(1)} %get-tuple-element.33), channel_id=1, source_target_pairs={{0,8},{4,12},{8,16},{12,20},{16,24},{20,28},{24,0},{28,4},{1,9},{5... | collective-permute-start | bytes 184328 | tf_op jit(solution)/shard_map/ppermute | solution.py:24
  12.6 2.3 %collective-permute-start.5 = (f32[3,2,20,128]{3,2,1,0:T(8,128)S(1)}, f32[3,2,20,128]{3,2,1,0:T(8,128)S(1)}, u32[]{:S(2)}, u32[]{:S(2)}) collective-permute-start(f32[3,2,20,128]{3,2,1,0:T(8,128)S(1)} %get-tuple-element.32), channel_id=1, source_target_pairs={{0,24},{4,28},{8,0},{12,4},{16,8},{20,12},{24,16},{28,20},{1,25},{... | collective-permute-start | bytes 184328 | tf_op jit(solution)/shard_map/ppermute | solution.py:24
  14.9 0.0 copy-done.2
  14.9 0.0 copy-done.3
  14.9 0.0 copy-done.5
  14.9 0.7 %prepare_later.1 = (bf16[3072,256]{1,0:T(8,128)(2,1)S(1)}, bf16[3072,256]{1,0:T(8,128)(2,1)S(1)}, bf16[96,1024]{1,0:T(8,128)(2,1)S(1)}) custom-call(bf16[3,3,3,64,64]{4,3,2,1,0:T(8,128)(2,1)S(1)} %copy-done.2, bf16[3,3,3,64,64]{4,3,2,1,0:T(8,128)(2,1)S(1)} %copy-done.3, bf16[3,3,3,6,64]{4,3,2,1,0:T(8,128)(2,1)S(1)} %copy-done.5), custom_call_target="tpu_custom_call" | custom-call | flops 1000000000 | bytes 1000000 | tf_op jit(solution)/shard_map/prepare_later/pallas_call | solution.py:191
  15.6 0.0 collective-permute-done.3.near.refs_1_
  15.6 0.4 collective-permute-done.4.far.refs_3_
  16.0 4.2 %inner.1 = (bf16[3,6,2,8,128,128]{5,4,3,2,1,0:T(8,128)(2,1)S(1)}, bf16[10,8,128,128]{3,2,1,0:T(8,128)(2,1)S(1)}) custom-call(f32[3,4,20,128]{3,2,1,0:T(8,128)S(1)} %collective-permute-done.3.near.refs_1_, f32[3,4,20,128]{3,2,1,0:T(8,128)S(1)} %pad_maximum_fusion.own.refs_2_, f32[3,4,20,128]{3,2,1,0:T(8,128)S(1)} %collective-permute-done.4.far.refs_3_, ...), custom_call_target="tpu_custom_call" | custom-call | flops 3221225472 | bytes 1000000 | tf_op jit(solution)/shard_map/inner/pallas_call | solution.py:451
  20.1 0.0 collective-permute-done.2.refs_0_
  20.2 0.0 collective-permute-done.5.refs_4_
  20.2 0.0 copy-start.7
  20.2 1.7 %outer.1 = (bf16[3,6,2,8,128,128]{5,4,3,2,1,0:T(8,128)(2,1)S(1)}, f32[1,1,1,128]{3,2,1,0:T(1,128)S(1)}) custom-call(f32[3,2,20,128]{3,2,1,0:T(8,128)S(1)} %collective-permute-done.2.refs_0_, f32[3,4,20,128]{3,2,1,0:T(8,128)S(1)} %collective-permute-done.3.near.refs_1_, ...), custom_call_target="tpu_custom_call", output_to_operand_aliasing={{0}: (8, {})} | custom-call | flops 1610612736 | bytes 1000000 | tf_op jit(solution)/shard_map/outer/pallas_call | solution.py:470
  21.9 1.6 %collective-permute-start.6 = (f32[1,1,1,128]{3,2,1,0:T(1,128)S(1)}, f32[1,1,1,128]{3,2,1,0:T(1,128)S(1)}, u32[]{:S(2)}, u32[]{:S(2)}) collective-permute-start(f32[1,1,1,128]{3,2,1,0:T(1,128)S(1)} %get-tuple-element.31), channel_id=1, source_target_pairs={{0,16},{4,20},{8,24},{12,28},{16,0},{20,4},{24,8},{28,12},{1,17},{... | collective-permute-start | bytes 1544 | tf_op jit(solution)/shard_map/ppermute | solution.py:24
  23.5 0.0 copy-done.7
  23.5 0.0 copy-start.8
  23.5 8.1 %second.1.h2 = bf16[3,5,2,7,128,128]{5,4,3,2,1,0:T(8,128)(2,1)S(1)} custom-call(bf16[3,6,2,8,128,128]{5,4,3,2,1,0:T(8,128)(2,1)S(1)} %get-tuple-element.24.h1, bf16[3072,256]{1,0:T(8,128)(2,1)S(1)} %get-tuple-element.28.w2, f32[1,64]{1,0:T(1,128)S(1)} %bitcast.6), custom_call_target="tpu_custom_call" | custom-call | flops 7046430720 | bytes 1000000 | tf_op jit(solution)/shard_map/second/pallas_call | solution.py:485
  31.7 0.0 collective-permute-done.6
  31.7 2.1 %collective-permute-start.7 = (f32[1,1,1,128]{3,2,1,0:T(1,128)S(1)}, f32[1,1,1,128]{3,2,1,0:T(1,128)S(1)}, u32[]{:S(2)}, u32[]{:S(2)}) collective-permute-start(f32[1,1,1,128]{3,2,1,0:T(1,128)S(1)} %add.6), channel_id=1, source_target_pairs={{0,2},{1,3},{2,0},{3,1},{4,6},{5,7},{6,4},{7,5},{8,10},{9,11},{10,... | collective-permute-start | bytes 1544 | tf_op jit(solution)/shard_map/ppermute | solution.py:24
  33.8 0.0 copy-done.8
  33.8 5.5 %third.1.h3 = bf16[4,2,6,128,128]{4,3,2,1,0:T(8,128)(2,1)S(1)} custom-call(bf16[3,5,2,7,128,128]{5,4,3,2,1,0:T(8,128)(2,1)S(1)} %second.1.h2, bf16[3072,256]{1,0:T(8,128)(2,1)S(1)} %get-tuple-element.29.w3, f32[1,64]{1,0:T(1,128)S(1)} %bitcast.7), custom_call_target="tpu_custom_call" | custom-call | flops 4831838208 | bytes 1000000 | tf_op jit(solution)/shard_map/third/pallas_call | solution.py:498
  39.4 0.0 collective-permute-done.7
  39.4 2.6 %final.1 = (f32[3,4,8,128]{3,2,1,0:T(8,128)}, f32[6,4,8,128]{3,2,1,0:T(8,128)}) custom-call(bf16[4,2,6,128,128]{4,3,2,1,0:T(8,128)(2,1)S(1)} %third.1.h3, bf16[96,1024]{1,0:T(8,128)(2,1)S(1)} %get-tuple-element.30.w4, f32[3,4,20,128]{3,2,1,0:T(8,128)S(1)} %collective-permute-done.3.near.refs_1_, f32[3,4,20,128]{3,2,1,0:T(8,128)S(1)} %pad_maximum_fusion.own.refs_2_, ...), custom_call_target="tpu_custom_call" | custom-call | flops 2013265920 | bytes 1000000 | tf_op jit(solution)/shard_map/final/pallas_call | solution.py:508
  (5 shorter events, 0.1 us)
Async XLA Ops:
  0.6 0.8 %copy-start = (f32[3,4,8,128]{3,2,1,0:T(8,128)S(1)}, f32[3,4,8,128]{3,2,1,0:T(8,128)}, u32[]{:S(2)}) copy-start(f32[3,4,8,128]{3,2,1,0:T(8,128)} %v.1) | copy-start | bytes 147460
  1.4 7.3 %collective-permute-start = (f32[3,4,6,128]{3,2,1,0:T(8,128)S(1)}, f32[3,4,6,128]{3,2,1,0:T(8,128)S(1)}, u32[]{:S(2)}, u32[]{:S(2)}) collective-permute-start(f32[3,4,6,128]{3,2,1,0:T(8,128)S(1)} %get-tuple-element.17), channel_id=1, source_target_pairs={{0,1},{1,2},{2,3},{3,0},{4,5},{5,6},{6,7},{7,4},{8,9},{9,10},{10,1... | collective-permute-start | bytes 110600 | tf_op jit(solution)/shard_map/ppermute | solution.py:24
  4.5 4.6 %collective-permute-start.1 = (f32[3,4,6,128]{3,2,1,0:T(8,128)S(1)}, f32[3,4,6,128]{3,2,1,0:T(8,128)S(1)}, u32[]{:S(2)}, u32[]{:S(2)}) collective-permute-start(f32[3,4,6,128]{3,2,1,0:T(8,128)S(1)} %get-tuple-element.18), channel_id=1, source_target_pairs={{0,3},{1,0},{2,1},{3,2},{4,7},{5,4},{6,5},{7,6},{8,11},{9,8},{10,9... | collective-permute-start | bytes 110600 | tf_op jit(solution)/shard_map/ppermute | solution.py:24
  6.6 0.9 %copy-start.4 = (bf16[3,3,3,64,9]{3,2,4,1,0:T(4,128)(2,1)S(1)}, bf16[3,3,3,64,9]{3,2,4,1,0:T(4,128)(2,1)}, u32[]{:S(2)}) copy-start(bf16[3,3,3,64,9]{3,2,4,1,0:T(4,128)(2,1)} %param.9) | copy-start | bytes 93316
  7.5 0.7 %copy-start.6 = (f32[64]{0:T(128)S(1)}, f32[64]{0:T(128)}, u32[]{:S(2)}) copy-start(f32[64]{0:T(128)} %param.10) | copy-start | bytes 772
  8.2 1.0 %copy-start.1 = (f32[3,4,8,128]{3,2,1,0:T(8,128)S(1)}, f32[3,4,8,128]{3,2,1,0:T(8,128)}, u32[]{:S(2)}) copy-start(f32[3,4,8,128]{3,2,1,0:T(8,128)} %v.1) | copy-start | bytes 147460
  8.2 6.7 %copy-start.2 = (bf16[3,3,3,64,64]{4,3,2,1,0:T(8,128)(2,1)S(1)}, bf16[3,3,3,64,64]{4,3,2,1,0:T(8,128)(2,1)}, u32[]{:S(2)}) copy-start(bf16[3,3,3,64,64]{4,3,2,1,0:T(8,128)(2,1)} %w2) | copy-start | bytes 663556
  8.2 6.7 %copy-start.3 = (bf16[3,3,3,64,64]{4,3,2,1,0:T(8,128)(2,1)S(1)}, bf16[3,3,3,64,64]{4,3,2,1,0:T(8,128)(2,1)}, u32[]{:S(2)}) copy-start(bf16[3,3,3,64,64]{4,3,2,1,0:T(8,128)(2,1)} %w3) | copy-start | bytes 663556
  8.2 6.7 %copy-start.5 = (bf16[3,3,3,6,64]{4,3,2,1,0:T(8,128)(2,1)S(1)}, bf16[3,3,3,6,64]{4,3,2,1,0:T(8,128)(2,1)}, u32[]{:S(2)}) copy-start(bf16[3,3,3,6,64]{4,3,2,1,0:T(8,128)(2,1)} %w4) | copy-start | bytes 62212
  9.2 6.4 %collective-permute-start.3 = (f32[3,4,20,128]{3,2,1,0:T(8,128)S(1)}, f32[3,4,20,128]{3,2,1,0:T(8,128)S(1)}, u32[]{:S(2)}, u32[]{:S(2)}) collective-permute-start(f32[3,4,20,128]{3,2,1,0:T(8,128)S(1)} %pad_maximum_fusion.own.refs_2_), channel_id=1, source_target_pairs={{0,4},{4,8},{8,12},{12,16},{16,20},{20,24},{24,28},{28,0},{1,5},{5... | collective-permute-start | bytes 368648 | tf_op jit(solution)/shard_map/ppermute | solution.py:24
  9.3 6.7 %collective-permute-start.4 = (f32[3,4,20,128]{3,2,1,0:T(8,128)S(1)}, f32[3,4,20,128]{3,2,1,0:T(8,128)S(1)}, u32[]{:S(2)}, u32[]{:S(2)}) collective-permute-start(f32[3,4,20,128]{3,2,1,0:T(8,128)S(1)} %pad_maximum_fusion.own.refs_2_), channel_id=1, source_target_pairs={{0,28},{4,0},{8,4},{12,8},{16,12},{20,16},{24,20},{28,24},{1,29},{... | collective-permute-start | bytes 368648 | tf_op jit(solution)/shard_map/ppermute | solution.py:24
  11.9 8.2 %collective-permute-start.2 = (f32[3,2,20,128]{3,2,1,0:T(8,128)S(1)}, f32[3,2,20,128]{3,2,1,0:T(8,128)S(1)}, u32[]{:S(2)}, u32[]{:S(2)}) collective-permute-start(f32[3,2,20,128]{3,2,1,0:T(8,128)S(1)} %get-tuple-element.33), channel_id=1, source_target_pairs={{0,8},{4,12},{8,16},{12,20},{16,24},{20,28},{24,0},{28,4},{1,9},{5... | collective-permute-start | bytes 184328 | tf_op jit(solution)/shard_map/ppermute | solution.py:24
  12.6 7.6 %collective-permute-start.5 = (f32[3,2,20,128]{3,2,1,0:T(8,128)S(1)}, f32[3,2,20,128]{3,2,1,0:T(8,128)S(1)}, u32[]{:S(2)}, u32[]{:S(2)}) collective-permute-start(f32[3,2,20,128]{3,2,1,0:T(8,128)S(1)} %get-tuple-element.32), channel_id=1, source_target_pairs={{0,24},{4,28},{8,0},{12,4},{16,8},{20,12},{24,16},{28,20},{1,25},{... | collective-permute-start | bytes 184328 | tf_op jit(solution)/shard_map/ppermute | solution.py:24
  20.2 3.4 %copy-start.7 = (f32[64]{0:T(128)S(1)}, f32[64]{0:T(128)}, u32[]{:S(2)}) copy-start(f32[64]{0:T(128)} %param.12) | copy-start | bytes 772
  21.9 9.7 %collective-permute-start.6 = (f32[1,1,1,128]{3,2,1,0:T(1,128)S(1)}, f32[1,1,1,128]{3,2,1,0:T(1,128)S(1)}, u32[]{:S(2)}, u32[]{:S(2)}) collective-permute-start(f32[1,1,1,128]{3,2,1,0:T(1,128)S(1)} %get-tuple-element.31), channel_id=1, source_target_pairs={{0,16},{4,20},{8,24},{12,28},{16,0},{20,4},{24,8},{28,12},{1,17},{... | collective-permute-start | bytes 1544 | tf_op jit(solution)/shard_map/ppermute | solution.py:24
  23.5 10.3 %copy-start.8 = (f32[64]{0:T(128)S(1)}, f32[64]{0:T(128)}, u32[]{:S(2)}) copy-start(f32[64]{0:T(128)} %param.14) | copy-start | bytes 772
  31.7 7.7 %collective-permute-start.7 = (f32[1,1,1,128]{3,2,1,0:T(1,128)S(1)}, f32[1,1,1,128]{3,2,1,0:T(1,128)S(1)}, u32[]{:S(2)}, u32[]{:S(2)}) collective-permute-start(f32[1,1,1,128]{3,2,1,0:T(1,128)S(1)} %add.6), channel_id=1, source_target_pairs={{0,2},{1,3},{2,0},{3,1},{4,6},{5,7},{6,4},{7,5},{8,10},{9,11},{10,... | collective-permute-start | bytes 1544 | tf_op jit(solution)/shard_map/ppermute | solution.py:24

commit v2 on v1

--- a/solution.py
+++ b/solution.py
@@ -22,21 +22,6 @@
 def shifted(cells, axis, step):
     count = lax.axis_size(axis)
     return lax.ppermute(cells, axis, [(i, (i + step) % count) for i in range(count)])
-
-
-def neighbours(cells, axis, dim):
-    extent = cells.shape[dim]
-    before, after = [], []
-    hop, need = 1, halo
-    while need > 0:
-        width = min(extent, need)
-        tail = lax.slice_in_dim(cells, extent - width, extent, axis=dim)
-        head = lax.slice_in_dim(cells, 0, width, axis=dim)
-        before.insert(0, shifted(tail, axis, hop))
-        after.append(shifted(head, axis, -hop))
-        hop += 1
-        need -= width
-    return before, after
 
 
 def blocks_in(extent, count):
@@ -139,9 +124,35 @@
 
 
 def ends_kernel(width, v, head, tail):
-    extent = v.shape[2]
-    head[...] = v[:, :, 0:width, :]
-    tail[...] = v[:, :, extent - width : extent, :]
+    parts, extent_x, extent_y = v.shape[:3]
+    for c in range(parts):
+        for x in range(extent_x):
+            at = (c * extent_x + x) * width
+            head[at : at + width, :] = v[c, x, 0:width, :]
+            tail[at : at + width, :] = v[c, x, extent_y - width : extent_y, :]
+
+
+def strip_kernel(v, left, right, strip, *rest):
+    parts, extent_x, extent_y = v.shape[:3]
+    width = left.shape[0] // (parts * extent_x)
+    tall = extent_y + 2 * width
+    for c in range(parts):
+        for x in range(extent_x):
+            source, at = (c * extent_x + x) * width, (c * extent_x + x) * tall
+            middle = at + width
+            strip[at:middle, :] = left[source : source + width, :]
+            strip[middle : middle + extent_y, :] = v[c, x]
+            strip[middle + extent_y : at + tall, :] = right[source : source + width, :]
+    if rest:
+        low, high, hold = rest
+        reach = low.shape[0] // (parts * tall)
+        for target, first in ((low, extent_x - reach), (high, 0)):
+            for c in range(parts):
+                start = (c * extent_x + first) * tall
+                hold[c * reach * tall : (c + 1) * reach * tall, :] = strip[
+                    start : start + reach * tall, :
+                ]
+            target[...] = hold[...].astype(target.dtype)
 
 
 def whole():
@@ -157,7 +168,7 @@
 
 
 def ends(v, width):
-    shape = jax.ShapeDtypeStruct(v.shape[:2] + (width,) + v.shape[3:], f32)
+    shape = jax.ShapeDtypeStruct((v.shape[0] * v.shape[1] * width, v.shape[3]), f32)
     return pl.pallas_call(
         functools.partial(ends_kernel, width),
         out_shape=(shape, shape),
@@ -166,6 +177,25 @@
         compiler_params=granted(4),
         name="ends",
     )(v)
+
+
+def strips(v, left, right, reach):
+    parts, extent_x, extent_y, depth = v.shape
+    tall = extent_y + 2 * halo
+    outs = [jax.ShapeDtypeStruct((parts * extent_x * tall, depth), f32)]
+    scratch = []
+    if reach:
+        outs += [jax.ShapeDtypeStruct((parts * reach * tall, depth), f32)] * 2
+        scratch = [pltpu.VMEM((parts * reach * tall, depth), f32)]
+    return pl.pallas_call(
+        strip_kernel,
+        out_shape=outs,
+        in_specs=[whole()] * 3,
+        out_specs=[whole()] * len(outs),
+        scratch_shapes=scratch,
+        compiler_params=granted(4),
+        name="strips",
+    )(v, left, right)
 
 
 def prepare_first(w1, b1):
@@ -203,11 +233,11 @@
     )(w2, w3, w4)
 
 
-def lay_rows(target, at, piece, x):
-    count = piece.shape[2]
+def lay_rows(target, at, piece, x, wide, tall):
     for c in range(3):
-        target[at, pl.ds(c, count, stride=4), :] = piece[c, x]
-    target[at, pl.ds(3, count, stride=4), :] = jnp.zeros((count, piece.shape[3]), f32)
+        start = (c * wide + x) * tall
+        target[at, pl.ds(c, tall, stride=4), :] = piece[start : start + tall, :]
+    target[at, pl.ds(3, tall, stride=4), :] = jnp.zeros((tall, piece.shape[1]), f32)
 
 
 def features(rows, at, depth):
@@ -273,11 +303,12 @@
 
 
 def inner_kernel(low, near, own, far, w1, bias, h1, turned, rows):
-    depth = own.shape[3]
+    depth, tall = own.shape[1], rows.shape[1] // 4
+    wide = own.shape[0] // (3 * tall)
     at = 0
     for piece in (near, own, far):
-        for x in range(piece.shape[1]):
-            lay_rows(rows, at, piece, x)
+        for x in range(wide):
+            lay_rows(rows, at, piece, x, wide, tall)
             at += 1
 
     def one(x, carry):
@@ -285,26 +316,32 @@
             turned[x, half] = block
         return carry
 
-    lax.fori_loop(0, turned.shape[0], one, 0, unroll=2)
+    lax.fori_loop(0, turned.shape[0], one, 0, unroll=True)
 
     def step(q, carry):
         left = jnp.concatenate([merge(turned[2 * q + a]) for a in range(4)], axis=1)
         layer(left, w1, bias[...], store_hidden(h1, q + low), depth, every)
         return carry
 
-    lax.fori_loop(0, turned.shape[0] // 2 - 1, step, 0)
-
-
-def outer_kernel(count, box, *refs):
-    pieces = refs[:count]
-    turned, w1, bias, _, h1, energy, rows, edges = refs[count:]
-    depth = pieces[0].shape[3]
-    columns = [(piece, x) for piece in pieces for x in range(piece.shape[1])]
+    lax.fori_loop(0, turned.shape[0] // 2 - 1, step, 0, unroll=True)
+
+
+def outer_kernel(box, *refs):
+    low, near, own, far, high, turned, w1, bias, _, h1, energy, rows, edges, ends = refs
+    depth, tall = own.shape[1], rows.shape[2] // 4
+    wide = own.shape[0] // (3 * tall)
+    reach = low.shape[0] // (3 * tall)
+    ends[0] = low[...].astype(f32)
+    ends[1] = high[...].astype(f32)
+    columns = [(ends.at[0], x, reach) for x in range(reach)]
+    for piece in (near, own, far):
+        columns += [(piece, x, wide) for x in range(wide)]
+    columns += [(ends.at[1], x, reach) for x in range(reach)]
     need = rows.shape[1]
     edge = need - 2
     for side, part in enumerate((columns[:need], columns[-need:])):
-        for at, (piece, x) in enumerate(part):
-            lay_rows(rows.at[side], at, piece, x)
+        for at, (piece, x, extent) in enumerate(part):
+            lay_rows(rows.at[side], at, piece, x, extent, tall)
         for at in range(edge):
             for half, block in enumerate(features(rows.at[side], at, depth)):
                 edges[side, at, half] = block
@@ -318,9 +355,10 @@
             layer(left, w1, bias[...], store_hidden(h1, xp), depth, every)
     low_x, span_x, low_y, span_y = box
     total = None
-    for piece, x in columns[low_x : low_x + span_x]:
+    for piece, x, extent in columns[low_x : low_x + span_x]:
         for c in range(3):
-            part = piece[c, x, low_y : low_y + span_y, :]
+            start = (c * extent + x) * tall + low_y
+            part = piece[start : start + span_y, :]
             total = part * part if total is None else total + part * part
     energy[...] = jnp.broadcast_to(0.5 * jnp.sum(total, keepdims=True), energy.shape)
 
@@ -332,7 +370,7 @@
         layer(gather_hidden(h1, xp, every), w2, jnp.concatenate([bias[...]] * 4, axis=1), store_hidden(h2, xp), depth, every)
         return carry
 
-    lax.fori_loop(0, h2.shape[1], step, 0)
+    lax.fori_loop(0, h2.shape[1], step, 0, unroll=True)
 
 
 def third_kernel(h2, w3, bias, h3):
@@ -342,11 +380,11 @@
         layer(gather_hidden(h2, xp, every), w3, jnp.concatenate([bias[...]] * 4, axis=1), store_hidden(h3, xp), depth, (1,))
         return carry
 
-    lax.fori_loop(0, h3.shape[0], step, 0)
+    lax.fori_loop(0, h3.shape[0], step, 0, unroll=True)
 
 
 def final_kernel(cells, h3, w4, near, own, far, energy, updated_ref, stress_ref, tau):
-    depth = own.shape[3]
+    depth = own.shape[1]
     forcing = power_input / (2.0 * (energy[0, 0] / cells) + 1e-06)
 
     def final(xp, carry):
@@ -366,7 +404,7 @@
                     tau[2 * xp + xo, row : row + 8, :] = total[cell : cell + 8]
         return carry
 
-    lax.fori_loop(0, h3.shape[0] - 1, final, 0)
+    lax.fori_loop(0, h3.shape[0] - 1, final, 0, unroll=True)
 
     own_x, own_y = updated_ref.shape[1], updated_ref.shape[2]
 
@@ -379,10 +417,11 @@
     def vel(i, x, y):
         piece, at = own, x
         if x < 0:
-            piece, at = near, x + near.shape[1]
+            piece, at = near, x + own_x
         elif x >= own_x:
             piece, at = far, x - own_x
-        return piece[i, at, halo + y : halo + y + own_y, :]
+        start = (i * own_x + at) * (own_y + 2 * halo) + halo + y
+        return piece[start : start + own_y, :]
 
     for x in range(own_x):
         for c in range(6):
@@ -427,22 +466,19 @@
     count_x, count_y = lax.axis_size(axis_x), lax.axis_size(axis_y)
     width = 2 * w2.shape[3]
     bias2, bias3 = b2.reshape(1, -1), b3.reshape(1, -1)
-    if own_y >= halo:
-        head, tail = ends(v, halo)
-        before, after = [shifted(tail, axis_y, 1)], [shifted(head, axis_y, -1)]
-    else:
-        before, after = neighbours(v, axis_y, 2)
+    head, tail = ends(v, halo)
+    left, right = shifted(tail, axis_y, 1), shifted(head, axis_y, -1)
     e1, bias1 = prepare_first(w1, b1)
-    strip = jnp.concatenate(before + [v] + after, axis=2)
+    left, right, e1, bias1 = lax.optimization_barrier((left, right, e1, bias1))
+    edge = halo - own_x
+    strip, low, high = strips(v, left, right, edge)
     w2, w3, w4, strip = lax.optimization_barrier((w2, w3, w4, strip))
     e2, e3, e4 = prepare_later(w2, w3, w4)
-    before, after = neighbours(strip, axis_x, 1)
-    near, far = before[-1], after[0]
-    pieces = before + [strip] + after
+    near, far = shifted(strip, axis_x, 1), shifted(strip, axis_x, -1)
+    low, high = shifted(low, axis_x, 2), shifted(high, axis_x, -2)
 
     wide_x, wide_y = own_x + 2 * halo, own_y + 2 * halo
     qx, qy = (wide_x - 4) // 2, (wide_y - 4) // 2
-    edge = halo - near.shape[1]
     inside = wide_x - 2 - 2 * edge
     h1_shape = jax.ShapeDtypeStruct((3, qx, 2, qy, depth, width), bf16)
     h2_shape = jax.ShapeDtypeStruct((3, qx - 1, 2, qy - 1, depth, width), bf16)
@@ -466,21 +502,21 @@
         (wide_y - size_y * own_y) // 2,
         size_y * own_y,
     )
-    count = len(pieces)
     h1, energy = pl.pallas_call(
-        functools.partial(outer_kernel, count, box),
+        functools.partial(outer_kernel, box),
         out_shape=(h1_shape, jax.ShapeDtypeStruct((1, 1, 1, depth), f32)),
-        in_specs=[whole()] * (count + 4),
+        in_specs=[whole()] * 9,
         out_specs=(whole(), whole()),
         scratch_shapes=[
             pltpu.VMEM((2, edge + 2, 4 * wide_y, depth), f32),
             pltpu.VMEM((2, edge, qy, depth, 128), bf16),
+            pltpu.VMEM((2,) + low.shape, f32),
         ],
-        input_output_aliases={count + 3: 0},
+        input_output_aliases={8: 0},
         cost_estimate=priced(2 * tile * qx * qy),
         compiler_params=granted(12),
         name="outer",
-    )(*pieces, turned, e1, bias1, h1)
+    )(low, near, strip, far, high, turned, e1, bias1, h1)
 
     h2 = pl.pallas_call(
         second_kernel,

time: 42.2 us -> 39.7 us (0.941)
  Pallas kernels: 23.2 us -> 21.3 us
  waiting for transfers between devices: 1.04 us -> 0.4 us
    ppermute x8, waiting for transfers between devices: 1.04 us -> 0.4 us  [shifted(): lax.ppermute(cells, axis, [(i, (i + step) % count) for i in range(count)])]
    pallas_call x1, Pallas kernels: 4.15 us -> 3.57 us  [local(): pl.pallas_call(functools.partial(inner_kernel, edge // 2), out_shape=(h1_...]
    pallas_call x1, Pallas kernels: 5.55 us -> 5.02 us  [local(): pl.pallas_call(third_kernel, out_shape=jax.ShapeDtypeStruct((qx - 2, 2, q...]
    pallas_call x1, Pallas kernels: 2.57 us -> 2.1 us  [local(): pl.pallas_call(functools.partial(final_kernel, cells), out_shape=(jax.Sha...]
    pallas_call x1 -> x2, Pallas kernels: 1.75 us -> 1.79 us  [the longest x1 1.77 us: local(): pl.pallas_call(functools.partial(outer_kernel, box), out_shape=(h1_shape,...]
  transfers between devices with their start and end apart: 8 -> 8, of which waited for: 3 -> 2; matrix products, arithmetic and copies ran while one was open for 0% -> 0% of each run, Pallas kernels for 45% -> 44%
where the time goes in v2:
time: 39.7 us; the launch traced here: 39.5 us
  Pallas kernels  21.3 us (54%)
  starting transfers between devices  14.6 us (37%)
  local copies, waits for them, and re-layouts  2.44 us (6%)
  between operations  0.78 us (2%)
  waiting for transfers between devices  0.4 us (1%)
    ppermute x8, starting transfers between devices, shifted(): lax.ppermute(cells, axis, [(i, (i + step) % count) for i in range(count)])  14.6 us
    pallas_call x1, Pallas kernels, local(): pl.pallas_call(second_kernel, out_shape=h2_shape, in_specs=[whole()] * 3,...  7.78 us
    pallas_call x1, Pallas kernels, local(): pl.pallas_call(third_kernel, out_shape=jax.ShapeDtypeStruct((qx - 2, 2, q...  5.02 us
    pallas_call x1, Pallas kernels, local(): pl.pallas_call(functools.partial(inner_kernel, edge // 2), out_shape=(h1_...  3.57 us
    unnamed x18, local copies, waits for them, and re-layouts  2.44 us
    pallas_call x1, Pallas kernels, local(): pl.pallas_call(functools.partial(final_kernel, cells), out_shape=(jax.Sha...  2.1 us
    pallas_call x1, Pallas kernels, local(): pl.pallas_call(functools.partial(outer_kernel, box), out_shape=(h1_shape,...  1.77 us
  transfers between devices with their start and end apart: 8, of which 2 were waited for; matrix products, arithmetic and copies ran while one was open for 0% of the time, Pallas kernels for 44%

profile of v2, /device:TPU:0, one launch (start us, length us, event | category | flops | bytes accessed | tf_op | source)
XLA Modules:
  0.0 39.5 jit_solution(13103359038895999617)
XLA Ops:
  0.6 0.0 copy-start
  0.6 0.8 %copy-done = f32[3,4,8,128]{3,2,1,0:T(8,128)S(1)} copy-done((f32[3,4,8,128]{3,2,1,0:T(8,128)S(1)}, f32[3,4,8,128]{3,2,1,0:T(8,128)}, u32[]{:S(2)}) %copy-start) | copy-done | bytes 49176
  1.4 3.1 %collective-permute-start = (f32[72,128]{1,0:T(8,128)S(1)}, f32[72,128]{1,0:T(8,128)S(1)}, u32[]{:S(2)}, u32[]{:S(2)}) collective-permute-start(f32[72,128]{1,0:T(8,128)S(1)} %get-tuple-element.24), channel_id=1, source_target_pairs={{0,1},{1,2},{2,3},{3,0},{4,5},{5,6},{6,7},{7,4},{8,9},{9,10},{10,1... | collective-permute-start | bytes 110600 | tf_op jit(solution)/shard_map/ppermute | solution.py:24
  4.5 2.1 %collective-permute-start.1 = (f32[72,128]{1,0:T(8,128)S(1)}, f32[72,128]{1,0:T(8,128)S(1)}, u32[]{:S(2)}, u32[]{:S(2)}) collective-permute-start(f32[72,128]{1,0:T(8,128)S(1)} %get-tuple-element.25), channel_id=1, source_target_pairs={{0,3},{1,0},{2,1},{3,2},{4,7},{5,4},{6,5},{7,6},{8,11},{9,8},{10,9... | collective-permute-start | bytes 110600 | tf_op jit(solution)/shard_map/ppermute | solution.py:24
  6.6 0.0 copy-start.4
  6.6 0.9 %copy-done.4 = bf16[3,3,3,64,9]{3,2,4,1,0:T(4,128)(2,1)S(1)} copy-done((bf16[3,3,3,64,9]{3,2,4,1,0:T(4,128)(2,1)S(1)}, bf16[3,3,3,64,9]{3,2,4,1,0:T(4,128)(2,1)}, u32[]{:S(2)}) %copy-start.4) | copy-done | bytes 31128
  7.5 0.0 copy-start.6
  7.5 0.7 %copy-done.6 = f32[64]{0:T(128)S(1)} copy-done((f32[64]{0:T(128)S(1)}, f32[64]{0:T(128)}, u32[]{:S(2)}) %copy-start.6) | copy-done | bytes 280
  8.2 0.0 copy-start.1
  8.2 0.0 copy-start.2
  8.2 0.0 copy-start.3
  8.2 0.0 copy-start.5
  8.2 0.3 prepare_first.1
  8.5 0.1 collective-permute-done.left
  8.6 0.3 collective-permute-done.1.right
  8.9 0.1 copy-done.1
  9.0 0.1 collective-permute-start.3
  9.1 2.6 %collective-permute-start.4 = (f32[240,128]{1,0:T(8,128)S(1)}, f32[240,128]{1,0:T(8,128)S(1)}, u32[]{:S(2)}, u32[]{:S(2)}) collective-permute-start(f32[240,128]{1,0:T(8,128)S(1)} %get-tuple-element.32.own.refs_2_), channel_id=1, source_target_pairs={{0,28},{4,0},{8,4},{12,8},{16,12},{20,16},{24,20},{28,24},{1,29},{... | collective-permute-start | bytes 368648 | tf_op jit(solution)/shard_map/ppermute | solution.py:24
  11.7 0.7 %collective-permute-start.2 = (f32[120,128]{1,0:T(8,128)S(1)}, f32[120,128]{1,0:T(8,128)S(1)}, u32[]{:S(2)}, u32[]{:S(2)}) collective-permute-start(f32[120,128]{1,0:T(8,128)S(1)} %get-tuple-element.30), channel_id=1, source_target_pairs={{0,8},{4,12},{8,16},{12,20},{16,24},{20,28},{24,0},{28,4},{1,9},{5... | collective-permute-start | bytes 184328 | tf_op jit(solution)/shard_map/ppermute | solution.py:24
  12.5 2.2 %collective-permute-start.5 = (f32[120,128]{1,0:T(8,128)S(1)}, f32[120,128]{1,0:T(8,128)S(1)}, u32[]{:S(2)}, u32[]{:S(2)}) collective-permute-start(f32[120,128]{1,0:T(8,128)S(1)} %get-tuple-element.33), channel_id=1, source_target_pairs={{0,24},{4,28},{8,0},{12,4},{16,8},{20,12},{24,16},{28,20},{1,25},{... | collective-permute-start | bytes 184328 | tf_op jit(solution)/shard_map/ppermute | solution.py:24
  14.6 0.0 copy-done.2
  14.6 0.0 copy-done.3
  14.6 0.0 copy-done.5
  14.6 0.7 %prepare_later.1 = (bf16[3072,256]{1,0:T(8,128)(2,1)S(1)}, bf16[3072,256]{1,0:T(8,128)(2,1)S(1)}, bf16[96,1024]{1,0:T(8,128)(2,1)S(1)}) custom-call(bf16[3,3,3,64,64]{4,3,2,1,0:T(8,128)(2,1)S(1)} %copy-done.2, bf16[3,3,3,64,64]{4,3,2,1,0:T(8,128)(2,1)S(1)} %copy-done.3, bf16[3,3,3,6,64]{4,3,2,1,0:T(8,128)(2,1)S(1)} %copy-done.5), custom_call_target="tpu_custom_call" | custom-call | flops 1000000000 | bytes 1000000 | tf_op jit(solution)/shard_map/prepare_later/pallas_call | solution.py:221
  15.3 0.0 collective-permute-done.3.near.refs_1_
  15.4 0.0 collective-permute-done.4.far.refs_3_
  15.4 3.6 %inner.1 = (bf16[3,6,2,8,128,128]{5,4,3,2,1,0:T(8,128)(2,1)S(1)}, bf16[10,8,128,128]{3,2,1,0:T(8,128)(2,1)S(1)}) custom-call(f32[240,128]{1,0:T(8,128)S(1)} %collective-permute-done.3.near.refs_1_, f32[240,128]{1,0:T(8,128)S(1)} %get-tuple-element.32.own.refs_2_, f32[240,128]{1,0:T(8,128)S(1)} %collective-permute-done.4.far.refs_3_, ...), custom_call_target="tpu_custom_call" | custom-call | flops 3221225472 | bytes 1000000 | tf_op jit(solution)/shard_map/inner/pallas_call | solution.py:487
  18.9 0.0 collective-permute-done.2.refs_0_
  19.0 0.0 collective-permute-done.5.refs_4_
  19.0 0.0 copy-start.7
  19.0 1.8 %outer.1 = (bf16[3,6,2,8,128,128]{5,4,3,2,1,0:T(8,128)(2,1)S(1)}, f32[1,1,1,128]{3,2,1,0:T(1,128)S(1)}) custom-call(f32[120,128]{1,0:T(8,128)S(1)} %collective-permute-done.2.refs_0_, f32[240,128]{1,0:T(8,128)S(1)} %collective-permute-done.3.near.refs_1_, f32[240,128]{1,0:T(8,128)S(1)} %get-tuple-element.32.own.refs_2_, ...), custom_call_target="tpu_custom_call", output_to_operand_aliasing={{0}: (8, {})} | custom-call | flops 1610612736 | bytes 1000000 | tf_op jit(solution)/shard_map/outer/pallas_call | solution.py:505
  20.8 1.7 %collective-permute-start.6 = (f32[1,1,1,128]{3,2,1,0:T(1,128)S(1)}, f32[1,1,1,128]{3,2,1,0:T(1,128)S(1)}, u32[]{:S(2)}, u32[]{:S(2)}) collective-permute-start(f32[1,1,1,128]{3,2,1,0:T(1,128)S(1)} %get-tuple-element.45), channel_id=1, source_target_pairs={{0,16},{4,20},{8,24},{12,28},{16,0},{20,4},{24,8},{28,12},{1,17},{... | collective-permute-start | bytes 1544 | tf_op jit(solution)/shard_map/ppermute | solution.py:24
  22.5 0.0 copy-done.7
  22.5 0.0 copy-start.8
  22.5 7.8 %second.1.h2 = bf16[3,5,2,7,128,128]{5,4,3,2,1,0:T(8,128)(2,1)S(1)} custom-call(bf16[3,6,2,8,128,128]{5,4,3,2,1,0:T(8,128)(2,1)S(1)} %get-tuple-element.38.h1, bf16[3072,256]{1,0:T(8,128)(2,1)S(1)} %get-tuple-element.42.w2, f32[1,64]{1,0:T(1,128)S(1)} %bitcast.6), custom_call_target="tpu_custom_call" | custom-call | flops 7046430720 | bytes 1000000 | tf_op jit(solution)/shard_map/second/pallas_call | solution.py:521
  30.3 0.0 collective-permute-done.6
  30.3 2.0 %collective-permute-start.7 = (f32[1,1,1,128]{3,2,1,0:T(1,128)S(1)}, f32[1,1,1,128]{3,2,1,0:T(1,128)S(1)}, u32[]{:S(2)}, u32[]{:S(2)}) collective-permute-start(f32[1,1,1,128]{3,2,1,0:T(1,128)S(1)} %add.6), channel_id=1, source_target_pairs={{0,2},{1,3},{2,0},{3,1},{4,6},{5,7},{6,4},{7,5},{8,10},{9,11},{10,... | collective-permute-start | bytes 1544 | tf_op jit(solution)/shard_map/ppermute | solution.py:24
  32.3 0.0 copy-done.8
  32.3 5.0 %third.1.h3 = bf16[4,2,6,128,128]{4,3,2,1,0:T(8,128)(2,1)S(1)} custom-call(bf16[3,5,2,7,128,128]{5,4,3,2,1,0:T(8,128)(2,1)S(1)} %second.1.h2, bf16[3072,256]{1,0:T(8,128)(2,1)S(1)} %get-tuple-element.43.w3, f32[1,64]{1,0:T(1,128)S(1)} %bitcast.7), custom_call_target="tpu_custom_call" | custom-call | flops 4831838208 | bytes 1000000 | tf_op jit(solution)/shard_map/third/pallas_call | solution.py:534
  37.4 0.0 collective-permute-done.7
  37.4 2.1 %final.1 = (f32[3,4,8,128]{3,2,1,0:T(8,128)}, f32[6,4,8,128]{3,2,1,0:T(8,128)}) custom-call(bf16[4,2,6,128,128]{4,3,2,1,0:T(8,128)(2,1)S(1)} %third.1.h3, bf16[96,1024]{1,0:T(8,128)(2,1)S(1)} %get-tuple-element.44.w4, f32[240,128]{1,0:T(8,128)S(1)} %collective-permute-done.3.near.refs_1_, f32[240,128]{1,0:T(8,128)S(1)} %get-tuple-element.32.own.refs_2_, ...), custom_call_target="tpu_custom_call" | custom-call | flops 2013265920 | bytes 1000000 | tf_op jit(solution)/shard_map/final/pallas_call | solution.py:544
  (4 shorter events, 0.0 us)
Async XLA Ops:
  0.6 0.8 %copy-start = (f32[3,4,8,128]{3,2,1,0:T(8,128)S(1)}, f32[3,4,8,128]{3,2,1,0:T(8,128)}, u32[]{:S(2)}) copy-start(f32[3,4,8,128]{3,2,1,0:T(8,128)} %v.3) | copy-start | bytes 147460
  1.4 7.2 %collective-permute-start = (f32[72,128]{1,0:T(8,128)S(1)}, f32[72,128]{1,0:T(8,128)S(1)}, u32[]{:S(2)}, u32[]{:S(2)}) collective-permute-start(f32[72,128]{1,0:T(8,128)S(1)} %get-tuple-element.24), channel_id=1, source_target_pairs={{0,1},{1,2},{2,3},{3,0},{4,5},{5,6},{6,7},{7,4},{8,9},{9,10},{10,1... | collective-permute-start | bytes 110600 | tf_op jit(solution)/shard_map/ppermute | solution.py:24
  4.5 4.4 %collective-permute-start.1 = (f32[72,128]{1,0:T(8,128)S(1)}, f32[72,128]{1,0:T(8,128)S(1)}, u32[]{:S(2)}, u32[]{:S(2)}) collective-permute-start(f32[72,128]{1,0:T(8,128)S(1)} %get-tuple-element.25), channel_id=1, source_target_pairs={{0,3},{1,0},{2,1},{3,2},{4,7},{5,4},{6,5},{7,6},{8,11},{9,8},{10,9... | collective-permute-start | bytes 110600 | tf_op jit(solution)/shard_map/ppermute | solution.py:24
  6.6 0.9 %copy-start.4 = (bf16[3,3,3,64,9]{3,2,4,1,0:T(4,128)(2,1)S(1)}, bf16[3,3,3,64,9]{3,2,4,1,0:T(4,128)(2,1)}, u32[]{:S(2)}) copy-start(bf16[3,3,3,64,9]{3,2,4,1,0:T(4,128)(2,1)} %param.9) | copy-start | bytes 93316
  7.5 0.7 %copy-start.6 = (f32[64]{0:T(128)S(1)}, f32[64]{0:T(128)}, u32[]{:S(2)}) copy-start(f32[64]{0:T(128)} %param.10) | copy-start | bytes 772
  8.2 0.8 %copy-start.1 = (f32[3,4,8,128]{3,2,1,0:T(8,128)S(1)}, f32[3,4,8,128]{3,2,1,0:T(8,128)}, u32[]{:S(2)}) copy-start(f32[3,4,8,128]{3,2,1,0:T(8,128)} %v.3) | copy-start | bytes 147460
  8.2 6.4 %copy-start.2 = (bf16[3,3,3,64,64]{4,3,2,1,0:T(8,128)(2,1)S(1)}, bf16[3,3,3,64,64]{4,3,2,1,0:T(8,128)(2,1)}, u32[]{:S(2)}) copy-start(bf16[3,3,3,64,64]{4,3,2,1,0:T(8,128)(2,1)} %w2) | copy-start | bytes 663556
  8.2 6.4 %copy-start.3 = (bf16[3,3,3,64,64]{4,3,2,1,0:T(8,128)(2,1)S(1)}, bf16[3,3,3,64,64]{4,3,2,1,0:T(8,128)(2,1)}, u32[]{:S(2)}) copy-start(bf16[3,3,3,64,64]{4,3,2,1,0:T(8,128)(2,1)} %w3) | copy-start | bytes 663556
  8.2 6.4 %copy-start.5 = (bf16[3,3,3,6,64]{4,3,2,1,0:T(8,128)(2,1)S(1)}, bf16[3,3,3,6,64]{4,3,2,1,0:T(8,128)(2,1)}, u32[]{:S(2)}) copy-start(bf16[3,3,3,6,64]{4,3,2,1,0:T(8,128)(2,1)} %w4) | copy-start | bytes 62212
  9.0 6.3 %collective-permute-start.3 = (f32[240,128]{1,0:T(8,128)S(1)}, f32[240,128]{1,0:T(8,128)S(1)}, u32[]{:S(2)}, u32[]{:S(2)}) collective-permute-start(f32[240,128]{1,0:T(8,128)S(1)} %get-tuple-element.32.own.refs_2_), channel_id=1, source_target_pairs={{0,4},{4,8},{8,12},{12,16},{16,20},{20,24},{24,28},{28,0},{1,5},{5... | collective-permute-start | bytes 368648 | tf_op jit(solution)/shard_map/ppermute | solution.py:24
  9.1 6.3 %collective-permute-start.4 = (f32[240,128]{1,0:T(8,128)S(1)}, f32[240,128]{1,0:T(8,128)S(1)}, u32[]{:S(2)}, u32[]{:S(2)}) collective-permute-start(f32[240,128]{1,0:T(8,128)S(1)} %get-tuple-element.32.own.refs_2_), channel_id=1, source_target_pairs={{0,28},{4,0},{8,4},{12,8},{16,12},{20,16},{24,20},{28,24},{1,29},{... | collective-permute-start | bytes 368648 | tf_op jit(solution)/shard_map/ppermute | solution.py:24
  11.7 7.2 %collective-permute-start.2 = (f32[120,128]{1,0:T(8,128)S(1)}, f32[120,128]{1,0:T(8,128)S(1)}, u32[]{:S(2)}, u32[]{:S(2)}) collective-permute-start(f32[120,128]{1,0:T(8,128)S(1)} %get-tuple-element.30), channel_id=1, source_target_pairs={{0,8},{4,12},{8,16},{12,20},{16,24},{20,28},{24,0},{28,4},{1,9},{5... | collective-permute-start | bytes 184328 | tf_op jit(solution)/shard_map/ppermute | solution.py:24
  12.5 6.5 %collective-permute-start.5 = (f32[120,128]{1,0:T(8,128)S(1)}, f32[120,128]{1,0:T(8,128)S(1)}, u32[]{:S(2)}, u32[]{:S(2)}) collective-permute-start(f32[120,128]{1,0:T(8,128)S(1)} %get-tuple-element.33), channel_id=1, source_target_pairs={{0,24},{4,28},{8,0},{12,4},{16,8},{20,12},{24,16},{28,20},{1,25},{... | collective-permute-start | bytes 184328 | tf_op jit(solution)/shard_map/ppermute | solution.py:24
  19.0 3.5 %copy-start.7 = (f32[64]{0:T(128)S(1)}, f32[64]{0:T(128)}, u32[]{:S(2)}) copy-start(f32[64]{0:T(128)} %param.12) | copy-start | bytes 772
  20.8 9.5 %collective-permute-start.6 = (f32[1,1,1,128]{3,2,1,0:T(1,128)S(1)}, f32[1,1,1,128]{3,2,1,0:T(1,128)S(1)}, u32[]{:S(2)}, u32[]{:S(2)}) collective-permute-start(f32[1,1,1,128]{3,2,1,0:T(1,128)S(1)} %get-tuple-element.45), channel_id=1, source_target_pairs={{0,16},{4,20},{8,24},{12,28},{16,0},{20,4},{24,8},{28,12},{1,17},{... | collective-permute-start | bytes 1544 | tf_op jit(solution)/shard_map/ppermute | solution.py:24
  22.5 9.8 %copy-start.8 = (f32[64]{0:T(128)S(1)}, f32[64]{0:T(128)}, u32[]{:S(2)}) copy-start(f32[64]{0:T(128)} %param.14) | copy-start | bytes 772
  30.3 7.1 %collective-permute-start.7 = (f32[1,1,1,128]{3,2,1,0:T(1,128)S(1)}, f32[1,1,1,128]{3,2,1,0:T(1,128)S(1)}, u32[]{:S(2)}, u32[]{:S(2)}) collective-permute-start(f32[1,1,1,128]{3,2,1,0:T(1,128)S(1)} %add.6), channel_id=1, source_target_pairs={{0,2},{1,3},{2,0},{3,1},{4,6},{5,7},{6,4},{7,5},{8,10},{9,11},{10,... | collective-permute-start | bytes 1544 | tf_op jit(solution)/shard_map/ppermute | solution.py:24

commit v3 on v2

--- a/solution.py
+++ b/solution.py
@@ -22,6 +22,12 @@
 def shifted(cells, axis, step):
     count = lax.axis_size(axis)
     return lax.ppermute(cells, axis, [(i, (i + step) % count) for i in range(count)])
+
+
+def swapped(cells, axis, odd):
+    count = lax.axis_size(axis)
+    order = [(i, (i + 1 if i % 2 == odd else i - 1) % count) for i in range(count)]
+    return lax.ppermute(cells, axis, order)
 
 
 def blocks_in(extent, count):
@@ -91,25 +97,21 @@
     outs, channels = w_ref.shape[3], w_ref.shape[4]
     zero = jnp.zeros((8, channels), f32)
     pad = jnp.zeros((8 - outs, channels), f32)
-    taps = {}
-    for dx in range(3):
+    for pair in range(2):
+        column = []
         for dy in range(3):
             for dz in range(3):
-                taps[dx, dy, dz] = jnp.concatenate([w_ref[dx, dy, dz].astype(f32), pad], axis=0)
-    for yin in range(4):
-        for pair in range(2):
-            column = []
-            for dz in range(3):
-                for yo in range(2):
-                    for xo in range(2):
-                        halves = []
-                        for xin in (2 * pair, 2 * pair + 1):
-                            dx, dy = xin - xo, yin - yo
-                            inside = 0 <= dx <= 2 and 0 <= dy <= 2
-                            halves.append(taps[dx, dy, dz] if inside else zero)
-                        column.append(jnp.concatenate(halves, axis=1))
-            base = (yin * 2 + pair) * 2 * channels
-            out_ref[:, base : base + 2 * channels] = jnp.concatenate(column, axis=0).astype(bf16)
+                for xo in range(2):
+                    halves = []
+                    for dx in (2 * pair - xo, 2 * pair + 1 - xo):
+                        if 0 <= dx <= 2:
+                            tap = w_ref[dx, dy, dz].astype(f32)
+                            halves.append(jnp.concatenate([tap, pad], axis=0))
+                        else:
+                            halves.append(zero)
+                    column.append(jnp.concatenate(halves, axis=1))
+        base = pair * 2 * channels
+        out_ref[:, base : base + 2 * channels] = jnp.concatenate(column, axis=0).astype(bf16)
 
 
 def first_kernel(w1, b1, out_ref, bias, flat):
@@ -223,7 +225,7 @@
         out_shape=(
             jax.ShapeDtypeStruct((48 * channels, 4 * outs), bf16),
             jax.ShapeDtypeStruct((48 * channels, 4 * outs), bf16),
-            jax.ShapeDtypeStruct((96, 16 * channels), bf16),
+            jax.ShapeDtypeStruct((144, 4 * channels), bf16),
         ),
         in_specs=[whole()] * 3,
         out_specs=(whole(),) * 3,
@@ -264,7 +266,7 @@
 
 
 def merge(block):
-    return block.reshape(block.shape[0] * block.shape[1], block.shape[2])
+    return block.reshape((block.shape[0] * block.shape[1],) + block.shape[2:])
 
 
 def layer(left, weight, bias, store, depth, variants):
@@ -302,14 +304,15 @@
     return store
 
 
-def inner_kernel(low, near, own, far, w1, bias, h1, turned, rows):
+def inner_kernel(low, odd, apart, own, twin, w1, bias, h1, turned, sides, rows):
     depth, tall = own.shape[1], rows.shape[1] // 4
     wide = own.shape[0] // (3 * tall)
-    at = 0
-    for piece in (near, own, far):
+    right = odd[0]
+    sides[right] = apart[...]
+    sides[1 - right] = twin[...]
+    for piece, at in ((apart, right * 2 * wide), (own, wide), (twin, (1 - right) * 2 * wide)):
         for x in range(wide):
-            lay_rows(rows, at, piece, x, wide, tall)
-            at += 1
+            lay_rows(rows, at + x, piece, x, wide, tall)
 
     def one(x, carry):
         for half, block in enumerate(features(rows, x, depth)):
@@ -327,7 +330,8 @@
 
 
 def outer_kernel(box, *refs):
-    low, near, own, far, high, turned, w1, bias, _, h1, energy, rows, edges, ends = refs
+    low, own, sides, high, turned, w1, bias, _, h1, energy, rows, edges, ends = refs
+    near, far = sides.at[0], sides.at[1]
     depth, tall = own.shape[1], rows.shape[2] // 4
     wide = own.shape[0] // (3 * tall)
     reach = low.shape[0] // (3 * tall)
@@ -383,25 +387,34 @@
     lax.fori_loop(0, h3.shape[0], step, 0, unroll=True)
 
 
-def final_kernel(cells, h3, w4, near, own, far, energy, updated_ref, stress_ref, tau):
+def final_kernel(cells, h3, w4, own, sides, energy, updated_ref, stress_ref, tau):
+    near, far = sides.at[0], sides.at[1]
     depth = own.shape[1]
     forcing = power_input / (2.0 * (energy[0, 0] / cells) + 1e-06)
 
+    rows = h3.shape[2]
+
     def final(xp, carry):
+        cells = [merge(merge(h3[xp + pair])) for pair in range(2)]
         sides = lax.dot_general(
             w4[...],
-            gather_hidden(h3, xp, (1,)),
+            jnp.concatenate(cells, axis=1),
             (((1,), (1,)), ((), ())),
             preferred_element_type=f32,
         )
-        for yp in range(sides.shape[1] // depth):
-            part = sides[:, yp * depth : (yp + 1) * depth]
-            total = pltpu.roll(part[0:32], 1, 1) + part[32:64] + pltpu.roll(part[64:96], depth - 1, 1)
-            for yo in range(2):
-                for xo in range(2):
-                    cell = (2 * yo + xo) * 8
-                    row = (2 * yp + yo) * 8
-                    tau[2 * xp + xo, row : row + 8, :] = total[cell : cell + 8]
+        for y in range(2 * rows - 2):
+            sums = []
+            for dz in range(3):
+                total = None
+                for dy in range(3):
+                    at = ((y + dy) % 2 * rows + (y + dy) // 2) * depth
+                    tap = (3 * dy + dz) * 16
+                    part = sides[tap : tap + 16, at : at + depth]
+                    total = part if total is None else total + part
+                sums.append(total)
+            total = pltpu.roll(sums[0], 1, 1) + sums[1] + pltpu.roll(sums[2], depth - 1, 1)
+            for xo in range(2):
+                tau[2 * xp + xo, y * 8 : y * 8 + 8, :] = total[xo * 8 : xo * 8 + 8]
         return carry
 
     lax.fori_loop(0, h3.shape[0] - 1, final, 0, unroll=True)
@@ -474,7 +487,8 @@
     strip, low, high = strips(v, left, right, edge)
     w2, w3, w4, strip = lax.optimization_barrier((w2, w3, w4, strip))
     e2, e3, e4 = prepare_later(w2, w3, w4)
-    near, far = shifted(strip, axis_x, 1), shifted(strip, axis_x, -1)
+    apart, twin = swapped(strip, axis_x, 1), swapped(strip, axis_x, 0)
+    odd = (lax.axis_index(axis_x) % 2).reshape(1)
     low, high = shifted(low, axis_x, 2), shifted(high, axis_x, -2)
 
     wide_x, wide_y = own_x + 2 * halo, own_y + 2 * halo
@@ -484,16 +498,20 @@
     h2_shape = jax.ShapeDtypeStruct((3, qx - 1, 2, qy - 1, depth, width), bf16)
 
     tile = 2 * depth * 256 * 256
-    h1, turned = pl.pallas_call(
+    h1, turned, sides = pl.pallas_call(
         functools.partial(inner_kernel, edge // 2),
-        out_shape=(h1_shape, jax.ShapeDtypeStruct((inside, qy, depth, 128), bf16)),
-        in_specs=[whole()] * 5,
-        out_specs=(whole(), whole()),
+        out_shape=(
+            h1_shape,
+            jax.ShapeDtypeStruct((inside, qy, depth, 128), bf16),
+            jax.ShapeDtypeStruct((2,) + strip.shape, f32),
+        ),
+        in_specs=[pl.BlockSpec(memory_space=pltpu.SMEM)] + [whole()] * 5,
+        out_specs=(whole(),) * 3,
         scratch_shapes=[pltpu.VMEM((inside + 2, 4 * wide_y, depth), f32)],
         cost_estimate=priced(4 * tile * qx * qy),
         compiler_params=granted(12),
         name="inner",
-    )(near, strip, far, e1, bias1)
+    )(odd, apart, strip, twin, e1, bias1)
 
     size_x, size_y = blocks_in(own_x, count_x), blocks_in(own_y, count_y)
     box = (
@@ -505,18 +523,18 @@
     h1, energy = pl.pallas_call(
         functools.partial(outer_kernel, box),
         out_shape=(h1_shape, jax.ShapeDtypeStruct((1, 1, 1, depth), f32)),
-        in_specs=[whole()] * 9,
+        in_specs=[whole()] * 8,
         out_specs=(whole(), whole()),
         scratch_shapes=[
             pltpu.VMEM((2, edge + 2, 4 * wide_y, depth), f32),
             pltpu.VMEM((2, edge, qy, depth, 128), bf16),
             pltpu.VMEM((2,) + low.shape, f32),
         ],
-        input_output_aliases={8: 0},
+        input_output_aliases={7: 0},
         cost_estimate=priced(2 * tile * qx * qy),
         compiler_params=granted(12),
         name="outer",
-    )(low, near, strip, far, high, turned, e1, bias1, h1)
+    )(low, strip, sides, high, turned, e1, bias1, h1)
 
     h2 = pl.pallas_call(
         second_kernel,
@@ -547,13 +565,13 @@
             jax.ShapeDtypeStruct(v.shape, f32),
             jax.ShapeDtypeStruct((6,) + v.shape[1:], f32),
         ),
-        in_specs=[whole()] * 6,
+        in_specs=[whole()] * 5,
         out_specs=(whole(), whole()),
         scratch_shapes=[pltpu.VMEM((2 * (qx - 3), 8 * 2 * (qy - 3), depth), f32)],
         cost_estimate=priced(8 * tile * (qx - 3) * (qy - 3)),
         compiler_params=granted(20),
         name="final",
-    )(h3, e4, near, strip, far, energy)
+    )(h3, e4, strip, sides, energy)
 
 
 def solution(mesh):

time: 39.7 us -> 38.7 us (0.975)
  starting transfers between devices: 14.6 us -> 13.1 us
  waiting for transfers between devices: 0.4 us -> 1.26 us
  Pallas kernels: 21.3 us -> 20.9 us
    ppermute x8 -> x6, starting transfers between devices: 14.6 us -> 11.2 us  [shifted(): lax.ppermute(cells, axis, [(i, (i + step) % count) for i in range(count)])]
    ppermute x0 -> x2, starting transfers between devices: none -> 1.83 us  [swapped(): return lax.ppermute(cells, axis, order)]
    ppermute x0 -> x2, waiting for transfers between devices: none -> 0.87 us  [swapped(): return lax.ppermute(cells, axis, order)]
  transfers between devices with their start and end apart: 8 -> 8, of which waited for: 2 -> 3; matrix products, arithmetic and copies ran while one was open for 0% -> 0% of each run, Pallas kernels for 44% -> 45%
where the time goes in v3:
time: 38.7 us; the launch traced here: 38.4 us
  Pallas kernels  20.9 us (54%)
  starting transfers between devices  13.1 us (34%)
  local copies, waits for them, and re-layouts  2.44 us (6%)
  waiting for transfers between devices  1.26 us (3%)
  between operations  0.75 us (2%)
    ppermute x6, starting transfers between devices, shifted(): lax.ppermute(cells, axis, [(i, (i + step) % count) for i in range(count)])  11.2 us
    pallas_call x1, Pallas kernels, local(): pl.pallas_call(second_kernel, out_shape=h2_shape, in_specs=[whole()] * 3,...  7.78 us
    pallas_call x1, Pallas kernels, local(): pl.pallas_call(third_kernel, out_shape=jax.ShapeDtypeStruct((qx - 2, 2, q...  5.02 us
    pallas_call x1, Pallas kernels, local(): pl.pallas_call(functools.partial(inner_kernel, edge // 2), out_shape=(h1_...  3.59 us
    unnamed x18, local copies, waits for them, and re-layouts  2.44 us
    ppermute x2, starting transfers between devices, swapped(): return lax.ppermute(cells, axis, order)  1.83 us
    pallas_call x1, Pallas kernels, local(): pl.pallas_call(functools.partial(outer_kernel, box), out_shape=(h1_shape,...  1.75 us
    pallas_call x1, Pallas kernels, local(): pl.pallas_call(functools.partial(final_kernel, cells), out_shape=(jax.Sha...  1.71 us
  transfers between devices with their start and end apart: 8, of which 3 were waited for; matrix products, arithmetic and copies ran while one was open for 0% of the time, Pallas kernels for 45%

profile of v3, /device:TPU:0, one launch (start us, length us, event | category | flops | bytes accessed | tf_op | source)
XLA Modules:
  0.0 38.4 jit_solution(10298102710078964559)
XLA Ops:
  0.6 0.0 copy-start
  0.6 0.8 %copy-done = f32[3,4,8,128]{3,2,1,0:T(8,128)S(1)} copy-done((f32[3,4,8,128]{3,2,1,0:T(8,128)S(1)}, f32[3,4,8,128]{3,2,1,0:T(8,128)}, u32[]{:S(2)}) %copy-start) | copy-done | bytes 49176
  1.4 3.1 %collective-permute-start = (f32[72,128]{1,0:T(8,128)S(1)}, f32[72,128]{1,0:T(8,128)S(1)}, u32[]{:S(2)}, u32[]{:S(2)}) collective-permute-start(f32[72,128]{1,0:T(8,128)S(1)} %get-tuple-element.25), channel_id=1, source_target_pairs={{0,1},{1,2},{2,3},{3,0},{4,5},{5,6},{6,7},{7,4},{8,9},{9,10},{10,1... | collective-permute-start | bytes 110600 | tf_op jit(solution)/shard_map/ppermute | solution.py:24
  4.5 2.1 %collective-permute-start.1 = (f32[72,128]{1,0:T(8,128)S(1)}, f32[72,128]{1,0:T(8,128)S(1)}, u32[]{:S(2)}, u32[]{:S(2)}) collective-permute-start(f32[72,128]{1,0:T(8,128)S(1)} %get-tuple-element.26), channel_id=1, source_target_pairs={{0,3},{1,0},{2,1},{3,2},{4,7},{5,4},{6,5},{7,6},{8,11},{9,8},{10,9... | collective-permute-start | bytes 110600 | tf_op jit(solution)/shard_map/ppermute | solution.py:24
  6.6 0.0 copy-start.4
  6.6 0.9 %copy-done.4 = bf16[3,3,3,64,9]{3,2,4,1,0:T(4,128)(2,1)S(1)} copy-done((bf16[3,3,3,64,9]{3,2,4,1,0:T(4,128)(2,1)S(1)}, bf16[3,3,3,64,9]{3,2,4,1,0:T(4,128)(2,1)}, u32[]{:S(2)}) %copy-start.4) | copy-done | bytes 31128
  7.5 0.0 copy-start.6
  7.5 0.7 %copy-done.6 = f32[64]{0:T(128)S(1)} copy-done((f32[64]{0:T(128)S(1)}, f32[64]{0:T(128)}, u32[]{:S(2)}) %copy-start.6) | copy-done | bytes 280
  8.2 0.0 copy-start.1
  8.2 0.0 copy-start.2
  8.2 0.0 copy-start.3
  8.2 0.0 copy-start.5
  8.2 0.3 prepare_first.1
  8.5 0.1 collective-permute-done.left
  8.6 0.3 collective-permute-done.1.right
  8.9 0.1 copy-done.1
  9.0 1.7 %collective-permute-start.3 = (f32[240,128]{1,0:T(8,128)S(1)}, f32[240,128]{1,0:T(8,128)S(1)}, u32[]{:S(2)}, u32[]{:S(2)}) collective-permute-start(f32[240,128]{1,0:T(8,128)S(1)} %get-tuple-element.33.own.refs_1_), channel_id=1, source_target_pairs={{0,28},{4,8},{8,4},{12,16},{16,12},{20,24},{24,20},{28,0},{1,29},{... | collective-permute-start | bytes 368648 | tf_op jit(solution)/shard_map/ppermute | solution.py:30
  10.7 0.2 collective-permute-start.4
  10.8 1.5 %collective-permute-start.2 = (f32[120,128]{1,0:T(8,128)S(1)}, f32[120,128]{1,0:T(8,128)S(1)}, u32[]{:S(2)}, u32[]{:S(2)}) collective-permute-start(f32[120,128]{1,0:T(8,128)S(1)} %get-tuple-element.31), channel_id=1, source_target_pairs={{0,8},{4,12},{8,16},{12,20},{16,24},{20,28},{24,0},{28,4},{1,9},{5... | collective-permute-start | bytes 184328 | tf_op jit(solution)/shard_map/ppermute | solution.py:24
  12.3 1.4 %collective-permute-start.5 = (f32[120,128]{1,0:T(8,128)S(1)}, f32[120,128]{1,0:T(8,128)S(1)}, u32[]{:S(2)}, u32[]{:S(2)}) collective-permute-start(f32[120,128]{1,0:T(8,128)S(1)} %get-tuple-element.37), channel_id=1, source_target_pairs={{0,24},{4,28},{8,0},{12,4},{16,8},{20,12},{24,16},{28,20},{1,25},{... | collective-permute-start | bytes 184328 | tf_op jit(solution)/shard_map/ppermute | solution.py:24
  13.8 0.0 copy-done.2
  13.8 0.0 copy-done.3
  13.8 0.0 copy-done.5
  13.8 0.7 %prepare_later.1 = (bf16[3072,256]{1,0:T(8,128)(2,1)S(1)}, bf16[3072,256]{1,0:T(8,128)(2,1)S(1)}, bf16[144,256]{1,0:T(8,128)(2,1)S(1)}) custom-call(bf16[3,3,3,64,64]{4,3,2,1,0:T(8,128)(2,1)S(1)} %copy-done.2, bf16[3,3,3,64,64]{4,3,2,1,0:T(8,128)(2,1)S(1)} %copy-done.3, bf16[3,3,3,6,64]{4,3,2,1,0:T(8,128)(2,1)S(1)} %copy-done.5), custom_call_target="tpu_custom_call" | custom-call | flops 1000000000 | bytes 1000000 | tf_op jit(solution)/shard_map/prepare_later/pallas_call | solution.py:223
  14.5 0.9 %collective-permute-done.3.apart = f32[240,128]{1,0:T(8,128)S(1)} collective-permute-done((f32[240,128]{1,0:T(8,128)S(1)}, f32[240,128]{1,0:T(8,128)S(1)}, u32[]{:S(2)}, u32[]{:S(2)}) %collective-permute-start.3) | collective-permute-done | bytes 122912 | tf_op jit(solution)/shard_map/ppermute | solution.py:30
  15.3 0.0 collective-permute-done.4.twin
  15.3 3.6 %inner.1 = (bf16[3,6,2,8,128,128]{5,4,3,2,1,0:T(8,128)(2,1)S(1)}, bf16[10,8,128,128]{3,2,1,0:T(8,128)(2,1)S(1)}, f32[2,240,128]{2,1,0:T(8,128)S(1)}) custom-call(s32[1]{0:T(128)} %bitcast.2.odd, f32[240,128]{1,0:T(8,128)S(1)} %collective-permute-done.3.apart, f32[240,128]{1,0:T(8,128)S(1)} %get-tuple-element.33.own.refs_1_, ...), custom_call_target="tpu_custom_call" | custom-call | flops 3221225472 | bytes 1000000 | tf_op jit(solution)/shard_map/inner/pallas_call | solution.py:501
  18.9 0.0 collective-permute-done.2.refs_0_
  18.9 0.0 collective-permute-done.5.refs_3_
  19.0 0.0 copy-start.7
  19.0 1.7 %outer.1 = (bf16[3,6,2,8,128,128]{5,4,3,2,1,0:T(8,128)(2,1)S(1)}, f32[1,1,1,128]{3,2,1,0:T(1,128)S(1)}) custom-call(f32[120,128]{1,0:T(8,128)S(1)} %collective-permute-done.2.refs_0_, f32[240,128]{1,0:T(8,128)S(1)} %get-tuple-element.33.own.refs_1_, f32[2,240,128]{2,1,0:T(8,128)S(1)} %get-tuple-element.36.refs_2_.sides, ...), custom_call_target="tpu_custom_call", output_to_operand_aliasing={{0}: (7, {})} | custom-call | flops 1610612736 | bytes 1000000 | tf_op jit(solution)/shard_map/outer/pallas_call | solution.py:523
  20.7 1.1 %collective-permute-start.6 = (f32[1,1,1,128]{3,2,1,0:T(1,128)S(1)}, f32[1,1,1,128]{3,2,1,0:T(1,128)S(1)}, u32[]{:S(2)}, u32[]{:S(2)}) collective-permute-start(f32[1,1,1,128]{3,2,1,0:T(1,128)S(1)} %get-tuple-element.47), channel_id=1, source_target_pairs={{0,16},{4,20},{8,24},{12,28},{16,0},{20,4},{24,8},{28,12},{1,17},{... | collective-permute-start | bytes 1544 | tf_op jit(solution)/shard_map/ppermute | solution.py:24
  21.8 0.0 copy-done.7
  21.8 0.0 copy-start.8
  21.8 7.8 %second.1.h2 = bf16[3,5,2,7,128,128]{5,4,3,2,1,0:T(8,128)(2,1)S(1)} custom-call(bf16[3,6,2,8,128,128]{5,4,3,2,1,0:T(8,128)(2,1)S(1)} %get-tuple-element.40.h1, bf16[3072,256]{1,0:T(8,128)(2,1)S(1)} %get-tuple-element.44.w2, f32[1,64]{1,0:T(1,128)S(1)} %bitcast.7), custom_call_target="tpu_custom_call" | custom-call | flops 7046430720 | bytes 1000000 | tf_op jit(solution)/shard_map/second/pallas_call | solution.py:539
  29.6 0.0 collective-permute-done.6
  29.6 2.0 %collective-permute-start.7 = (f32[1,1,1,128]{3,2,1,0:T(1,128)S(1)}, f32[1,1,1,128]{3,2,1,0:T(1,128)S(1)}, u32[]{:S(2)}, u32[]{:S(2)}) collective-permute-start(f32[1,1,1,128]{3,2,1,0:T(1,128)S(1)} %add.15), channel_id=1, source_target_pairs={{0,2},{1,3},{2,0},{3,1},{4,6},{5,7},{6,4},{7,5},{8,10},{9,11},{10,... | collective-permute-start | bytes 1544 | tf_op jit(solution)/shard_map/ppermute | solution.py:24
  31.7 0.0 copy-done.8
  31.7 5.0 %third.1.h3 = bf16[4,2,6,128,128]{4,3,2,1,0:T(8,128)(2,1)S(1)} custom-call(bf16[3,5,2,7,128,128]{5,4,3,2,1,0:T(8,128)(2,1)S(1)} %second.1.h2, bf16[3072,256]{1,0:T(8,128)(2,1)S(1)} %get-tuple-element.45.w3, f32[1,64]{1,0:T(1,128)S(1)} %bitcast.8), custom_call_target="tpu_custom_call" | custom-call | flops 4831838208 | bytes 1000000 | tf_op jit(solution)/shard_map/third/pallas_call | solution.py:552
  36.7 0.0 collective-permute-done.7
  36.7 1.7 %final.1 = (f32[3,4,8,128]{3,2,1,0:T(8,128)}, f32[6,4,8,128]{3,2,1,0:T(8,128)}) custom-call(bf16[4,2,6,128,128]{4,3,2,1,0:T(8,128)(2,1)S(1)} %third.1.h3, bf16[144,256]{1,0:T(8,128)(2,1)S(1)} %get-tuple-element.46.w4, f32[240,128]{1,0:T(8,128)S(1)} %get-tuple-element.33.own.refs_1_, f32[2,240,128]{2,1,0:T(8,128)S(1)} %get-tuple-element.36.refs_2_.sides, ...), custom_call_target="tpu_custom_call" | custom-call | flops 2013265920 | bytes 1000000 | tf_op jit(solution)/shard_map/final/pallas_call | solution.py:562
  (4 shorter events, 0.0 us)
Async XLA Ops:
  0.6 0.8 %copy-start = (f32[3,4,8,128]{3,2,1,0:T(8,128)S(1)}, f32[3,4,8,128]{3,2,1,0:T(8,128)}, u32[]{:S(2)}) copy-start(f32[3,4,8,128]{3,2,1,0:T(8,128)} %v.3) | copy-start | bytes 147460
  1.4 7.2 %collective-permute-start = (f32[72,128]{1,0:T(8,128)S(1)}, f32[72,128]{1,0:T(8,128)S(1)}, u32[]{:S(2)}, u32[]{:S(2)}) collective-permute-start(f32[72,128]{1,0:T(8,128)S(1)} %get-tuple-element.25), channel_id=1, source_target_pairs={{0,1},{1,2},{2,3},{3,0},{4,5},{5,6},{6,7},{7,4},{8,9},{9,10},{10,1... | collective-permute-start | bytes 110600 | tf_op jit(solution)/shard_map/ppermute | solution.py:24
  4.5 4.4 %collective-permute-start.1 = (f32[72,128]{1,0:T(8,128)S(1)}, f32[72,128]{1,0:T(8,128)S(1)}, u32[]{:S(2)}, u32[]{:S(2)}) collective-permute-start(f32[72,128]{1,0:T(8,128)S(1)} %get-tuple-element.26), channel_id=1, source_target_pairs={{0,3},{1,0},{2,1},{3,2},{4,7},{5,4},{6,5},{7,6},{8,11},{9,8},{10,9... | collective-permute-start | bytes 110600 | tf_op jit(solution)/shard_map/ppermute | solution.py:24
  6.6 0.9 %copy-start.4 = (bf16[3,3,3,64,9]{3,2,4,1,0:T(4,128)(2,1)S(1)}, bf16[3,3,3,64,9]{3,2,4,1,0:T(4,128)(2,1)}, u32[]{:S(2)}) copy-start(bf16[3,3,3,64,9]{3,2,4,1,0:T(4,128)(2,1)} %param.9) | copy-start | bytes 93316
  7.5 0.7 %copy-start.6 = (f32[64]{0:T(128)S(1)}, f32[64]{0:T(128)}, u32[]{:S(2)}) copy-start(f32[64]{0:T(128)} %param.10) | copy-start | bytes 772
  8.2 0.8 %copy-start.1 = (f32[3,4,8,128]{3,2,1,0:T(8,128)S(1)}, f32[3,4,8,128]{3,2,1,0:T(8,128)}, u32[]{:S(2)}) copy-start(f32[3,4,8,128]{3,2,1,0:T(8,128)} %v.3) | copy-start | bytes 147460
  8.2 5.6 %copy-start.2 = (bf16[3,3,3,64,64]{4,3,2,1,0:T(8,128)(2,1)S(1)}, bf16[3,3,3,64,64]{4,3,2,1,0:T(8,128)(2,1)}, u32[]{:S(2)}) copy-start(bf16[3,3,3,64,64]{4,3,2,1,0:T(8,128)(2,1)} %w2) | copy-start | bytes 663556
  8.2 5.6 %copy-start.3 = (bf16[3,3,3,64,64]{4,3,2,1,0:T(8,128)(2,1)S(1)}, bf16[3,3,3,64,64]{4,3,2,1,0:T(8,128)(2,1)}, u32[]{:S(2)}) copy-start(bf16[3,3,3,64,64]{4,3,2,1,0:T(8,128)(2,1)} %w3) | copy-start | bytes 663556
  8.2 5.6 %copy-start.5 = (bf16[3,3,3,6,64]{4,3,2,1,0:T(8,128)(2,1)S(1)}, bf16[3,3,3,6,64]{4,3,2,1,0:T(8,128)(2,1)}, u32[]{:S(2)}) copy-start(bf16[3,3,3,6,64]{4,3,2,1,0:T(8,128)(2,1)} %w4) | copy-start | bytes 62212
  9.0 6.3 %collective-permute-start.3 = (f32[240,128]{1,0:T(8,128)S(1)}, f32[240,128]{1,0:T(8,128)S(1)}, u32[]{:S(2)}, u32[]{:S(2)}) collective-permute-start(f32[240,128]{1,0:T(8,128)S(1)} %get-tuple-element.33.own.refs_1_), channel_id=1, source_target_pairs={{0,28},{4,8},{8,4},{12,16},{16,12},{20,24},{24,20},{28,0},{1,29},{... | collective-permute-start | bytes 368648 | tf_op jit(solution)/shard_map/ppermute | solution.py:30
  10.7 4.7 %collective-permute-start.4 = (f32[240,128]{1,0:T(8,128)S(1)}, f32[240,128]{1,0:T(8,128)S(1)}, u32[]{:S(2)}, u32[]{:S(2)}) collective-permute-start(f32[240,128]{1,0:T(8,128)S(1)} %get-tuple-element.33.own.refs_1_), channel_id=1, source_target_pairs={{0,4},{4,0},{8,12},{12,8},{16,20},{20,16},{24,28},{28,24},{1,5},{5... | collective-permute-start | bytes 368648 | tf_op jit(solution)/shard_map/ppermute | solution.py:30
  10.8 8.1 %collective-permute-start.2 = (f32[120,128]{1,0:T(8,128)S(1)}, f32[120,128]{1,0:T(8,128)S(1)}, u32[]{:S(2)}, u32[]{:S(2)}) collective-permute-start(f32[120,128]{1,0:T(8,128)S(1)} %get-tuple-element.31), channel_id=1, source_target_pairs={{0,8},{4,12},{8,16},{12,20},{16,24},{20,28},{24,0},{28,4},{1,9},{5... | collective-permute-start | bytes 184328 | tf_op jit(solution)/shard_map/ppermute | solution.py:24
  12.3 6.6 %collective-permute-start.5 = (f32[120,128]{1,0:T(8,128)S(1)}, f32[120,128]{1,0:T(8,128)S(1)}, u32[]{:S(2)}, u32[]{:S(2)}) collective-permute-start(f32[120,128]{1,0:T(8,128)S(1)} %get-tuple-element.37), channel_id=1, source_target_pairs={{0,24},{4,28},{8,0},{12,4},{16,8},{20,12},{24,16},{28,20},{1,25},{... | collective-permute-start | bytes 184328 | tf_op jit(solution)/shard_map/ppermute | solution.py:24
  19.0 2.9 %copy-start.7 = (f32[64]{0:T(128)S(1)}, f32[64]{0:T(128)}, u32[]{:S(2)}) copy-start(f32[64]{0:T(128)} %param.12) | copy-start | bytes 772
  20.7 8.9 %collective-permute-start.6 = (f32[1,1,1,128]{3,2,1,0:T(1,128)S(1)}, f32[1,1,1,128]{3,2,1,0:T(1,128)S(1)}, u32[]{:S(2)}, u32[]{:S(2)}) collective-permute-start(f32[1,1,1,128]{3,2,1,0:T(1,128)S(1)} %get-tuple-element.47), channel_id=1, source_target_pairs={{0,16},{4,20},{8,24},{12,28},{16,0},{20,4},{24,8},{28,12},{1,17},{... | collective-permute-start | bytes 1544 | tf_op jit(solution)/shard_map/ppermute | solution.py:24
  21.8 9.8 %copy-start.8 = (f32[64]{0:T(128)S(1)}, f32[64]{0:T(128)}, u32[]{:S(2)}) copy-start(f32[64]{0:T(128)} %param.14) | copy-start | bytes 772
  29.6 7.1 %collective-permute-start.7 = (f32[1,1,1,128]{3,2,1,0:T(1,128)S(1)}, f32[1,1,1,128]{3,2,1,0:T(1,128)S(1)}, u32[]{:S(2)}, u32[]{:S(2)}) collective-permute-start(f32[1,1,1,128]{3,2,1,0:T(1,128)S(1)} %add.15), channel_id=1, source_target_pairs={{0,2},{1,3},{2,0},{3,1},{4,6},{5,7},{6,4},{7,5},{8,10},{9,11},{10,... | collective-permute-start | bytes 1544 | tf_op jit(solution)/shard_map/ppermute | solution.py:24

commit v4 on v3

--- a/solution.py
+++ b/solution.py
@@ -28,6 +28,11 @@
     count = lax.axis_size(axis)
     order = [(i, (i + 1 if i % 2 == odd else i - 1) % count) for i in range(count)]
     return lax.ppermute(cells, axis, order)
+
+
+def crossed(cells, axis):
+    count = lax.axis_size(axis)
+    return lax.ppermute(cells, axis, [(i, (i - 2 if i % 2 else i + 2) % count) for i in range(count)])
 
 
 def blocks_in(extent, count):
@@ -134,7 +139,7 @@
             tail[at : at + width, :] = v[c, x, extent_y - width : extent_y, :]
 
 
-def strip_kernel(v, left, right, strip, *rest):
+def strip_kernel(odd, v, left, right, strip, piece):
     parts, extent_x, extent_y = v.shape[:3]
     width = left.shape[0] // (parts * extent_x)
     tall = extent_y + 2 * width
@@ -145,16 +150,24 @@
             strip[at:middle, :] = left[source : source + width, :]
             strip[middle : middle + extent_y, :] = v[c, x]
             strip[middle + extent_y : at + tall, :] = right[source : source + width, :]
-    if rest:
-        low, high, hold = rest
-        reach = low.shape[0] // (parts * tall)
-        for target, first in ((low, extent_x - reach), (high, 0)):
-            for c in range(parts):
-                start = (c * extent_x + first) * tall
-                hold[c * reach * tall : (c + 1) * reach * tall, :] = strip[
-                    start : start + reach * tall, :
-                ]
-            target[...] = hold[...].astype(target.dtype)
+    reach = piece.shape[0] // (parts * tall)
+    size = reach * tall
+    for c in range(parts):
+        head = c * extent_x * tall
+        tail = head + (extent_x - reach) * tall
+        piece[c * size : (c + 1) * size, :] = jnp.where(
+            odd[0] == 1, strip[head : head + size, :], strip[tail : tail + size, :]
+        )
+
+
+def energy_kernel(box, own, twin, energy):
+    wide, tall, low, span = box
+    total = None
+    for piece in (own, twin):
+        for k in range(3 * wide):
+            part = piece[k * tall + low : k * tall + low + span, :]
+            total = part * part if total is None else total + part * part
+    energy[...] = jnp.broadcast_to(0.5 * jnp.sum(total, keepdims=True), energy.shape)
 
 
 def whole():
@@ -181,23 +194,24 @@
     )(v)
 
 
-def strips(v, left, right, reach):
+def scalar():
+    return pl.BlockSpec(memory_space=pltpu.SMEM)
+
+
+def strips(odd, v, left, right, reach):
     parts, extent_x, extent_y, depth = v.shape
     tall = extent_y + 2 * halo
-    outs = [jax.ShapeDtypeStruct((parts * extent_x * tall, depth), f32)]
-    scratch = []
-    if reach:
-        outs += [jax.ShapeDtypeStruct((parts * reach * tall, depth), f32)] * 2
-        scratch = [pltpu.VMEM((parts * reach * tall, depth), f32)]
     return pl.pallas_call(
         strip_kernel,
-        out_shape=outs,
-        in_specs=[whole()] * 3,
-        out_specs=[whole()] * len(outs),
-        scratch_shapes=scratch,
+        out_shape=(
+            jax.ShapeDtypeStruct((parts * extent_x * tall, depth), f32),
+            jax.ShapeDtypeStruct((parts * reach * tall, depth), f32),
+        ),
+        in_specs=[scalar()] + [whole()] * 3,
+        out_specs=(whole(), whole()),
         compiler_params=granted(4),
         name="strips",
-    )(v, left, right)
+    )(odd, v, left, right)
 
 
 def prepare_first(w1, b1):
@@ -304,7 +318,7 @@
     return store
 
 
-def inner_kernel(low, odd, apart, own, twin, w1, bias, h1, turned, sides, rows):
+def inner_kernel(edge, odd, apart, own, twin, w1, bias, h1, turned, sides, rows):
     depth, tall = own.shape[1], rows.shape[1] // 4
     wide = own.shape[0] // (3 * tall)
     right = odd[0]
@@ -313,78 +327,81 @@
     for piece, at in ((apart, right * 2 * wide), (own, wide), (twin, (1 - right) * 2 * wide)):
         for x in range(wide):
             lay_rows(rows, at + x, piece, x, wide, tall)
+    first = (1 - right) * edge
+    inside = turned.shape[0] - edge
 
     def one(x, carry):
         for half, block in enumerate(features(rows, x, depth)):
-            turned[x, half] = block
+            turned[x + first, half] = block
         return carry
 
-    lax.fori_loop(0, turned.shape[0], one, 0, unroll=True)
+    lax.fori_loop(0, inside, one, 0, unroll=True)
+    low = (1 - right) * (edge // 2)
 
     def step(q, carry):
-        left = jnp.concatenate([merge(turned[2 * q + a]) for a in range(4)], axis=1)
+        left = jnp.concatenate([merge(turned[2 * q + first + a]) for a in range(4)], axis=1)
         layer(left, w1, bias[...], store_hidden(h1, q + low), depth, every)
         return carry
 
-    lax.fori_loop(0, turned.shape[0] // 2 - 1, step, 0, unroll=True)
-
-
-def outer_kernel(box, *refs):
-    low, own, sides, high, turned, w1, bias, _, h1, energy, rows, edges, ends = refs
-    near, far = sides.at[0], sides.at[1]
-    depth, tall = own.shape[1], rows.shape[2] // 4
-    wide = own.shape[0] // (3 * tall)
-    reach = low.shape[0] // (3 * tall)
-    ends[0] = low[...].astype(f32)
-    ends[1] = high[...].astype(f32)
-    columns = [(ends.at[0], x, reach) for x in range(reach)]
-    for piece in (near, own, far):
-        columns += [(piece, x, wide) for x in range(wide)]
-    columns += [(ends.at[1], x, reach) for x in range(reach)]
-    need = rows.shape[1]
-    edge = need - 2
-    for side, part in enumerate((columns[:need], columns[-need:])):
-        for at, (piece, x, extent) in enumerate(part):
-            lay_rows(rows.at[side], at, piece, x, extent, tall)
-        for at in range(edge):
-            for half, block in enumerate(features(rows.at[side], at, depth)):
-                edges[side, at, half] = block
-    inside = turned.shape[0]
-    held = [edges.at[0, k] for k in range(edge)] + [turned.at[k] for k in range(inside)]
-    held += [edges.at[1, k] for k in range(edge)]
-    pairs = h1.shape[1]
+    lax.fori_loop(0, inside // 2 - 1, step, 0, unroll=True)
+
+
+def outer_kernel(edge, odd, piece, sides, w1, bias, _, __, turned, h1, rows):
+    depth, tall = piece.shape[1], rows.shape[1] // 4
+    reach = piece.shape[0] // (3 * tall)
+    wide = sides.shape[1] // (3 * tall)
+    right = odd[0]
+    for x in range(reach):
+        lay_rows(rows, right * 2 + x, piece, x, reach, tall)
+    near = sides.at[right]
+    for x in range(2):
+        for c in range(3):
+            head = (c * wide + x) * tall
+            tail = (c * wide + wide - 2 + x) * tall
+            value = jnp.where(right == 1, near[tail : tail + tall, :], near[head : head + tall, :])
+            rows[(1 - right) * reach + x, pl.ds(c, tall, stride=4), :] = value
+        rows[(1 - right) * reach + x, pl.ds(3, tall, stride=4), :] = jnp.zeros((tall, depth), f32)
+    base = right * (turned.shape[0] - edge)
+    for at in range(edge):
+        for half, block in enumerate(features(rows, at, depth)):
+            turned[base + at, half] = block
+    start = right * (turned.shape[0] - 2 - edge)
     for k in range(edge // 2):
-        for xp in (k, pairs - 1 - k):
-            left = jnp.concatenate([merge(held[2 * xp + a][...]) for a in range(4)], axis=1)
-            layer(left, w1, bias[...], store_hidden(h1, xp), depth, every)
-    low_x, span_x, low_y, span_y = box
-    total = None
-    for piece, x, extent in columns[low_x : low_x + span_x]:
-        for c in range(3):
-            start = (c * extent + x) * tall + low_y
-            part = piece[start : start + span_y, :]
-            total = part * part if total is None else total + part * part
-    energy[...] = jnp.broadcast_to(0.5 * jnp.sum(total, keepdims=True), energy.shape)
-
-
-def second_kernel(h1, w2, bias, h2):
+        left = jnp.concatenate([merge(turned[start + 2 * k + a]) for a in range(4)], axis=1)
+        xp = right * (h1.shape[1] - edge // 2) + k
+        layer(left, w1, bias[...], store_hidden(h1, xp), depth, every)
+
+
+def second_kernel(odd, h1, w2, bias, h2, gift):
     depth = h1.shape[4]
 
     def step(xp, carry):
-        layer(gather_hidden(h1, xp, every), w2, jnp.concatenate([bias[...]] * 4, axis=1), store_hidden(h2, xp), depth, every)
+        store = store_hidden(h2, xp + odd[0])
+        layer(gather_hidden(h1, xp, every), w2, jnp.concatenate([bias[...]] * 4, axis=1), store, depth, every)
         return carry
 
-    lax.fori_loop(0, h2.shape[1], step, 0, unroll=True)
-
-
-def third_kernel(h2, w3, bias, h3):
+    lax.fori_loop(0, h2.shape[1] - 1, step, 0, unroll=True)
+    gift[...] = h2[:, h2.shape[1] // 2]
+
+
+def alone_kernel(odd, h2, w3, bias, h3):
     depth = h2.shape[4]
 
-    def step(xp, carry):
-        layer(gather_hidden(h2, xp, every), w3, jnp.concatenate([bias[...]] * 4, axis=1), store_hidden(h3, xp), depth, (1,))
+    def step(k, carry):
+        xp = k + odd[0]
+        store = store_hidden(h3, xp)
+        layer(gather_hidden(h2, xp, every), w3, jnp.concatenate([bias[...]] * 4, axis=1), store, depth, (1,))
         return carry
 
-    lax.fori_loop(0, h3.shape[0], step, 0, unroll=True)
+    lax.fori_loop(0, h3.shape[0] - 1, step, 0, unroll=True)
+
+
+def shared_kernel(odd, gift, w3, bias, _, __, h2, h3):
+    depth = h2.shape[4]
+    h2[:, (1 - odd[0]) * (h2.shape[1] - 1)] = gift[...]
+    xp = (1 - odd[0]) * (h3.shape[0] - 1)
+    store = store_hidden(h3, xp)
+    layer(gather_hidden(h2, xp, every), w3, jnp.concatenate([bias[...]] * 4, axis=1), store, depth, (1,))
 
 
 def final_kernel(cells, h3, w4, own, sides, energy, updated_ref, stress_ref, tau):
@@ -460,18 +477,16 @@
             updated_ref[i, x] = center[i] + time_step * tendency
 
 
-def box_total(box, size_x, size_y):
+def box_rounds(size_x, size_y):
     count_x, count_y = lax.axis_size(axis_x), lax.axis_size(axis_y)
-    left_x, left_y = count_x // size_x, count_y // size_y
-    if (left_x & (left_x - 1)) or (left_y & (left_y - 1)):
-        return lax.psum(box, axis_x + (axis_y,)) / (size_x * size_y)
+    rounds = []
     while size_x < count_x:
-        box = box + shifted(box, axis_x, size_x)
+        rounds.append((axis_x, size_x))
         size_x *= 2
     while size_y < count_y:
-        box = box + shifted(box, axis_y, size_y)
+        rounds.append((axis_y, size_y))
         size_y *= 2
-    return box
+    return rounds
 
 
 def local(v, w1, b1, w2, b2, w3, b3, w4):
@@ -479,85 +494,110 @@
     count_x, count_y = lax.axis_size(axis_x), lax.axis_size(axis_y)
     width = 2 * w2.shape[3]
     bias2, bias3 = b2.reshape(1, -1), b3.reshape(1, -1)
+    odd = (lax.axis_index(axis_x) % 2).reshape(1)
     head, tail = ends(v, halo)
     left, right = shifted(tail, axis_y, 1), shifted(head, axis_y, -1)
     e1, bias1 = prepare_first(w1, b1)
     left, right, e1, bias1 = lax.optimization_barrier((left, right, e1, bias1))
     edge = halo - own_x
-    strip, low, high = strips(v, left, right, edge)
+    strip, piece = strips(odd, v, left, right, edge)
     w2, w3, w4, strip = lax.optimization_barrier((w2, w3, w4, strip))
     e2, e3, e4 = prepare_later(w2, w3, w4)
     apart, twin = swapped(strip, axis_x, 1), swapped(strip, axis_x, 0)
-    odd = (lax.axis_index(axis_x) % 2).reshape(1)
-    low, high = shifted(low, axis_x, 2), shifted(high, axis_x, -2)
-
-    wide_x, wide_y = own_x + 2 * halo, own_y + 2 * halo
-    qx, qy = (wide_x - 4) // 2, (wide_y - 4) // 2
-    inside = wide_x - 2 - 2 * edge
-    h1_shape = jax.ShapeDtypeStruct((3, qx, 2, qy, depth, width), bf16)
-    h2_shape = jax.ShapeDtypeStruct((3, qx - 1, 2, qy - 1, depth, width), bf16)
-
+    piece = crossed(piece, axis_x)
+
+    wide_y = own_y + 2 * halo
+    span = 3 * own_x + edge
+    q1, qy = (span - 4) // 2, (wide_y - 4) // 2
+    h1_shape = jax.ShapeDtypeStruct((3, q1, 2, qy, depth, width), bf16)
+    h2_shape = jax.ShapeDtypeStruct((3, q1, 2, qy - 1, depth, width), bf16)
+    h3_shape = jax.ShapeDtypeStruct((q1 - 1, 2, qy - 2, depth, width), bf16)
+    turned_shape = jax.ShapeDtypeStruct((span - 2, qy, depth, 128), bf16)
     tile = 2 * depth * 256 * 256
+
+    size_y = blocks_in(own_y, count_y)
+    box = (own_x, wide_y, (wide_y - size_y * own_y) // 2, size_y * own_y)
+    energy = pl.pallas_call(
+        functools.partial(energy_kernel, box),
+        out_shape=jax.ShapeDtypeStruct((1, 1, 1, depth), f32),
+        in_specs=[whole()] * 2,
+        out_specs=whole(),
+        compiler_params=granted(4),
+        name="energy",
+    )(strip, twin)
+
+    rounds = box_rounds(2, size_y)
+    plain = (count_x & (count_x - 1)) == 0 and (count_y & (count_y - 1)) == 0
+    if plain:
+        early = max(len(rounds) - 2, 0)
+        for axis, step in rounds[:early]:
+            energy = energy + shifted(energy, axis, step)
+        e2, energy = lax.optimization_barrier((e2, energy))
+        for axis, step in rounds[early : early + 1]:
+            energy = energy + shifted(energy, axis, step)
+    else:
+        energy = lax.psum(energy, axis_x + (axis_y,)) / (2 * size_y)
+
     h1, turned, sides = pl.pallas_call(
-        functools.partial(inner_kernel, edge // 2),
-        out_shape=(
-            h1_shape,
-            jax.ShapeDtypeStruct((inside, qy, depth, 128), bf16),
-            jax.ShapeDtypeStruct((2,) + strip.shape, f32),
-        ),
-        in_specs=[pl.BlockSpec(memory_space=pltpu.SMEM)] + [whole()] * 5,
+        functools.partial(inner_kernel, edge),
+        out_shape=(h1_shape, turned_shape, jax.ShapeDtypeStruct((2,) + strip.shape, f32)),
+        in_specs=[scalar()] + [whole()] * 5,
         out_specs=(whole(),) * 3,
-        scratch_shapes=[pltpu.VMEM((inside + 2, 4 * wide_y, depth), f32)],
-        cost_estimate=priced(4 * tile * qx * qy),
+        scratch_shapes=[pltpu.VMEM((3 * own_x, 4 * wide_y, depth), f32)],
+        cost_estimate=priced(4 * tile * q1 * qy),
         compiler_params=granted(12),
         name="inner",
     )(odd, apart, strip, twin, e1, bias1)
 
-    size_x, size_y = blocks_in(own_x, count_x), blocks_in(own_y, count_y)
-    box = (
-        (wide_x - size_x * own_x) // 2,
-        size_x * own_x,
-        (wide_y - size_y * own_y) // 2,
-        size_y * own_y,
-    )
-    h1, energy = pl.pallas_call(
-        functools.partial(outer_kernel, box),
-        out_shape=(h1_shape, jax.ShapeDtypeStruct((1, 1, 1, depth), f32)),
-        in_specs=[whole()] * 8,
+    turned, h1 = pl.pallas_call(
+        functools.partial(outer_kernel, edge),
+        out_shape=(turned_shape, h1_shape),
+        in_specs=[scalar()] + [whole()] * 6,
         out_specs=(whole(), whole()),
-        scratch_shapes=[
-            pltpu.VMEM((2, edge + 2, 4 * wide_y, depth), f32),
-            pltpu.VMEM((2, edge, qy, depth, 128), bf16),
-            pltpu.VMEM((2,) + low.shape, f32),
-        ],
-        input_output_aliases={7: 0},
-        cost_estimate=priced(2 * tile * qx * qy),
+        scratch_shapes=[pltpu.VMEM((edge + 2, 4 * wide_y, depth), f32)],
+        input_output_aliases={5: 0, 6: 1},
+        cost_estimate=priced(2 * tile * q1 * qy),
         compiler_params=granted(12),
         name="outer",
-    )(low, strip, sides, high, turned, e1, bias1, h1)
-
-    h2 = pl.pallas_call(
+    )(odd, piece, sides, e1, bias1, turned, h1)
+
+    h2, gift = pl.pallas_call(
         second_kernel,
-        out_shape=h2_shape,
-        in_specs=[whole()] * 3,
-        out_specs=whole(),
-        cost_estimate=priced(12 * tile * (qx - 1) * (qy - 1)),
+        out_shape=(h2_shape, jax.ShapeDtypeStruct(h2_shape.shape[:1] + h2_shape.shape[2:], bf16)),
+        in_specs=[scalar()] + [whole()] * 3,
+        out_specs=(whole(), whole()),
+        cost_estimate=priced(12 * tile * (q1 - 1) * (qy - 1)),
         compiler_params=granted(20),
         name="second",
-    )(h1, e2, bias2)
-
-    energy = box_total(energy, size_x, size_y)
-    cells = own_x * own_y * depth * count_x * count_y
+    )(odd, h1, e2, bias2)
+    gift, energy = lax.optimization_barrier((gift, energy))
+    if plain:
+        for axis, step in rounds[early + 1 :]:
+            energy = energy + shifted(energy, axis, step)
+    gift = swapped(gift, axis_x, 0)
 
     h3 = pl.pallas_call(
-        third_kernel,
-        out_shape=jax.ShapeDtypeStruct((qx - 2, 2, qy - 2, depth, width), bf16),
-        in_specs=[whole()] * 3,
+        alone_kernel,
+        out_shape=h3_shape,
+        in_specs=[scalar()] + [whole()] * 3,
         out_specs=whole(),
-        cost_estimate=priced(12 * tile * (qx - 2) * (qy - 2)),
+        cost_estimate=priced(12 * tile * (q1 - 2) * (qy - 2)),
         compiler_params=granted(20),
         name="third",
-    )(h2, e3, bias3)
+    )(odd, h2, e3, bias3)
+
+    h2, h3 = pl.pallas_call(
+        shared_kernel,
+        out_shape=(h2_shape, h3_shape),
+        in_specs=[scalar()] + [whole()] * 5,
+        out_specs=(whole(), whole()),
+        input_output_aliases={4: 0, 5: 1},
+        cost_estimate=priced(12 * tile * (qy - 2)),
+        compiler_params=granted(12),
+        name="shared",
+    )(odd, gift, e3, bias3, h2, h3)
+
+    cells = own_x * own_y * depth * count_x * count_y
 
     return pl.pallas_call(
         functools.partial(final_kernel, cells),
@@ -567,9 +607,9 @@
         ),
         in_specs=[whole()] * 5,
         out_specs=(whole(), whole()),
-        scratch_shapes=[pltpu.VMEM((2 * (qx - 3), 8 * 2 * (qy - 3), depth), f32)],
-        cost_estimate=priced(8 * tile * (qx - 3) * (qy - 3)),
-        compiler_params=granted(20),
+        scratch_shapes=[pltpu.VMEM((2 * (q1 - 2), 8 * 2 * (qy - 3), depth), f32)],
+        cost_estimate=priced(8 * tile * (q1 - 2) * (qy - 3)),
+        compiler_params=granted(10),
         name="final",
     )(h3, e4, strip, sides, energy)
 

time: 38.7 us -> 37.7 us (0.974)
  Pallas kernels: 20.9 us -> 19.1 us
  starting transfers between devices: 13.1 us -> 14.5 us
  waiting for transfers between devices: 1.26 us -> 0.55 us
    pallas_call x5 -> x7, Pallas kernels: 18.2 us -> 16.4 us  [the longest x1 6.44 us: local(): pl.pallas_call(second_kernel, out_shape=(h2_shape, jax.ShapeDtypeStruct(h...]
    ppermute x2 -> x3, starting transfers between devices: 1.83 us -> 2.85 us  [swapped(): return lax.ppermute(cells, axis, order)]
    ppermute x2 -> x3, waiting for transfers between devices: 0.87 us -> 0.17 us  [swapped(): return lax.ppermute(cells, axis, order)]
    ppermute x6 -> x5, starting transfers between devices: 11.2 us -> 11.7 us  [shifted(): lax.ppermute(cells, axis, [(i, (i + step) % count) for i in range(count)])]
  transfers between devices with their start and end apart: 8 -> 9, of which waited for: 3 -> 3; matrix products, arithmetic and copies ran while one was open for 0% -> 0% of each run, Pallas kernels for 45% -> 42%
where the time goes in v4:
time: 37.7 us; the launch traced here: 37.5 us
  Pallas kernels  19.1 us (51%)
  starting transfers between devices  14.5 us (38%)
  local copies, waits for them, and re-layouts  2.44 us (6%)
  between operations  0.83 us (2%)
  waiting for transfers between devices  0.55 us (1%)
    ppermute x5, starting transfers between devices, shifted(): lax.ppermute(cells, axis, [(i, (i + step) % count) for i in range(count)])  11.7 us
    pallas_call x1, Pallas kernels, local(): pl.pallas_call(second_kernel, out_shape=(h2_shape, jax.ShapeDtypeStruct(h...  6.44 us
    pallas_call x1, Pallas kernels, local(): pl.pallas_call(alone_kernel, out_shape=h3_shape, in_specs=[scalar()] + [w...  3.84 us
    pallas_call x1, Pallas kernels, local(): pl.pallas_call(functools.partial(inner_kernel, edge), out_shape=(h1_shape...  3.62 us
    ppermute x3, starting transfers between devices, swapped(): return lax.ppermute(cells, axis, order)  2.85 us
    unnamed x18, local copies, waits for them, and re-layouts  2.44 us
    pallas_call x1, Pallas kernels, local(): pl.pallas_call(functools.partial(final_kernel, cells), out_shape=(jax.Sha...  1.7 us
    pallas_call x1, Pallas kernels, local(): pl.pallas_call(shared_kernel, out_shape=(h2_shape, h3_shape), in_specs=[s...  1.47 us
  transfers between devices with their start and end apart: 9, of which 3 were waited for; matrix products, arithmetic and copies ran while one was open for 0% of the time, Pallas kernels for 42%

profile of v4, /device:TPU:0, one launch (start us, length us, event | category | flops | bytes accessed | tf_op | source)
XLA Modules:
  0.0 37.5 jit_solution(4530526976246302426)
XLA Ops:
  0.6 0.0 copy-start
  0.6 0.8 %copy-done = f32[3,4,8,128]{3,2,1,0:T(8,128)S(1)} copy-done((f32[3,4,8,128]{3,2,1,0:T(8,128)S(1)}, f32[3,4,8,128]{3,2,1,0:T(8,128)}, u32[]{:S(2)}) %copy-start) | copy-done | bytes 49176
  1.4 3.1 %collective-permute-start = (f32[72,128]{1,0:T(8,128)S(1)}, f32[72,128]{1,0:T(8,128)S(1)}, u32[]{:S(2)}, u32[]{:S(2)}) collective-permute-start(f32[72,128]{1,0:T(8,128)S(1)} %get-tuple-element.30), channel_id=1, source_target_pairs={{0,1},{1,2},{2,3},{3,0},{4,5},{5,6},{6,7},{7,4},{8,9},{9,10},{10,1... | collective-permute-start | bytes 110600 | tf_op jit(solution)/shard_map/ppermute | solution.py:24
  4.5 2.1 %collective-permute-start.1 = (f32[72,128]{1,0:T(8,128)S(1)}, f32[72,128]{1,0:T(8,128)S(1)}, u32[]{:S(2)}, u32[]{:S(2)}) collective-permute-start(f32[72,128]{1,0:T(8,128)S(1)} %get-tuple-element.31), channel_id=1, source_target_pairs={{0,3},{1,0},{2,1},{3,2},{4,7},{5,4},{6,5},{7,6},{8,11},{9,8},{10,9... | collective-permute-start | bytes 110600 | tf_op jit(solution)/shard_map/ppermute | solution.py:24
  6.6 0.0 copy-start.5
  6.6 0.9 %copy-done.5 = bf16[3,3,3,64,9]{3,2,4,1,0:T(4,128)(2,1)S(1)} copy-done((bf16[3,3,3,64,9]{3,2,4,1,0:T(4,128)(2,1)S(1)}, bf16[3,3,3,64,9]{3,2,4,1,0:T(4,128)(2,1)}, u32[]{:S(2)}) %copy-start.5) | copy-done | bytes 31128
  7.5 0.0 copy-start.7
  7.5 0.7 %copy-done.7 = f32[64]{0:T(128)S(1)} copy-done((f32[64]{0:T(128)S(1)}, f32[64]{0:T(128)}, u32[]{:S(2)}) %copy-start.7) | copy-done | bytes 280
  8.2 0.0 copy-start.1
  8.2 0.0 copy-start.3
  8.2 0.0 copy-start.4
  8.2 0.0 copy-start.6
  8.2 0.3 prepare_first.1
  8.5 0.1 collective-permute-done.left
  8.6 0.3 collective-permute-done.1.right
  8.9 0.1 copy-done.1
  9.0 0.1 collective-permute-start.4
  9.1 2.7 %collective-permute-start.3 = (f32[240,128]{1,0:T(8,128)S(1)}, f32[240,128]{1,0:T(8,128)S(1)}, u32[]{:S(2)}, u32[]{:S(2)}) collective-permute-start(f32[240,128]{1,0:T(8,128)S(1)} %get-tuple-element.38.own), channel_id=1, source_target_pairs={{0,28},{4,8},{8,4},{12,16},{16,12},{20,24},{24,20},{28,0},{1,29},{... | collective-permute-start | bytes 368648 | tf_op jit(solution)/shard_map/ppermute | solution.py:30
  11.8 0.0 collective-permute-start.2
  11.8 0.0 copy-done.3
  11.8 0.0 copy-done.4
  11.8 0.0 copy-done.6
  11.8 0.7 %prepare_later.1 = (bf16[3072,256]{1,0:T(8,128)(2,1)S(1)}, bf16[3072,256]{1,0:T(8,128)(2,1)S(1)}, bf16[144,256]{1,0:T(8,128)(2,1)S(1)}) custom-call(bf16[3,3,3,64,64]{4,3,2,1,0:T(8,128)(2,1)S(1)} %copy-done.3, bf16[3,3,3,64,64]{4,3,2,1,0:T(8,128)(2,1)S(1)} %copy-done.4, bf16[3,3,3,6,64]{4,3,2,1,0:T(8,128)(2,1)S(1)} %copy-done.6), custom_call_target="tpu_custom_call" | custom-call | flops 1000000000 | bytes 1000000 | tf_op jit(solution)/shard_map/prepare_later/pallas_call | solution.py:237
  12.5 0.0 collective-permute-done.4.twin
  12.5 0.1 energy.1
  12.7 2.0 %collective-permute-start.5 = (f32[1,1,1,128]{3,2,1,0:T(1,128)S(1)}, f32[1,1,1,128]{3,2,1,0:T(1,128)S(1)}, u32[]{:S(2)}, u32[]{:S(2)}) collective-permute-start(f32[1,1,1,128]{3,2,1,0:T(1,128)S(1)} %energy.1), channel_id=1, source_target_pairs={{0,8},{4,12},{8,16},{12,20},{16,24},{20,28},{24,0},{28,4},{1,9},{5... | collective-permute-start | bytes 1544 | tf_op jit(solution)/shard_map/ppermute | solution.py:24
  14.7 0.2 collective-permute-done.3.apart
  14.8 3.6 %inner.1 = (bf16[3,5,2,8,128,128]{5,4,3,2,1,0:T(8,128)(2,1)S(1)}, bf16[12,8,128,128]{3,2,1,0:T(8,128)(2,1)S(1)}, f32[2,240,128]{2,1,0:T(8,128)S(1)}) custom-call(s32[1]{0:T(128)} %bitcast.odd, f32[240,128]{1,0:T(8,128)S(1)} %collective-permute-done.3.apart, f32[240,128]{1,0:T(8,128)S(1)} %get-tuple-element.38.own, ...), custom_call_target="tpu_custom_call" | custom-call | flops 2684354560 | bytes 1000000 | tf_op jit(solution)/shard_map/inner/pallas_call | solution.py:541
  18.5 0.0 collective-permute-done.2.piece
  18.5 0.0 copy-start.8
  18.5 0.8 %outer.1 = (bf16[12,8,128,128]{3,2,1,0:T(8,128)(2,1)S(1)}, bf16[3,5,2,8,128,128]{5,4,3,2,1,0:T(8,128)(2,1)S(1)}) custom-call(s32[1]{0:T(128)} %bitcast.odd, f32[120,128]{1,0:T(8,128)S(1)} %collective-permute-done.2.piece, f32[2,240,128]{2,1,0:T(8,128)S(1)} %get-tuple-element.41.sides, ...), custom_call_target="tpu_custom_call", output_to_operand_aliasing={{0}: (5, {}), {1}: (6, {})} | custom-call | flops 1342177280 | bytes 1000000 | tf_op jit(solution)/shard_map/outer/pallas_call | solution.py:552
  19.3 0.0 collective-permute-done.5
  19.4 2.1 %collective-permute-start.6 = (f32[1,1,1,128]{3,2,1,0:T(1,128)S(1)}, f32[1,1,1,128]{3,2,1,0:T(1,128)S(1)}, u32[]{:S(2)}, u32[]{:S(2)}) collective-permute-start(f32[1,1,1,128]{3,2,1,0:T(1,128)S(1)} %add.18), channel_id=1, source_target_pairs={{0,16},{4,20},{8,24},{12,28},{16,0},{20,4},{24,8},{28,12},{1,17},{... | collective-permute-start | bytes 1544 | tf_op jit(solution)/shard_map/ppermute | solution.py:24
  21.5 0.0 copy-done.8
  21.5 0.0 copy-start.2
  21.5 6.4 %second.1 = (bf16[3,5,2,7,128,128]{5,4,3,2,1,0:T(8,128)(2,1)S(1)}, bf16[3,2,7,128,128]{4,3,2,1,0:T(8,128)(2,1)S(1)}) custom-call(s32[1]{0:T(128)} %bitcast.odd, bf16[3,5,2,8,128,128]{5,4,3,2,1,0:T(8,128)(2,1)S(1)} %get-tuple-element.44.h1, bf16[3072,256]{1,0:T(8,128)(2,1)S(1)} %get-tuple-element.49.w2, f32[1,64]{1,0:T(1,128)S(1)} %bitcast.9), custom_call_target="tpu_custom_call" | custom-call | flops 5637144576 | bytes 1000000 | tf_op jit(solution)/shard_map/second/pallas_call | solution.py:564
  27.9 0.0 collective-permute-done.6
  28.0 0.1 collective-permute-start.7
  28.0 2.3 %collective-permute-start.8 = (f32[1,1,1,128]{3,2,1,0:T(1,128)S(1)}, f32[1,1,1,128]{3,2,1,0:T(1,128)S(1)}, u32[]{:S(2)}, u32[]{:S(2)}) collective-permute-start(f32[1,1,1,128]{3,2,1,0:T(1,128)S(1)} %add.19), channel_id=1, source_target_pairs={{0,2},{1,3},{2,0},{3,1},{4,6},{5,7},{6,4},{7,5},{8,10},{9,11},{10,... | collective-permute-start | bytes 1544 | tf_op jit(solution)/shard_map/ppermute | solution.py:24
  30.4 0.0 copy-done.2
  30.4 3.8 %third.1.__ = bf16[4,2,6,128,128]{4,3,2,1,0:T(8,128)(2,1)S(1)} custom-call(s32[1]{0:T(128)} %bitcast.odd, bf16[3,5,2,7,128,128]{5,4,3,2,1,0:T(8,128)(2,1)S(1)} %get-tuple-element.54.h2._, bf16[3072,256]{1,0:T(8,128)(2,1)S(1)} %get-tuple-element.53.w3, f32[1,64]{1,0:T(1,128)S(1)} %bitcast.5), custom_call_target="tpu_custom_call" | custom-call | flops 3623878656 | bytes 1000000 | tf_op jit(solution)/shard_map/third/pallas_call | solution.py:579
  34.2 0.0 collective-permute-done.8
  34.3 0.0 collective-permute-done.7.gift
  34.3 1.5 %shared.1 = (bf16[3,5,2,7,128,128]{5,4,3,2,1,0:T(8,128)(2,1)S(1)}, bf16[4,2,6,128,128]{4,3,2,1,0:T(8,128)(2,1)S(1)}) custom-call(s32[1]{0:T(128)} %bitcast.odd, bf16[3,2,7,128,128]{4,3,2,1,0:T(8,128)(2,1)S(1)} %collective-permute-done.7.gift, bf16[3072,256]{1,0:T(8,128)(2,1)S(1)} %get-tuple-element.53.w3, ...), custom_call_target="tpu_custom_call", output_to_operand_aliasing={{0}: (4, {}), {1}: (5, {})} | custom-call | flops 1207959552 | bytes 1000000 | tf_op jit(solution)/shard_map/shared/pallas_call | solution.py:589
  35.8 1.7 %final.1 = (f32[3,4,8,128]{3,2,1,0:T(8,128)}, f32[6,4,8,128]{3,2,1,0:T(8,128)}) custom-call(bf16[4,2,6,128,128]{4,3,2,1,0:T(8,128)(2,1)S(1)} %get-tuple-element.55.h3, bf16[144,256]{1,0:T(8,128)(2,1)S(1)} %get-tuple-element.56.w4, f32[240,128]{1,0:T(8,128)S(1)} %get-tuple-element.38.own, f32[2,240,128]{2,1,0:T(8,128)S(1)} %get-tuple-element.41.sides, ...), custom_call_target="tpu_custom_call" | custom-call | flops 2013265920 | bytes 1000000 | tf_op jit(solution)/shard_map/final/pallas_call | solution.py:602
  (5 shorter events, 0.0 us)
Async XLA Ops:
  0.6 0.8 %copy-start = (f32[3,4,8,128]{3,2,1,0:T(8,128)S(1)}, f32[3,4,8,128]{3,2,1,0:T(8,128)}, u32[]{:S(2)}) copy-start(f32[3,4,8,128]{3,2,1,0:T(8,128)} %v.3) | copy-start | bytes 147460
  1.4 7.2 %collective-permute-start = (f32[72,128]{1,0:T(8,128)S(1)}, f32[72,128]{1,0:T(8,128)S(1)}, u32[]{:S(2)}, u32[]{:S(2)}) collective-permute-start(f32[72,128]{1,0:T(8,128)S(1)} %get-tuple-element.30), channel_id=1, source_target_pairs={{0,1},{1,2},{2,3},{3,0},{4,5},{5,6},{6,7},{7,4},{8,9},{9,10},{10,1... | collective-permute-start | bytes 110600 | tf_op jit(solution)/shard_map/ppermute | solution.py:24
  4.5 4.4 %collective-permute-start.1 = (f32[72,128]{1,0:T(8,128)S(1)}, f32[72,128]{1,0:T(8,128)S(1)}, u32[]{:S(2)}, u32[]{:S(2)}) collective-permute-start(f32[72,128]{1,0:T(8,128)S(1)} %get-tuple-element.31), channel_id=1, source_target_pairs={{0,3},{1,0},{2,1},{3,2},{4,7},{5,4},{6,5},{7,6},{8,11},{9,8},{10,9... | collective-permute-start | bytes 110600 | tf_op jit(solution)/shard_map/ppermute | solution.py:24
  6.6 0.9 %copy-start.5 = (bf16[3,3,3,64,9]{3,2,4,1,0:T(4,128)(2,1)S(1)}, bf16[3,3,3,64,9]{3,2,4,1,0:T(4,128)(2,1)}, u32[]{:S(2)}) copy-start(bf16[3,3,3,64,9]{3,2,4,1,0:T(4,128)(2,1)} %param.9) | copy-start | bytes 93316
  7.5 0.7 %copy-start.7 = (f32[64]{0:T(128)S(1)}, f32[64]{0:T(128)}, u32[]{:S(2)}) copy-start(f32[64]{0:T(128)} %param.10) | copy-start | bytes 772
  8.2 0.8 %copy-start.1 = (f32[3,4,8,128]{3,2,1,0:T(8,128)S(1)}, f32[3,4,8,128]{3,2,1,0:T(8,128)}, u32[]{:S(2)}) copy-start(f32[3,4,8,128]{3,2,1,0:T(8,128)} %v.3) | copy-start | bytes 147460
  8.2 3.6 %copy-start.3 = (bf16[3,3,3,64,64]{4,3,2,1,0:T(8,128)(2,1)S(1)}, bf16[3,3,3,64,64]{4,3,2,1,0:T(8,128)(2,1)}, u32[]{:S(2)}) copy-start(bf16[3,3,3,64,64]{4,3,2,1,0:T(8,128)(2,1)} %w2) | copy-start | bytes 663556
  8.2 3.6 %copy-start.4 = (bf16[3,3,3,64,64]{4,3,2,1,0:T(8,128)(2,1)S(1)}, bf16[3,3,3,64,64]{4,3,2,1,0:T(8,128)(2,1)}, u32[]{:S(2)}) copy-start(bf16[3,3,3,64,64]{4,3,2,1,0:T(8,128)(2,1)} %w3) | copy-start | bytes 663556
  8.2 3.6 %copy-start.6 = (bf16[3,3,3,6,64]{4,3,2,1,0:T(8,128)(2,1)S(1)}, bf16[3,3,3,6,64]{4,3,2,1,0:T(8,128)(2,1)}, u32[]{:S(2)}) copy-start(bf16[3,3,3,6,64]{4,3,2,1,0:T(8,128)(2,1)} %w4) | copy-start | bytes 62212
  9.0 3.5 %collective-permute-start.4 = (f32[240,128]{1,0:T(8,128)S(1)}, f32[240,128]{1,0:T(8,128)S(1)}, u32[]{:S(2)}, u32[]{:S(2)}) collective-permute-start(f32[240,128]{1,0:T(8,128)S(1)} %get-tuple-element.38.own), channel_id=1, source_target_pairs={{0,4},{4,0},{8,12},{12,8},{16,20},{20,16},{24,28},{28,24},{1,5},{5... | collective-permute-start | bytes 368648 | tf_op jit(solution)/shard_map/ppermute | solution.py:30
  9.1 5.8 %collective-permute-start.3 = (f32[240,128]{1,0:T(8,128)S(1)}, f32[240,128]{1,0:T(8,128)S(1)}, u32[]{:S(2)}, u32[]{:S(2)}) collective-permute-start(f32[240,128]{1,0:T(8,128)S(1)} %get-tuple-element.38.own), channel_id=1, source_target_pairs={{0,28},{4,8},{8,4},{12,16},{16,12},{20,24},{24,20},{28,0},{1,29},{... | collective-permute-start | bytes 368648 | tf_op jit(solution)/shard_map/ppermute | solution.py:30
  11.8 6.7 %collective-permute-start.2 = (f32[120,128]{1,0:T(8,128)S(1)}, f32[120,128]{1,0:T(8,128)S(1)}, u32[]{:S(2)}, u32[]{:S(2)}) collective-permute-start(f32[120,128]{1,0:T(8,128)S(1)} %get-tuple-element.36), channel_id=1, source_target_pairs={{0,8},{4,28},{8,16},{12,4},{16,24},{20,12},{24,0},{28,20},{1,9},{5... | collective-permute-start | bytes 184328 | tf_op jit(solution)/shard_map/ppermute | solution.py:35
  12.7 6.7 %collective-permute-start.5 = (f32[1,1,1,128]{3,2,1,0:T(1,128)S(1)}, f32[1,1,1,128]{3,2,1,0:T(1,128)S(1)}, u32[]{:S(2)}, u32[]{:S(2)}) collective-permute-start(f32[1,1,1,128]{3,2,1,0:T(1,128)S(1)} %energy.1), channel_id=1, source_target_pairs={{0,8},{4,12},{8,16},{12,20},{16,24},{20,28},{24,0},{28,4},{1,9},{5... | collective-permute-start | bytes 1544 | tf_op jit(solution)/shard_map/ppermute | solution.py:24
  18.5 3.0 %copy-start.8 = (f32[64]{0:T(128)S(1)}, f32[64]{0:T(128)}, u32[]{:S(2)}) copy-start(f32[64]{0:T(128)} %param.12) | copy-start | bytes 772
  19.4 8.6 %collective-permute-start.6 = (f32[1,1,1,128]{3,2,1,0:T(1,128)S(1)}, f32[1,1,1,128]{3,2,1,0:T(1,128)S(1)}, u32[]{:S(2)}, u32[]{:S(2)}) collective-permute-start(f32[1,1,1,128]{3,2,1,0:T(1,128)S(1)} %add.18), channel_id=1, source_target_pairs={{0,16},{4,20},{8,24},{12,28},{16,0},{20,4},{24,8},{28,12},{1,17},{... | collective-permute-start | bytes 1544 | tf_op jit(solution)/shard_map/ppermute | solution.py:24
  21.5 8.9 %copy-start.2 = (f32[64]{0:T(128)S(1)}, f32[64]{0:T(128)}, u32[]{:S(2)}) copy-start(f32[64]{0:T(128)} %param.14) | copy-start | bytes 772
  28.0 6.3 %collective-permute-start.7 = (bf16[3,2,7,128,128]{4,3,2,1,0:T(8,128)(2,1)S(1)}, bf16[3,2,7,128,128]{4,3,2,1,0:T(8,128)(2,1)S(1)}, u32[]{:S(2)}, u32[]{:S(2)}) collective-permute-start(bf16[3,2,7,128,128]{4,3,2,1,0:T(8,128)(2,1)S(1)} %get-tuple-element.52), channel_id=1, source_target_pairs={{0,4},{4,0},{8,12},{12,8},{16,20},{20,16},{24,28},{28,24},{1,5},{5... | collective-permute-start | bytes 4128776 | tf_op jit(solution)/shard_map/ppermute | solution.py:30
  28.0 6.2 %collective-permute-start.8 = (f32[1,1,1,128]{3,2,1,0:T(1,128)S(1)}, f32[1,1,1,128]{3,2,1,0:T(1,128)S(1)}, u32[]{:S(2)}, u32[]{:S(2)}) collective-permute-start(f32[1,1,1,128]{3,2,1,0:T(1,128)S(1)} %add.19), channel_id=1, source_target_pairs={{0,2},{1,3},{2,0},{3,1},{4,6},{5,7},{6,4},{7,5},{8,10},{9,11},{10,... | collective-permute-start | bytes 1544 | tf_op jit(solution)/shard_map/ppermute | solution.py:24

commit v5 on v4

--- a/solution.py
+++ b/solution.py
@@ -480,12 +480,12 @@
 def box_rounds(size_x, size_y):
     count_x, count_y = lax.axis_size(axis_x), lax.axis_size(axis_y)
     rounds = []
+    while size_y < count_y:
+        rounds.append((axis_y, size_y))
+        size_y *= 2
     while size_x < count_x:
         rounds.append((axis_x, size_x))
         size_x *= 2
-    while size_y < count_y:
-        rounds.append((axis_y, size_y))
-        size_y *= 2
     return rounds
 
 

time: 37.7 us -> 36.9 us (0.979)
  starting transfers between devices: 14.5 us -> 13.7 us
    ppermute x5, starting transfers between devices: 11.7 us -> 10.1 us  [shifted(): lax.ppermute(cells, axis, [(i, (i + step) % count) for i in range(count)])]
    ppermute x3, starting transfers between devices: 2.85 us -> 3.65 us  [swapped(): return lax.ppermute(cells, axis, order)]
  transfers between devices with their start and end apart: 9 -> 9, of which waited for: 3 -> 3; matrix products, arithmetic and copies ran while one was open for 0% -> 0% of each run, Pallas kernels for 42% -> 43%
where the time goes in v5:
time: 36.9 us; the launch traced here: 36.6 us
  Pallas kernels  19.1 us (52%)
  starting transfers between devices  13.7 us (37%)
  local copies, waits for them, and re-layouts  2.44 us (7%)
  between operations  0.83 us (2%)
  waiting for transfers between devices  0.54 us (1%)
    ppermute x5, starting transfers between devices, shifted(): lax.ppermute(cells, axis, [(i, (i + step) % count) for i in range(count)])  10.1 us
    pallas_call x1, Pallas kernels, local(): pl.pallas_call(second_kernel, out_shape=(h2_shape, jax.ShapeDtypeStruct(h...  6.44 us
    pallas_call x1, Pallas kernels, local(): pl.pallas_call(alone_kernel, out_shape=h3_shape, in_specs=[scalar()] + [w...  3.84 us
    ppermute x3, starting transfers between devices, swapped(): return lax.ppermute(cells, axis, order)  3.65 us
    pallas_call x1, Pallas kernels, local(): pl.pallas_call(functools.partial(inner_kernel, edge), out_shape=(h1_shape...  3.61 us
    unnamed x18, local copies, waits for them, and re-layouts  2.44 us
    pallas_call x1, Pallas kernels, local(): pl.pallas_call(functools.partial(final_kernel, cells), out_shape=(jax.Sha...  1.71 us
    pallas_call x1, Pallas kernels, local(): pl.pallas_call(shared_kernel, out_shape=(h2_shape, h3_shape), in_specs=[s...  1.48 us
  transfers between devices with their start and end apart: 9, of which 3 were waited for; matrix products, arithmetic and copies ran while one was open for 0% of the time, Pallas kernels for 43%

profile of v5, /device:TPU:0, one launch (start us, length us, event | category | flops | bytes accessed | tf_op | source)
XLA Modules:
  0.0 36.6 jit_solution(4027116096956249103)
XLA Ops:
  0.6 0.0 copy-start
  0.6 0.8 %copy-done = f32[3,4,8,128]{3,2,1,0:T(8,128)S(1)} copy-done((f32[3,4,8,128]{3,2,1,0:T(8,128)S(1)}, f32[3,4,8,128]{3,2,1,0:T(8,128)}, u32[]{:S(2)}) %copy-start) | copy-done | bytes 49176
  1.4 3.1 %collective-permute-start = (f32[72,128]{1,0:T(8,128)S(1)}, f32[72,128]{1,0:T(8,128)S(1)}, u32[]{:S(2)}, u32[]{:S(2)}) collective-permute-start(f32[72,128]{1,0:T(8,128)S(1)} %get-tuple-element.30), channel_id=1, source_target_pairs={{0,1},{1,2},{2,3},{3,0},{4,5},{5,6},{6,7},{7,4},{8,9},{9,10},{10,1... | collective-permute-start | bytes 110600 | tf_op jit(solution)/shard_map/ppermute | solution.py:24
  4.5 2.1 %collective-permute-start.1 = (f32[72,128]{1,0:T(8,128)S(1)}, f32[72,128]{1,0:T(8,128)S(1)}, u32[]{:S(2)}, u32[]{:S(2)}) collective-permute-start(f32[72,128]{1,0:T(8,128)S(1)} %get-tuple-element.31), channel_id=1, source_target_pairs={{0,3},{1,0},{2,1},{3,2},{4,7},{5,4},{6,5},{7,6},{8,11},{9,8},{10,9... | collective-permute-start | bytes 110600 | tf_op jit(solution)/shard_map/ppermute | solution.py:24
  6.6 0.0 copy-start.5
  6.6 0.9 %copy-done.5 = bf16[3,3,3,64,9]{3,2,4,1,0:T(4,128)(2,1)S(1)} copy-done((bf16[3,3,3,64,9]{3,2,4,1,0:T(4,128)(2,1)S(1)}, bf16[3,3,3,64,9]{3,2,4,1,0:T(4,128)(2,1)}, u32[]{:S(2)}) %copy-start.5) | copy-done | bytes 31128
  7.5 0.0 copy-start.7
  7.5 0.7 %copy-done.7 = f32[64]{0:T(128)S(1)} copy-done((f32[64]{0:T(128)S(1)}, f32[64]{0:T(128)}, u32[]{:S(2)}) %copy-start.7) | copy-done | bytes 280
  8.2 0.0 copy-start.1
  8.2 0.0 copy-start.3
  8.2 0.0 copy-start.4
  8.2 0.0 copy-start.6
  8.2 0.3 prepare_first.1
  8.5 0.1 collective-permute-done.left
  8.6 0.3 collective-permute-done.1.right
  8.9 0.1 copy-done.1
  9.0 0.1 collective-permute-start.4
  9.1 2.7 %collective-permute-start.3 = (f32[240,128]{1,0:T(8,128)S(1)}, f32[240,128]{1,0:T(8,128)S(1)}, u32[]{:S(2)}, u32[]{:S(2)}) collective-permute-start(f32[240,128]{1,0:T(8,128)S(1)} %get-tuple-element.38.own), channel_id=1, source_target_pairs={{0,28},{4,8},{8,4},{12,16},{16,12},{20,24},{24,20},{28,0},{1,29},{... | collective-permute-start | bytes 368648 | tf_op jit(solution)/shard_map/ppermute | solution.py:30
  11.8 0.0 collective-permute-start.2
  11.8 0.0 copy-done.3
  11.8 0.0 copy-done.4
  11.8 0.0 copy-done.6
  11.8 0.7 %prepare_later.1 = (bf16[3072,256]{1,0:T(8,128)(2,1)S(1)}, bf16[3072,256]{1,0:T(8,128)(2,1)S(1)}, bf16[144,256]{1,0:T(8,128)(2,1)S(1)}) custom-call(bf16[3,3,3,64,64]{4,3,2,1,0:T(8,128)(2,1)S(1)} %copy-done.3, bf16[3,3,3,64,64]{4,3,2,1,0:T(8,128)(2,1)S(1)} %copy-done.4, bf16[3,3,3,6,64]{4,3,2,1,0:T(8,128)(2,1)S(1)} %copy-done.6), custom_call_target="tpu_custom_call" | custom-call | flops 1000000000 | bytes 1000000 | tf_op jit(solution)/shard_map/prepare_later/pallas_call | solution.py:237
  12.5 0.0 collective-permute-done.4.twin
  12.5 0.1 energy.1
  12.7 2.0 %collective-permute-start.5 = (f32[1,1,1,128]{3,2,1,0:T(1,128)S(1)}, f32[1,1,1,128]{3,2,1,0:T(1,128)S(1)}, u32[]{:S(2)}, u32[]{:S(2)}) collective-permute-start(f32[1,1,1,128]{3,2,1,0:T(1,128)S(1)} %energy.1), channel_id=1, source_target_pairs={{0,2},{1,3},{2,0},{3,1},{4,6},{5,7},{6,4},{7,5},{8,10},{9,11},{10,... | collective-permute-start | bytes 1544 | tf_op jit(solution)/shard_map/ppermute | solution.py:24
  14.7 0.1 collective-permute-done.3.apart
  14.8 3.6 %inner.1 = (bf16[3,5,2,8,128,128]{5,4,3,2,1,0:T(8,128)(2,1)S(1)}, bf16[12,8,128,128]{3,2,1,0:T(8,128)(2,1)S(1)}, f32[2,240,128]{2,1,0:T(8,128)S(1)}) custom-call(s32[1]{0:T(128)} %bitcast.odd, f32[240,128]{1,0:T(8,128)S(1)} %collective-permute-done.3.apart, f32[240,128]{1,0:T(8,128)S(1)} %get-tuple-element.38.own, ...), custom_call_target="tpu_custom_call" | custom-call | flops 2684354560 | bytes 1000000 | tf_op jit(solution)/shard_map/inner/pallas_call | solution.py:541
  18.5 0.0 collective-permute-done.2.piece
  18.5 0.0 copy-start.8
  18.5 0.8 %outer.1 = (bf16[12,8,128,128]{3,2,1,0:T(8,128)(2,1)S(1)}, bf16[3,5,2,8,128,128]{5,4,3,2,1,0:T(8,128)(2,1)S(1)}) custom-call(s32[1]{0:T(128)} %bitcast.odd, f32[120,128]{1,0:T(8,128)S(1)} %collective-permute-done.2.piece, f32[2,240,128]{2,1,0:T(8,128)S(1)} %get-tuple-element.41.sides, ...), custom_call_target="tpu_custom_call", output_to_operand_aliasing={{0}: (5, {}), {1}: (6, {})} | custom-call | flops 1342177280 | bytes 1000000 | tf_op jit(solution)/shard_map/outer/pallas_call | solution.py:552
  19.3 0.0 collective-permute-done.5
  19.3 2.1 %collective-permute-start.6 = (f32[1,1,1,128]{3,2,1,0:T(1,128)S(1)}, f32[1,1,1,128]{3,2,1,0:T(1,128)S(1)}, u32[]{:S(2)}, u32[]{:S(2)}) collective-permute-start(f32[1,1,1,128]{3,2,1,0:T(1,128)S(1)} %add.18), channel_id=1, source_target_pairs={{0,8},{4,12},{8,16},{12,20},{16,24},{20,28},{24,0},{28,4},{1,9},{5... | collective-permute-start | bytes 1544 | tf_op jit(solution)/shard_map/ppermute | solution.py:24
  21.4 0.0 copy-done.8
  21.4 0.0 copy-start.2
  21.4 6.4 %second.1 = (bf16[3,5,2,7,128,128]{5,4,3,2,1,0:T(8,128)(2,1)S(1)}, bf16[3,2,7,128,128]{4,3,2,1,0:T(8,128)(2,1)S(1)}) custom-call(s32[1]{0:T(128)} %bitcast.odd, bf16[3,5,2,8,128,128]{5,4,3,2,1,0:T(8,128)(2,1)S(1)} %get-tuple-element.44.h1, bf16[3072,256]{1,0:T(8,128)(2,1)S(1)} %get-tuple-element.49.w2, f32[1,64]{1,0:T(1,128)S(1)} %bitcast.9), custom_call_target="tpu_custom_call" | custom-call | flops 5637144576 | bytes 1000000 | tf_op jit(solution)/shard_map/second/pallas_call | solution.py:564
  27.9 0.0 collective-permute-done.6
  27.9 0.9 %collective-permute-start.7 = (bf16[3,2,7,128,128]{4,3,2,1,0:T(8,128)(2,1)S(1)}, bf16[3,2,7,128,128]{4,3,2,1,0:T(8,128)(2,1)S(1)}, u32[]{:S(2)}, u32[]{:S(2)}) collective-permute-start(bf16[3,2,7,128,128]{4,3,2,1,0:T(8,128)(2,1)S(1)} %get-tuple-element.52), channel_id=1, source_target_pairs={{0,4},{4,0},{8,12},{12,8},{16,20},{20,16},{24,28},{28,24},{1,5},{5... | collective-permute-start | bytes 4128776 | tf_op jit(solution)/shard_map/ppermute | solution.py:30
  28.8 0.8 %collective-permute-start.8 = (f32[1,1,1,128]{3,2,1,0:T(1,128)S(1)}, f32[1,1,1,128]{3,2,1,0:T(1,128)S(1)}, u32[]{:S(2)}, u32[]{:S(2)}) collective-permute-start(f32[1,1,1,128]{3,2,1,0:T(1,128)S(1)} %add.19), channel_id=1, source_target_pairs={{0,16},{4,20},{8,24},{12,28},{16,0},{20,4},{24,8},{28,12},{1,17},{... | collective-permute-start | bytes 1544 | tf_op jit(solution)/shard_map/ppermute | solution.py:24
  29.5 0.0 copy-done.2
  29.5 3.8 %third.1.__ = bf16[4,2,6,128,128]{4,3,2,1,0:T(8,128)(2,1)S(1)} custom-call(s32[1]{0:T(128)} %bitcast.odd, bf16[3,5,2,7,128,128]{5,4,3,2,1,0:T(8,128)(2,1)S(1)} %get-tuple-element.54.h2._, bf16[3072,256]{1,0:T(8,128)(2,1)S(1)} %get-tuple-element.53.w3, f32[1,64]{1,0:T(1,128)S(1)} %bitcast.5), custom_call_target="tpu_custom_call" | custom-call | flops 3623878656 | bytes 1000000 | tf_op jit(solution)/shard_map/third/pallas_call | solution.py:579
  33.4 0.0 collective-permute-done.8
  33.4 0.0 collective-permute-done.7.gift
  33.4 1.5 %shared.1 = (bf16[3,5,2,7,128,128]{5,4,3,2,1,0:T(8,128)(2,1)S(1)}, bf16[4,2,6,128,128]{4,3,2,1,0:T(8,128)(2,1)S(1)}) custom-call(s32[1]{0:T(128)} %bitcast.odd, bf16[3,2,7,128,128]{4,3,2,1,0:T(8,128)(2,1)S(1)} %collective-permute-done.7.gift, bf16[3072,256]{1,0:T(8,128)(2,1)S(1)} %get-tuple-element.53.w3, ...), custom_call_target="tpu_custom_call", output_to_operand_aliasing={{0}: (4, {}), {1}: (5, {})} | custom-call | flops 1207959552 | bytes 1000000 | tf_op jit(solution)/shard_map/shared/pallas_call | solution.py:589
  34.9 1.7 %final.1 = (f32[3,4,8,128]{3,2,1,0:T(8,128)}, f32[6,4,8,128]{3,2,1,0:T(8,128)}) custom-call(bf16[4,2,6,128,128]{4,3,2,1,0:T(8,128)(2,1)S(1)} %get-tuple-element.55.h3, bf16[144,256]{1,0:T(8,128)(2,1)S(1)} %get-tuple-element.56.w4, f32[240,128]{1,0:T(8,128)S(1)} %get-tuple-element.38.own, f32[2,240,128]{2,1,0:T(8,128)S(1)} %get-tuple-element.41.sides, ...), custom_call_target="tpu_custom_call" | custom-call | flops 2013265920 | bytes 1000000 | tf_op jit(solution)/shard_map/final/pallas_call | solution.py:602
  (5 shorter events, 0.0 us)
Async XLA Ops:
  0.6 0.8 %copy-start = (f32[3,4,8,128]{3,2,1,0:T(8,128)S(1)}, f32[3,4,8,128]{3,2,1,0:T(8,128)}, u32[]{:S(2)}) copy-start(f32[3,4,8,128]{3,2,1,0:T(8,128)} %v.3) | copy-start | bytes 147460
  1.4 7.2 %collective-permute-start = (f32[72,128]{1,0:T(8,128)S(1)}, f32[72,128]{1,0:T(8,128)S(1)}, u32[]{:S(2)}, u32[]{:S(2)}) collective-permute-start(f32[72,128]{1,0:T(8,128)S(1)} %get-tuple-element.30), channel_id=1, source_target_pairs={{0,1},{1,2},{2,3},{3,0},{4,5},{5,6},{6,7},{7,4},{8,9},{9,10},{10,1... | collective-permute-start | bytes 110600 | tf_op jit(solution)/shard_map/ppermute | solution.py:24
  4.5 4.4 %collective-permute-start.1 = (f32[72,128]{1,0:T(8,128)S(1)}, f32[72,128]{1,0:T(8,128)S(1)}, u32[]{:S(2)}, u32[]{:S(2)}) collective-permute-start(f32[72,128]{1,0:T(8,128)S(1)} %get-tuple-element.31), channel_id=1, source_target_pairs={{0,3},{1,0},{2,1},{3,2},{4,7},{5,4},{6,5},{7,6},{8,11},{9,8},{10,9... | collective-permute-start | bytes 110600 | tf_op jit(solution)/shard_map/ppermute | solution.py:24
  6.6 0.9 %copy-start.5 = (bf16[3,3,3,64,9]{3,2,4,1,0:T(4,128)(2,1)S(1)}, bf16[3,3,3,64,9]{3,2,4,1,0:T(4,128)(2,1)}, u32[]{:S(2)}) copy-start(bf16[3,3,3,64,9]{3,2,4,1,0:T(4,128)(2,1)} %param.9) | copy-start | bytes 93316
  7.5 0.7 %copy-start.7 = (f32[64]{0:T(128)S(1)}, f32[64]{0:T(128)}, u32[]{:S(2)}) copy-start(f32[64]{0:T(128)} %param.10) | copy-start | bytes 772
  8.2 0.8 %copy-start.1 = (f32[3,4,8,128]{3,2,1,0:T(8,128)S(1)}, f32[3,4,8,128]{3,2,1,0:T(8,128)}, u32[]{:S(2)}) copy-start(f32[3,4,8,128]{3,2,1,0:T(8,128)} %v.3) | copy-start | bytes 147460
  8.2 3.6 %copy-start.3 = (bf16[3,3,3,64,64]{4,3,2,1,0:T(8,128)(2,1)S(1)}, bf16[3,3,3,64,64]{4,3,2,1,0:T(8,128)(2,1)}, u32[]{:S(2)}) copy-start(bf16[3,3,3,64,64]{4,3,2,1,0:T(8,128)(2,1)} %w2) | copy-start | bytes 663556
  8.2 3.6 %copy-start.4 = (bf16[3,3,3,64,64]{4,3,2,1,0:T(8,128)(2,1)S(1)}, bf16[3,3,3,64,64]{4,3,2,1,0:T(8,128)(2,1)}, u32[]{:S(2)}) copy-start(bf16[3,3,3,64,64]{4,3,2,1,0:T(8,128)(2,1)} %w3) | copy-start | bytes 663556
  8.2 3.6 %copy-start.6 = (bf16[3,3,3,6,64]{4,3,2,1,0:T(8,128)(2,1)S(1)}, bf16[3,3,3,6,64]{4,3,2,1,0:T(8,128)(2,1)}, u32[]{:S(2)}) copy-start(bf16[3,3,3,6,64]{4,3,2,1,0:T(8,128)(2,1)} %w4) | copy-start | bytes 62212
  9.0 3.5 %collective-permute-start.4 = (f32[240,128]{1,0:T(8,128)S(1)}, f32[240,128]{1,0:T(8,128)S(1)}, u32[]{:S(2)}, u32[]{:S(2)}) collective-permute-start(f32[240,128]{1,0:T(8,128)S(1)} %get-tuple-element.38.own), channel_id=1, source_target_pairs={{0,4},{4,0},{8,12},{12,8},{16,20},{20,16},{24,28},{28,24},{1,5},{5... | collective-permute-start | bytes 368648 | tf_op jit(solution)/shard_map/ppermute | solution.py:30
  9.1 5.8 %collective-permute-start.3 = (f32[240,128]{1,0:T(8,128)S(1)}, f32[240,128]{1,0:T(8,128)S(1)}, u32[]{:S(2)}, u32[]{:S(2)}) collective-permute-start(f32[240,128]{1,0:T(8,128)S(1)} %get-tuple-element.38.own), channel_id=1, source_target_pairs={{0,28},{4,8},{8,4},{12,16},{16,12},{20,24},{24,20},{28,0},{1,29},{... | collective-permute-start | bytes 368648 | tf_op jit(solution)/shard_map/ppermute | solution.py:30
  11.8 6.7 %collective-permute-start.2 = (f32[120,128]{1,0:T(8,128)S(1)}, f32[120,128]{1,0:T(8,128)S(1)}, u32[]{:S(2)}, u32[]{:S(2)}) collective-permute-start(f32[120,128]{1,0:T(8,128)S(1)} %get-tuple-element.36), channel_id=1, source_target_pairs={{0,8},{4,28},{8,16},{12,4},{16,24},{20,12},{24,0},{28,20},{1,9},{5... | collective-permute-start | bytes 184328 | tf_op jit(solution)/shard_map/ppermute | solution.py:35
  12.7 6.7 %collective-permute-start.5 = (f32[1,1,1,128]{3,2,1,0:T(1,128)S(1)}, f32[1,1,1,128]{3,2,1,0:T(1,128)S(1)}, u32[]{:S(2)}, u32[]{:S(2)}) collective-permute-start(f32[1,1,1,128]{3,2,1,0:T(1,128)S(1)} %energy.1), channel_id=1, source_target_pairs={{0,2},{1,3},{2,0},{3,1},{4,6},{5,7},{6,4},{7,5},{8,10},{9,11},{10,... | collective-permute-start | bytes 1544 | tf_op jit(solution)/shard_map/ppermute | solution.py:24
  18.5 2.9 %copy-start.8 = (f32[64]{0:T(128)S(1)}, f32[64]{0:T(128)}, u32[]{:S(2)}) copy-start(f32[64]{0:T(128)} %param.12) | copy-start | bytes 772
  19.3 8.5 %collective-permute-start.6 = (f32[1,1,1,128]{3,2,1,0:T(1,128)S(1)}, f32[1,1,1,128]{3,2,1,0:T(1,128)S(1)}, u32[]{:S(2)}, u32[]{:S(2)}) collective-permute-start(f32[1,1,1,128]{3,2,1,0:T(1,128)S(1)} %add.18), channel_id=1, source_target_pairs={{0,8},{4,12},{8,16},{12,20},{16,24},{20,28},{24,0},{28,4},{1,9},{5... | collective-permute-start | bytes 1544 | tf_op jit(solution)/shard_map/ppermute | solution.py:24
  21.4 8.1 %copy-start.2 = (f32[64]{0:T(128)S(1)}, f32[64]{0:T(128)}, u32[]{:S(2)}) copy-start(f32[64]{0:T(128)} %param.14) | copy-start | bytes 772
  27.9 5.5 %collective-permute-start.7 = (bf16[3,2,7,128,128]{4,3,2,1,0:T(8,128)(2,1)S(1)}, bf16[3,2,7,128,128]{4,3,2,1,0:T(8,128)(2,1)S(1)}, u32[]{:S(2)}, u32[]{:S(2)}) collective-permute-start(bf16[3,2,7,128,128]{4,3,2,1,0:T(8,128)(2,1)S(1)} %get-tuple-element.52), channel_id=1, source_target_pairs={{0,4},{4,0},{8,12},{12,8},{16,20},{20,16},{24,28},{28,24},{1,5},{5... | collective-permute-start | bytes 4128776 | tf_op jit(solution)/shard_map/ppermute | solution.py:30
  28.8 4.6 %collective-permute-start.8 = (f32[1,1,1,128]{3,2,1,0:T(1,128)S(1)}, f32[1,1,1,128]{3,2,1,0:T(1,128)S(1)}, u32[]{:S(2)}, u32[]{:S(2)}) collective-permute-start(f32[1,1,1,128]{3,2,1,0:T(1,128)S(1)} %add.19), channel_id=1, source_target_pairs={{0,16},{4,20},{8,24},{12,28},{16,0},{20,4},{24,8},{28,12},{1,17},{... | collective-permute-start | bytes 1544 | tf_op jit(solution)/shard_map/ppermute | solution.py:24
